TPU v7x, 8 devices: a whole 2x2x1 slice. The times are simulated.
8 devices in a mesh: rep: 2 (over y, z), dp: 4 (over x, core).
Axes of the slice: x: 2, y: 2, z: 1, core: 2. Of those that a mesh axis runs over, the one named last changes fastest.
Arguments:
- x: bfloat16 [8, 2048, 1024], P(('rep', 'dp')), parts along dimension 0
- dy: bfloat16 [8, 2048, 1024], P(('rep', 'dp')), parts along dimension 0
- w_gate: bfloat16 [2, 1024, 2816], replicated
- w_up: bfloat16 [2, 1024, 2816], replicated
- w_down: bfloat16 [2, 2816, 1024], replicated
- m_w_gate: float32 [2, 1024, 2816], P(None, 'dp')
- m_w_up: float32 [2, 1024, 2816], P(None, 'dp')
- m_w_down: float32 [2, 2816, 1024], P(None, 'dp')
- v_w_gate: float32 [2, 1024, 2816], P(None, 'dp')
- v_w_up: float32 [2, 1024, 2816], P(None, 'dp')
- v_w_down: float32 [2, 2816, 1024], P(None, 'dp')
Outputs:
- output 1: bfloat16 [4, 1024, 2816], P('rep'), parts along dimension 0
- output 2: bfloat16 [4, 1024, 2816], P('rep'), parts along dimension 0
- output 3: bfloat16 [4, 2816, 1024], P('rep'), parts along dimension 0
- output 4: float32 [4, 1024, 2816], P('rep', 'dp'), parts along dimension 0
- output 5: float32 [4, 1024, 2816], P('rep', 'dp'), parts along dimension 0
- output 6: float32 [4, 2816, 1024], P('rep', 'dp'), parts along dimension 0
- output 7: float32 [4, 1024, 2816], P('rep', 'dp'), parts along dimension 0
- output 8: float32 [4, 1024, 2816], P('rep', 'dp'), parts along dimension 0
- output 9: float32 [4, 2816, 1024], P('rep', 'dp'), parts along dimension 0
There are 2 independent parts. A program takes and returns all parts, laid end to end along the dimension named above; an argument that names none is the same for every part.
All inputs are finite; a program needn't handle non-finite values.
Results may differ from a plain program's by a relative error of at most 0.022.
Values are sent between devices in bfloat16 or wider.
A program may use at most 2 GiB of HBM per device.

v0:
```python
import jax
import jax.numpy as jnp
from jax import lax
from jax.experimental import pallas as pl
from jax.experimental.pallas import tpu as pltpu
from jax.sharding import PartitionSpec as P


F32, BF16 = jnp.float32, jnp.bfloat16
T, D, FF, DP, CORES = 2048, 1024, 2816, 4, 2
COUNT = 3 * 2 * D * FF
CHUNK = 256
CHUNKS = FF // CHUNK
ROWS = 512
VMEM_LIMIT = 62 * 2**20
ANY = pl.BlockSpec(memory_space=pl.ANY)
MESH = pl.DeviceIdType.MESH


def dot(a, b):
    return lax.dot_general(a, b, (((1,), (0,)), ((), ())), preferred_element_type=F32)


def dot_t(a, b):
    return lax.dot_general(a, b, (((1,), (1,)), ((), ())), preferred_element_type=F32)


def whole(shape):
    return pl.BlockSpec(shape, lambda *_: (0,) * len(shape), pipeline_mode=pl.Buffered(1))


def params():
    return pltpu.CompilerParams(vmem_limit_bytes=VMEM_LIMIT, dimension_semantics=("arbitrary",))


def cost(matmuls, moved):
    return pl.CostEstimate(flops=int(2 * T * D * FF * matmuls), bytes_accessed=int(moved), transcendentals=0)


def root_mean_scale(wide):
    return lax.rsqrt(jnp.mean(wide * wide, -1, keepdims=True) + 1e-6)


def forward_first(x, w_gate, w_up, w_down):
    piece = 128
    pieces = D // piece

    def kernel(x_ref, wg_ref, wu_ref, wd_ref, g_ref, u_ref, t_ref, h_ref, n_ref, a_ref, acc):
        j = pl.program_id(0)

        @pl.when(j == 0)
        def _():
            for t in range(0, T, ROWS):
                rows = slice(t, t + ROWS)
                wide = x_ref[rows].astype(F32)
                a_ref[rows] = (wide * root_mean_scale(wide)).astype(BF16)
                acc[rows] = jnp.zeros((ROWS, D), F32)

        k = jnp.minimum(j, pieces - 1)
        per = D // DP // piece
        source = pl.multiple_of(block_of(k // per) * (D // DP) + lax.rem(k, per) * piece, piece)
        t_ref[pl.ds(pl.multiple_of(k * piece, piece), piece)] = a_ref[:, pl.ds(source, piece)].T

        for t in range(0, T, ROWS):
            rows = slice(t, t + ROWS)
            a = a_ref[rows]
            g = dot(a, wg_ref[...])
            u = dot(a, wu_ref[...])
            g_ref[rows] = g
            u_ref[rows] = u
            act = (g * jax.nn.sigmoid(g) * u).astype(BF16)
            acc[rows] += dot(act, wd_ref[...])

        @pl.when(j == CHUNKS - 1)
        def _():
            for t in range(0, T, ROWS):
                rows = slice(t, t + ROWS)
                h = x_ref[rows] + acc[rows].astype(BF16)
                h_ref[rows] = h
                wide = h.astype(F32)
                n_ref[rows] = (wide * root_mean_scale(wide)).astype(BF16)

    tall = jax.ShapeDtypeStruct((T, FF), F32)
    flat = jax.ShapeDtypeStruct((T, D), BF16)
    wide_block = pl.BlockSpec((T, CHUNK), lambda j: (0, j))
    return pl.pallas_call(
        kernel,
        grid=(CHUNKS,),
        in_specs=[
            whole((T, D)),
            pl.BlockSpec((None, D, CHUNK), lambda j: (0, 0, j)),
            pl.BlockSpec((None, D, CHUNK), lambda j: (0, 0, j)),
            pl.BlockSpec((None, CHUNK, D), lambda j: (0, j, 0)),
        ],
        out_specs=[wide_block, wide_block, whole((D, T)), whole((T, D)), whole((T, D))],
        out_shape=[tall, tall, jax.ShapeDtypeStruct((D, T), BF16), flat, flat],
        scratch_shapes=[pltpu.VMEM((T, D), BF16), pltpu.VMEM((T, D), F32)],
        compiler_params=params(),
        cost_estimate=cost(3, 90e6),
    )(x, w_gate, w_up, w_down)


def peers():
    me = lax.axis_index("dp")
    core = lax.rem(me, CORES)
    chip = me // CORES
    return chip, core, me + 1 - 2 * core, me + CORES - 2 * CORES * chip


def greet(*others):
    barrier = pltpu.get_barrier_semaphore()
    for other in others:
        pl.semaphore_signal(barrier, inc=1, device_id={"dp": other}, device_id_type=MESH)
    pl.semaphore_wait(barrier, len(others))


def block_of(i):
    chip, core, *_ = peers()
    side = lax.rem(i, CORES)
    return (side * chip + (1 - side) * (1 - chip)) * CORES + jnp.where(i < CORES, 1 - core, core)


def remote_params(ident):
    return pltpu.CompilerParams(
        vmem_limit_bytes=VMEM_LIMIT, dimension_semantics=("arbitrary",), collective_id=ident, has_side_effects=True
    )


def remote(source, landing, send_sem, recv_sem, to):
    return pltpu.make_async_remote_copy(
        src_ref=source, dst_ref=landing, send_sem=send_sem, recv_sem=recv_sem, device_id={"dp": to}, device_id_type=MESH
    )


def hidden(ident, layer, inside, lag, normed, by_out, weights, gate_up, after):
    w_gate, w_up, w_down = weights
    computed = gate_up is None
    n_after = len(after)
    rows_w = D // DP
    outside = CHUNKS - inside

    def kernel(n_ref, by_ref, wd_ref, a_ref, b_ref, *rest):
        rest = rest[n_after:]
        sum_ref, far_ref, near_ref, act_ref, *rest = rest
        if computed:
            dg_ref, du_ref, n_t, *rest = rest
        else:
            n_t = n_ref
        act, out, keep, got, far, near, landed, send_sem, recv_sem, over_send, over_recv, *rest = rest
        if not computed:
            dg_ref, du_ref = rest
        j = pl.program_id(0)
        _, _, sib, opposite = peers()

        def beside(k):
            slot = lax.rem(k, 2)
            return remote(out.at[slot], got.at[k], send_sem.at[k], recv_sem.at[k], sib)

        def over(k):
            return remote(far.at[k], landed.at[k], over_send.at[k], over_recv.at[k], opposite)

        def add(k):
            mine = keep.at[lax.rem(k, 2)]

            def sums(which):
                there = (mine[which, 0].astype(F32) + got[k, which, 0].astype(F32)).astype(BF16)
                return there, mine[which, 1].astype(F32) + got[k, which, 1].astype(F32)

            @pl.when(k < inside)
            def _():
                for which in range(2):
                    far[k, which], near[k, which] = sums(which)

            @pl.when(k >= inside)
            def _():
                columns = pl.ds(pl.multiple_of((k - inside) * CHUNK, CHUNK), CHUNK)
                for which in range(2):
                    far_ref[which, :, columns], near_ref[which, :, columns] = sums(which)

        def finish(k):
            over(k).wait()
            columns = pl.ds(pl.multiple_of(k * CHUNK, CHUNK), CHUNK)
            for which in range(2):
                sum_ref[which, :, columns] = (near[k, which] + landed[k, which].astype(F32)).astype(BF16)

        @pl.when(j == 0)
        def _():
            greet(sib, opposite)
            if computed:
                for k in range(DP):
                    columns = pl.ds(pl.multiple_of(block_of(k) * rows_w, rows_w), rows_w)
                    n_t[k * rows_w : (k + 1) * rows_w] = n_ref[:, columns].T

        for t in range(0, T, ROWS):
            rows = slice(t, t + ROWS)
            if computed:
                n = n_ref[rows]
                g, u = dot(n, a_ref[...]), dot(n, b_ref[...])
            else:
                g, u = a_ref[rows], b_ref[rows]
            p = dot_t(by_ref[rows], wd_ref[...]).astype(BF16).astype(F32)
            sig = jax.nn.sigmoid(g)
            silu = g * sig
            act[rows] = (silu * u).astype(BF16)
            du_ref[rows] = (p * silu).astype(BF16)
            dg_ref[rows] = (p * u * (sig + silu * (1.0 - sig))).astype(BF16)

        @pl.when(j > 0)
        def _():
            beside(j - 1).wait()
            add(j - 1)

        act_ref[...] = act[...].T
        half = D // CORES
        for which, d_ref in ((0, dg_ref), (1, du_ref)):
            out[lax.rem(j, 2), which] = dot(n_t[:half], d_ref[...]).astype(BF16).reshape(CORES, rows_w, CHUNK)
        for which, d_ref in ((0, dg_ref), (1, du_ref)):
            keep[lax.rem(j, 2), which] = dot(n_t[half:], d_ref[...]).astype(BF16).reshape(CORES, rows_w, CHUNK)
        beside(j).start()

        @pl.when((j > 0) & (j <= inside))
        def _():
            over(j - 1).start()

        @pl.when((j >= lag) & (j < lag + inside))
        def _():
            finish(j - lag)

        @pl.when(j == CHUNKS - 1)
        def _():
            beside(j).wait()
            add(j)
            for k in range(CHUNKS - lag, inside):
                finish(k)

    column = pl.BlockSpec((None, D, CHUNK), lambda j: (layer, 0, j))
    block = pl.BlockSpec((T, CHUNK), lambda j: (0, j))
    inner, outer = (2, rows_w, inside * CHUNK), (2, rows_w, outside * CHUNK)
    turned = pl.BlockSpec((CHUNK, T), lambda j: (j, 0))
    out_specs = [whole(inner), whole(outer), whole(outer), turned]
    out_shape = [(inner, BF16), (outer, BF16), (outer, F32), ((FF, T), BF16)]
    part, block_part = (2, CORES, rows_w, CHUNK), (inside, 2, rows_w, CHUNK)
    scratch = [
        pltpu.VMEM((T, CHUNK), BF16),
        pltpu.VMEM((2, *part), BF16),
        pltpu.VMEM((2, *part), BF16),
        pltpu.VMEM((CHUNKS, *part), BF16),
        pltpu.VMEM(block_part, BF16),
        pltpu.VMEM(block_part, F32),
        pltpu.VMEM(block_part, BF16),
        *(pltpu.SemaphoreType.DMA((CHUNKS,)),) * 2,
        *(pltpu.SemaphoreType.DMA((inside,)),) * 2,
    ]
    if computed:
        out_specs += [block, block]
        out_shape += [((T, FF), BF16)] * 2
        scratch = [pltpu.VMEM((D, T), BF16), *scratch]
    else:
        scratch += [pltpu.VMEM((T, CHUNK), BF16)] * 2
    return pl.pallas_call(
        kernel,
        grid=(CHUNKS,),
        in_specs=[
            whole(normed.shape),
            whole((T, D)),
            pl.BlockSpec((None, CHUNK, D), lambda j: (layer, j, 0)),
            *((column, column) if computed else (block, block)),
            *(ANY,) * n_after,
        ],
        out_specs=out_specs,
        out_shape=[jax.ShapeDtypeStruct(*one) for one in out_shape],
        scratch_shapes=scratch,
        compiler_params=remote_params(ident),
        cost_estimate=cost(5 if computed else 3, 60e6),
    )(normed, by_out, w_down, *((w_gate, w_up) if computed else gate_up), *after)


def down_grad(ident, act_t, by_out, first, count, after):
    n_after = len(after)
    rows_w = FF // DP

    def kernel(act_ref, by_ref, *rest):
        far_ref, near_ref, out, got, send_sem, recv_sem = rest[n_after:]
        i = pl.program_id(0)
        sib = peers()[2]

        def copy(k):
            return remote(out.at[k], got.at[k], send_sem.at[k], recv_sem.at[k], sib)

        pl.when(i == 0)(lambda: greet(sib))
        term = dot(act_ref[...], by_ref[...]).astype(BF16)

        @pl.when(i < CORES)
        def _():
            out[lax.rem(i, CORES)] = term

        for k in range(CORES):

            @pl.when(i == k + 1)
            def _(k=k):
                copy(k).start()

        @pl.when(i == CORES)
        def _():
            copy(0).wait()
            far_ref[...] = (term.astype(F32) + got[0].astype(F32)).astype(BF16)

        @pl.when(i == CORES + 1)
        def _():
            copy(1).wait()
            near_ref[...] = term.astype(F32) + got[1].astype(F32)

    shape = (rows_w, count)
    return pl.pallas_call(
        kernel,
        grid=(DP,),
        in_specs=[
            pl.BlockSpec((rows_w, T), lambda i: (block_of(i), 0)),
            pl.BlockSpec((T, count), lambda i: (0, first // count), pipeline_mode=pl.Buffered(1)),
            *(ANY,) * n_after,
        ],
        out_specs=[whole(shape), whole(shape)],
        out_shape=[jax.ShapeDtypeStruct(shape, BF16), jax.ShapeDtypeStruct(shape, F32)],
        scratch_shapes=[
            pltpu.VMEM((CORES, *shape), BF16),
            pltpu.VMEM((CORES, *shape), BF16),
            pltpu.SemaphoreType.DMA((CORES,)),
            pltpu.SemaphoreType.DMA((CORES,)),
        ],
        compiler_params=remote_params(ident),
        cost_estimate=cost(count / D, 20e6),
    )(act_t, by_out, *after)


def new_weight(layer, me, factor, g, m, v, w, full):
    rows, columns = g.shape
    steps = 4
    tile = rows // steps
    n_full = full is not None

    def kernel(me_ref, factor_ref, g_ref, m_ref, v_ref, w_ref, *rest):
        out_ref, full_ref = rest[n_full:]
        g = g_ref[...].astype(F32) * factor_ref[0]
        m = 0.9 * m_ref[...] + 0.1 * g
        v = 0.95 * v_ref[...] + 0.05 * g * g
        w = w_ref[...].astype(F32)
        new = (w - 0.02 * (m * lax.rsqrt(v + 1e-8) + 0.1 * w)).astype(BF16)
        out_ref[...] = new
        full_ref[...] = new

    mine = pl.BlockSpec((tile, columns), lambda i, _: (i, 0))
    state = pl.BlockSpec((None, tile, columns), lambda i, _: (layer, i, 0))
    own = pl.BlockSpec((None, tile, columns), lambda i, me_ref: (layer, me_ref[0] * steps + i, 0))
    return pl.pallas_call(
        kernel,
        grid_spec=pltpu.PrefetchScalarGridSpec(
            num_scalar_prefetch=1,
            grid=(steps,),
            in_specs=[pl.BlockSpec(memory_space=pltpu.SMEM), mine, state, state, own, *(ANY,) * n_full],
            out_specs=[mine, own],
        ),
        out_shape=[jax.ShapeDtypeStruct((rows, columns), BF16), jax.ShapeDtypeStruct(w.shape, BF16)],
        input_output_aliases={6: 1} if n_full else {},
        compiler_params=params(),
        cost_estimate=cost(0.1, 10e6),
    )(me.reshape(1), factor.reshape(1), g, m, v, w, *((full,) if n_full else ()))


def into_states(dg, du, w_gate, w_up, h, by_out, after):
    tile = 256
    n_after = len(after)

    def kernel(dg_ref, du_ref, wg_ref, wu_ref, h_ref, by_ref, *rest):
        out_ref = rest[n_after]
        by_a = dot_t(dg_ref[...], wg_ref[...]).astype(BF16) + dot_t(du_ref[...], wu_ref[...]).astype(BF16)
        c, wide = by_a.astype(F32), h_ref[...].astype(F32)
        scale = root_mean_scale(wide)
        along = jnp.sum(c * wide, -1, keepdims=True)
        out_ref[...] = by_ref[...] + (c * scale - wide * (scale * scale * scale * along * (1.0 / D))).astype(BF16)

    long = pl.BlockSpec((tile, FF), lambda i: (i, 0))
    short = pl.BlockSpec((tile, D), lambda i: (i, 0))
    weight = pl.BlockSpec((None, D, FF), lambda i: (1, 0, 0), pipeline_mode=pl.Buffered(1))
    return pl.pallas_call(
        kernel,
        grid=(T // tile,),
        in_specs=[long, long, weight, weight, short, short, *(ANY,) * n_after],
        out_specs=short,
        out_shape=jax.ShapeDtypeStruct((T, D), BF16),
        compiler_params=params(),
        cost_estimate=cost(2, 50e6),
    )(dg, du, w_gate, w_up, h, by_out, *after)


def solution(mesh):
    sibling = [(i, i ^ 1) for i in range(DP)]
    across = [(i, i ^ 2) for i in range(DP)]

    def step(x, dy, w_gate, w_up, w_down, m_gate, m_up, m_down, v_gate, v_up, v_down):
        x, dy = x[0], dy[0]
        me = lax.axis_index("dp")
        weights = (w_gate, w_up, w_down)

        def cross(far):
            return lax.ppermute(far, "dp", across)

        g1, u1, a1, h1, a2 = forward_first(x, *weights)
        units = {}
        sum_b, far, near, act2, dg2, du2 = hidden(0, 1, 9, 3, a2, dy, weights, None, ())
        units["b"] = near, cross(far)
        far, near = down_grad(1, act2, dy, 0, D, (far,))
        units["d"] = near, cross(far)
        dh1 = into_states(dg2, du2, w_gate, w_up, h1, dy, (far,))
        sum_e, far, near, act1 = hidden(2, 0, 7, 5, a1, dh1, weights, (g1, u1), ())
        units["e"] = near, cross(far)
        far, near = down_grad(3, act1, dh1, 0, D, (far,))
        units["f"] = near, cross(far)

        nears = {name: near for name, (near, _) in units.items()}
        nears, sum_b, sum_e, _ = lax.optimization_barrier((nears, sum_b, sum_e, far))
        units = {name: (nears[name], landed) for name, (_, landed) in units.items()}
        grads, squared = {}, []
        for name, (near, landed) in units.items():
            grads[name] = (near + landed.astype(F32)).astype(BF16)
            squared.append(jnp.sum(grads[name].astype(F32) ** 2))
            if name in "be":
                inner = sum_b if name == "b" else sum_e
                squared.append(jnp.sum(inner.astype(F32) ** 2))
                grads[name] = jnp.concatenate([inner, grads[name]], 2)

        def of(which, layer):
            if which == 2:
                return grads["d" if layer else "f"]
            return grads["b" if layer else "e"][which]

        each = {(which, layer): of(which, layer) for which in range(3) for layer in range(2)}
        squares, each = lax.optimization_barrier((sum(squared), each))
        squares = lax.psum(squares, "dp")
        factor = jnp.minimum(1.0, 0.5 * lax.rsqrt(squares / COUNT + 1e-30))

        ms, vs = (m_gate, m_up, m_down), (v_gate, v_up, v_down)
        full, sent = [None] * 3, []
        for (which, layer), g in each.items():
            name = f"{which}{layer}"
            mine, full[which] = new_weight(layer, me, factor, g, ms[which], vs[which], weights[which], full[which])
            over = lax.ppermute(mine, "dp", across)
            beside = lax.ppermute(mine, "dp", sibling)
            sent.append((which, layer, over, beside))
        factor, _ = lax.optimization_barrier((factor, mine))
        new_m, new_v = [], []
        for which in range(3):
            g = jnp.stack([each[which, 0], each[which, 1]]).astype(F32) * factor
            new_m.append(0.9 * ms[which] + 0.1 * g)
            new_v.append(0.95 * vs[which] + 0.05 * g * g)
        for k, (which, layer, over, beside) in enumerate(sent):
            if 1 <= k <= 3:
                full, new_m[k - 1], new_v[k - 1] = lax.optimization_barrier((full, new_m[k - 1], new_v[k - 1]))
            over, beside, full = lax.optimization_barrier((over, beside, full))
            corner = lax.ppermute(over, "dp", sibling)
            for piece, who in ((beside, me ^ 1), (over, me ^ 2), (corner, me ^ 3)):
                full[which] = lax.dynamic_update_slice(full[which], piece[None], (layer, who * piece.shape[0], 0))
        return (*full, *new_m, *new_v)

    batch, replicated, rows = P(("rep", "dp"), None, None), P(None, None, None), P(None, "dp", None)
    return jax.shard_map(
        step,
        mesh=mesh,
        in_specs=(batch, batch, *(replicated,) * 3, *(rows,) * 6),
        out_specs=(*(P("rep", None, None),) * 3, *(P("rep", "dp", None),) * 6),
        check_vma=False,
    )
```

profile of v0, /device:TPU:0, one launch (start us, length us, event | category | flops | bytes accessed | tf_op | source)
XLA Modules:
  0.0 521.0 jit_solution(595036990563394517)
XLA Ops:
  0.6 51.4 %shard_map.178 = (f32[2048,2816]{1,0:T(8,128)}, f32[2048,2816]{1,0:T(8,128)}, bf16[1024,2048]{1,0:T(8,128)(2,1)}, bf16[2048,1024]{1,0:T(8,128)(2,1)}, bf16[2048,1024]{1,0:T(8,128)(2,1)}) custom-call(bf16[2048,1024]{1,0:T(8,128)(2,1)} %bitcast.62, bf16[2,1024,2816]{2,1,0:T(8,128)(2,1)} %w_ref.11, bf16[2,1024,2816]{2,1,0:T(8,128)(2,1)} %w_ref.9, ...), custom_call_target="tpu_custom_call" | custom-call | flops 35433480192 | bytes 90000000 | tf_op jit(solution)/shard_map/pallas_call | solution.py:86
  52.0 82.1 %shard_map.179 = (bf16[2,256,2304]{2,1,0:T(8,128)(2,1)}, bf16[2,256,512]{2,1,0:T(8,128)(2,1)}, f32[2,256,512]{2,1,0:T(8,128)}, bf16[2816,2048]{1,0:T(8,128)(2,1)...) custom-call(bf16[2048,1024]{1,0:T(8,128)(2,1)} %get-tuple-element.99.n_ref, bf16[2048,1024]{1,0:T(8,128)(2,1)} %bitcast.63, ...), custom_call_target="tpu_custom_call" | custom-call | flops 59055800320 | bytes 60000000 | tf_op jit(solution)/shard_map/pallas_call | solution.py:260
  134.5 18.9 %shard_map.180 = (bf16[704,1024]{1,0:T(8,128)(2,1)}, f32[704,1024]{1,0:T(8,128)}) custom-call(bf16[2816,2048]{1,0:T(8,128)(2,1)} %get-tuple-element.101.act_ref, bf16[2048,1024]{1,0:T(8,128)(2,1)} %bitcast.64, bf16[2,256,512]{2,1,0:T(8,128)(2,1)} %get-tuple-element.102.rest_0_), custom_call_target="tpu_custom_call" | custom-call | flops 11811160064 | bytes 20000000 | tf_op jit(solution)/shard_map/pallas_call | solution.py:314
  155.1 33.8 %shard_map.181.by_ref = bf16[2048,1024]{1,0:T(8,128)(2,1)} custom-call(bf16[2048,2816]{1,0:T(8,128)(2,1)} %get-tuple-element.105.dg_ref, bf16[2048,2816]{1,0:T(8,128)(2,1)} %get-tuple-element.106.du_ref, bf16[2,1024,2816]{2,1,0:T(8,128)(2,1)} %w_ref.11, bf16[2,1024,2816]{2,1,0:T(8,128)(2,1)} %w_ref.9, bf16[2048,1024]{1,0:T(8,128)(2,1)} %get-tuple-element.107.h_ref, ...), custom_call_target="tpu_custom_call" | custom-call | flops 23622320128 | bytes 50000000 | tf_op jit(solution)/shard_map/pallas_call | solution.py:384
  188.9 59.8 %shard_map.182 = (bf16[2,256,1792]{2,1,0:T(8,128)(2,1)}, bf16[2,256,1024]{2,1,0:T(8,128)(2,1)}, f32[2,256,1024]{2,1,0:T(8,128)}, bf16[2816,2048]{1,0:T(8,128)(2,1)}) custom-call(bf16[1024,2048]{1,0:T(8,128)(2,1)} %get-tuple-element.104.n_ref, bf16[2048,1024]{1,0:T(8,128)(2,1)} %shard_map.181.by_ref, bf16[2,2816,1024]{2,1,0:T(8,128)(2,1)} %w_ref.7, ...), custom_call_target="tpu_custom_call" | custom-call | flops 35433480192 | bytes 60000000 | tf_op jit(solution)/shard_map/pallas_call | solution.py:260
  250.4 19.1 %shard_map.183 = (bf16[704,1024]{1,0:T(8,128)(2,1)}, f32[704,1024]{1,0:T(8,128)}) custom-call(bf16[2816,2048]{1,0:T(8,128)(2,1)} %get-tuple-element.112.act_ref, bf16[2048,1024]{1,0:T(8,128)(2,1)} %shard_map.181.by_ref, bf16[2,256,1024]{2,1,0:T(8,128)(2,1)} %get-tuple-element.113.rest_0_), custom_call_target="tpu_custom_call" | custom-call | flops 11811160064 | bytes 20000000 | tf_op jit(solution)/shard_map/pallas_call | solution.py:314
  271.4 3.6 multiply_reduce_fusion
  285.5 3.8 multiply_reduce_fusion.3
  291.3 14.1 %collective-permute-done.3 = bf16[704,1024]{1,0:T(8,128)(2,1)} collective-permute-done((bf16[704,1024]{1,0:T(8,128)(2,1)}, bf16[704,1024]{1,0:T(8,128)(2,1)}, u32[]{:S(2)}, u32[]{:S(2)}) %collective-permute-start.3) | collective-permute-done | bytes 1441824 | tf_op jit(solution)/shard_map/ppermute | solution.py:405
  305.4 3.8 multiply_reduce_fusion.2
  309.8 7.2 %psum.7 = f32[]{:T(128)} all-reduce(f32[]{:T(128)S(6)} %add.88), channel_id=1, replica_groups=mesh['rep'=2,'dp'=4] {'dp'}, use_global_device_ids=true, to_apply=%region_6.0 | all-reduce | flops 1 | bytes 8 | tf_op jit(solution)/shard_map/psum | solution.py:438
  317.6 6.1 %shard_map.188 = (bf16[256,2816]{1,0:T(8,128)(2,1)}, bf16[2,1024,2816]{2,1,0:T(8,128)(2,1)}) custom-call(s32[1]{0:T(128)} %bitcast.me_ref, f32[1]{0:T(128)} %bitcast.7.factor_ref, bf16[256,2816]{1,0:T(8,128)(2,1)} %get-tuple-element.136.g_ref, f32[2,256,2816]{2,1,0:T(8,128)} %m_ref.11, f32[2,256,2816]{2,1,0:T(8,128)} %v_ref.11, bf16[2,1024,2816]{2,1,0:T(8,128)(2,1)} %w_ref.11), custom_call_target="tpu_custom_call" | custom-call | flops 1181116032 | bytes 10000000 | tf_op jit(solution)/shard_map/pallas_call | solution.py:354
  324.7 6.0 %shard_map.189 = (bf16[256,2816]{1,0:T(8,128)(2,1)}, bf16[2,1024,2816]{2,1,0:T(8,128)(2,1)}) custom-call(s32[1]{0:T(128)} %bitcast.me_ref, f32[1]{0:T(128)} %bitcast.7.factor_ref, bf16[256,2816]{1,0:T(8,128)(2,1)} %get-tuple-element.135.g_ref, f32[2,256,2816]{2,1,0:T(8,128)} %m_ref.11, f32[2,256,2816]{2,1,0:T(8,128)} %v_ref.11, ...), custom_call_target="tpu_custom_call", output_to_operand_aliasing={{1}: (6, {})} | custom-call | flops 1181116032 | bytes 10000000 | tf_op jit(solution)/shard_map/pallas_call | solution.py:354
  332.0 6.0 %shard_map.184 = (bf16[704,1024]{1,0:T(8,128)(2,1)}, bf16[2,2816,1024]{2,1,0:T(8,128)(2,1)}) custom-call(s32[1]{0:T(128)} %bitcast.me_ref, f32[1]{0:T(128)} %bitcast.7.factor_ref, bf16[704,1024]{1,0:T(8,128)(2,1)} %get-tuple-element.126.g_ref, f32[2,704,1024]{2,1,0:T(8,128)} %m_ref.7, f32[2,704,1024]{2,1,0:T(8,128)} %v_ref.7, bf16[2,2816,1024]{2,1,0:T(8,128)(2,1)} %w_ref.7), custom_call_target="tpu_custom_call" | custom-call | flops 1181116032 | bytes 10000000 | tf_op jit(solution)/shard_map/pallas_call | solution.py:354
  338.0 6.0 %shard_map.185 = (bf16[704,1024]{1,0:T(8,128)(2,1)}, bf16[2,2816,1024]{2,1,0:T(8,128)(2,1)}) custom-call(s32[1]{0:T(128)} %bitcast.me_ref, f32[1]{0:T(128)} %bitcast.7.factor_ref, bf16[704,1024]{1,0:T(8,128)(2,1)} %get-tuple-element.125.g_ref, f32[2,704,1024]{2,1,0:T(8,128)} %m_ref.7, f32[2,704,1024]{2,1,0:T(8,128)} %v_ref.7, ...), custom_call_target="tpu_custom_call", output_to_operand_aliasing={{1}: (6, {})} | custom-call | flops 1181116032 | bytes 10000000 | tf_op jit(solution)/shard_map/pallas_call | solution.py:354
  344.1 6.2 %shard_map.186 = (bf16[256,2816]{1,0:T(8,128)(2,1)}, bf16[2,1024,2816]{2,1,0:T(8,128)(2,1)}) custom-call(s32[1]{0:T(128)} %bitcast.me_ref, f32[1]{0:T(128)} %bitcast.7.factor_ref, bf16[256,2816]{1,0:T(8,128)(2,1)} %get-tuple-element.131.g_ref, f32[2,256,2816]{2,1,0:T(8,128)} %m_ref.9, f32[2,256,2816]{2,1,0:T(8,128)} %v_ref.9, bf16[2,1024,2816]{2,1,0:T(8,128)(2,1)} %w_ref.9), custom_call_target="tpu_custom_call" | custom-call | flops 1181116032 | bytes 10000000 | tf_op jit(solution)/shard_map/pallas_call | solution.py:354
  351.2 9.8 %fusion.1 = (f32[2,256,2816]{2,1,0:T(8,128)}, f32[2,256,2816]{2,1,0:T(8,128)}) fusion(f32[2,256,2816]{2,1,0:T(8,128)} %v_ref.9, f32[]{:T(128)} %min_shard_map.3, bf16[1,256,2816]{2,1,0:T(8,128)(2,1)} %bitcast.60, bf16[1,256,2816]{2,1,0:T(8,128)(2,1)} %bitcast.57, f32[2,256,2816]{2,1,0:T(8,128)} %m_ref.9), kind=kLoop, calls=%fused_computation.4 | loop fusion | flops 14417920 | bytes 25952260 | tf_op jit(solution)/shard_map/add | solution.py:454
  362.4 7.6 %fusion.2 = (f32[2,704,1024]{2,1,0:T(8,128)}, f32[2,704,1024]{2,1,0:T(8,128)}) fusion(f32[2,704,1024]{2,1,0:T(8,128)} %v_ref.7, f32[]{:T(128)} %min_shard_map.3, bf16[1,704,1024]{2,1,0:T(8,128)(2,1)S(1)} %bitcast.61, bf16[1,704,1024]{2,1,0:T(8,128)(2,1)S(1)} %bitcast.58, f32[2,704,1024]{2,1,0:T(8,128)S(1)} %bitcast.55), kind=kLoop, calls=%fused_computation.5 | loop fusion | flops 14417920 | bytes 25952260 | tf_op jit(solution)/shard_map/add | solution.py:454
  370.1 6.2 %shard_map.187 = (bf16[256,2816]{1,0:T(8,128)(2,1)}, bf16[2,1024,2816]{2,1,0:T(8,128)(2,1)}) custom-call(s32[1]{0:T(128)} %bitcast.me_ref, f32[1]{0:T(128)} %bitcast.7.factor_ref, bf16[256,2816]{1,0:T(8,128)(2,1)} %get-tuple-element.130.g_ref, f32[2,256,2816]{2,1,0:T(8,128)} %m_ref.9, f32[2,256,2816]{2,1,0:T(8,128)} %v_ref.9, ...), custom_call_target="tpu_custom_call", output_to_operand_aliasing={{1}: (6, {})} | custom-call | flops 1181116032 | bytes 10000000 | tf_op jit(solution)/shard_map/pallas_call | solution.py:354
  376.2 8.2 %fusion = (f32[2,256,2816]{2,1,0:T(8,128)}, f32[2,256,2816]{2,1,0:T(8,128)}) fusion(f32[2,256,2816]{2,1,0:T(8,128)} %v_ref.11, f32[]{:T(128)} %min_shard_map.3, bf16[1,256,2816]{2,1,0:T(8,128)(2,1)} %bitcast.59, bf16[1,256,2816]{2,1,0:T(8,128)(2,1)S(1)} %bitcast.56, f32[2,256,2816]{2,1,0:T(8,128)} %m_ref.11), kind=kLoop, calls=%fused_computation.3 | loop fusion | flops 14417920 | bytes 25952260 | tf_op jit(solution)/shard_map/add | solution.py:454
  400.2 20.1 %collective-permute-done.10 = bf16[256,2816]{1,0:T(8,128)(2,1)} collective-permute-done((bf16[256,2816]{1,0:T(8,128)(2,1)}, bf16[256,2816]{1,0:T(8,128)(2,1)}, u32[]{:S(2)}, u32[]{:S(2)}) %collective-permute-start.10) | collective-permute-done | bytes 1441824 | tf_op jit(solution)/shard_map/ppermute | solution.py:446
  426.7 24.3 %collective-permute-done.8 = bf16[256,2816]{1,0:T(8,128)(2,1)S(1)} collective-permute-done((bf16[256,2816]{1,0:T(8,128)(2,1)S(1)}, bf16[256,2816]{1,0:T(8,128)(2,1)S(1)}, u32[]{:S(2)}, u32[]{:S(2)}) %collective-permute-start.8) | collective-permute-done | bytes 1441824 | tf_op jit(solution)/shard_map/ppermute | solution.py:446
  455.5 24.6 %collective-permute-done.6 = bf16[704,1024]{1,0:T(8,128)(2,1)S(1)} collective-permute-done((bf16[704,1024]{1,0:T(8,128)(2,1)S(1)}, bf16[704,1024]{1,0:T(8,128)(2,1)S(1)}, u32[]{:S(2)}, u32[]{:S(2)}) %collective-permute-start.6) | collective-permute-done | bytes 1441824 | tf_op jit(solution)/shard_map/ppermute | solution.py:446
  487.0 27.5 %collective-permute-done.4 = bf16[704,1024]{1,0:T(8,128)(2,1)} collective-permute-done((bf16[704,1024]{1,0:T(8,128)(2,1)}, bf16[704,1024]{1,0:T(8,128)(2,1)}, u32[]{:S(2)}, u32[]{:S(2)}) %collective-permute-start.4) | collective-permute-done | bytes 1441824 | tf_op jit(solution)/shard_map/ppermute | solution.py:446
  (88 shorter events, 59.3 us)
Async XLA Ops:
  134.1 140.9 %collective-permute-start = (bf16[2,256,512]{2,1,0:T(8,128)(2,1)}, bf16[2,256,512]{2,1,0:T(8,128)(2,1)}, u32[]{:S(2)}, u32[]{:S(2)}) collective-permute-start(bf16[2,256,512]{2,1,0:T(8,128)(2,1)} %get-tuple-element.102.rest_0_), channel_id=1, source_target_pairs={{0,2},{1,3},{2,0},{3,1},{4,6},{5,7},{6,4},{7,5}} | collective-permute-start | bytes 1572872 | tf_op jit(solution)/shard_map/ppermute | solution.py:405
  153.4 131.3 %collective-permute-start.1 = (bf16[704,1024]{1,0:T(8,128)(2,1)}, bf16[704,1024]{1,0:T(8,128)(2,1)}, u32[]{:S(2)}, u32[]{:S(2)}) collective-permute-start(bf16[704,1024]{1,0:T(8,128)(2,1)} %get-tuple-element.108.rest_0_), channel_id=1, source_target_pairs={{0,2},{1,3},{2,0},{3,1},{4,6},{5,7},{6,4},{7,5}} | collective-permute-start | bytes 4325384 | tf_op jit(solution)/shard_map/ppermute | solution.py:405
  248.7 29.9 %collective-permute-start.2 = (bf16[2,256,1024]{2,1,0:T(8,128)(2,1)}, bf16[2,256,1024]{2,1,0:T(8,128)(2,1)}, u32[]{:S(2)}, u32[]{:S(2)}) collective-permute-start(bf16[2,256,1024]{2,1,0:T(8,128)(2,1)} %get-tuple-element.113.rest_0_), channel_id=1, source_target_pairs={{0,2},{1,3},{2,0},{3,1},{4,6},{5,7},{6,4},{7,5}} | collective-permute-start | bytes 3145736 | tf_op jit(solution)/shard_map/ppermute | solution.py:405
  250.4 19.5 %copy-start.4 = (bf16[2,256,1792]{2,1,0:T(8,128)(2,1)S(1)}, bf16[2,256,1792]{2,1,0:T(8,128)(2,1)}, u32[]{:S(2)}) copy-start(bf16[2,256,1792]{2,1,0:T(8,128)(2,1)} %get-tuple-element.122) | copy-start | bytes 5505028
  269.5 35.9 %collective-permute-start.3 = (bf16[704,1024]{1,0:T(8,128)(2,1)}, bf16[704,1024]{1,0:T(8,128)(2,1)}, u32[]{:S(2)}, u32[]{:S(2)}) collective-permute-start(bf16[704,1024]{1,0:T(8,128)(2,1)} %get-tuple-element.117), channel_id=1, source_target_pairs={{0,2},{1,3},{2,0},{3,1},{4,6},{5,7},{6,4},{7,5}} | collective-permute-start | bytes 4325384 | tf_op jit(solution)/shard_map/ppermute | solution.py:405
  284.7 20.7 %copy-start.7 = (f32[704,1024]{1,0:T(8,128)S(1)}, f32[704,1024]{1,0:T(8,128)}, u32[]{:S(2)}) copy-start(f32[704,1024]{1,0:T(8,128)} %get-tuple-element.123) | copy-start | bytes 8650756
  323.7 60.7 %collective-permute-start.14 = (bf16[256,2816]{1,0:T(8,128)(2,1)}, bf16[256,2816]{1,0:T(8,128)(2,1)}, u32[]{:S(2)}, u32[]{:S(2)}) collective-permute-start(bf16[256,2816]{1,0:T(8,128)(2,1)} %get-tuple-element.139), channel_id=1, source_target_pairs={{0,2},{1,3},{2,0},{3,1},{4,6},{5,7},{6,4},{7,5}} | collective-permute-start | bytes 4325384 | tf_op jit(solution)/shard_map/ppermute | solution.py:446
  324.7 59.8 %collective-permute-start.15 = (bf16[256,2816]{1,0:T(8,128)(2,1)}, bf16[256,2816]{1,0:T(8,128)(2,1)}, u32[]{:S(2)}, u32[]{:S(2)}) collective-permute-start(bf16[256,2816]{1,0:T(8,128)(2,1)} %get-tuple-element.139), channel_id=1, source_target_pairs={{0,1},{1,0},{2,3},{3,2},{4,5},{5,4},{6,7},{7,6}} | collective-permute-start | bytes 4325384 | tf_op jit(solution)/shard_map/ppermute | solution.py:447
  330.7 61.6 %collective-permute-start.12 = (bf16[256,2816]{1,0:T(8,128)(2,1)}, bf16[256,2816]{1,0:T(8,128)(2,1)}, u32[]{:S(2)}, u32[]{:S(2)}) collective-permute-start(bf16[256,2816]{1,0:T(8,128)(2,1)} %get-tuple-element.138), channel_id=1, source_target_pairs={{0,2},{1,3},{2,0},{3,1},{4,6},{5,7},{6,4},{7,5}} | collective-permute-start | bytes 4325384 | tf_op jit(solution)/shard_map/ppermute | solution.py:446
  331.8 60.6 %collective-permute-start.13 = (bf16[256,2816]{1,0:T(8,128)(2,1)}, bf16[256,2816]{1,0:T(8,128)(2,1)}, u32[]{:S(2)}, u32[]{:S(2)}) collective-permute-start(bf16[256,2816]{1,0:T(8,128)(2,1)} %get-tuple-element.138), channel_id=1, source_target_pairs={{0,1},{1,0},{2,3},{3,2},{4,5},{5,4},{6,7},{7,6}} | collective-permute-start | bytes 4325384 | tf_op jit(solution)/shard_map/ppermute | solution.py:447
  350.2 70.0 %collective-permute-start.10 = (bf16[256,2816]{1,0:T(8,128)(2,1)}, bf16[256,2816]{1,0:T(8,128)(2,1)}, u32[]{:S(2)}, u32[]{:S(2)}) collective-permute-start(bf16[256,2816]{1,0:T(8,128)(2,1)} %get-tuple-element.134), channel_id=1, source_target_pairs={{0,2},{1,3},{2,0},{3,1},{4,6},{5,7},{6,4},{7,5}} | collective-permute-start | bytes 4325384 | tf_op jit(solution)/shard_map/ppermute | solution.py:446
  384.5 35.8 %collective-permute-start.11 = (bf16[256,2816]{1,0:T(8,128)(2,1)S(1)}, bf16[256,2816]{1,0:T(8,128)(2,1)S(1)}, u32[]{:S(2)}, u32[]{:S(2)}) collective-permute-start(bf16[256,2816]{1,0:T(8,128)(2,1)S(1)} %copy-done.10), channel_id=1, source_target_pairs={{0,1},{1,0},{2,3},{3,2},{4,5},{5,4},{6,7},{7,6}} | collective-permute-start | bytes 4325384 | tf_op jit(solution)/shard_map/ppermute | solution.py:447
  384.5 5.6 %collective-permute-start.16 = (bf16[256,2816]{1,0:T(8,128)(2,1)}, bf16[256,2816]{1,0:T(8,128)(2,1)S(1)}, u32[]{:S(2)}, u32[]{:S(2)}) collective-permute-start(bf16[256,2816]{1,0:T(8,128)(2,1)} %collective-permute-done.14), channel_id=1, source_target_pairs={{0,1},{1,0},{2,3},{3,2},{4,5},{5,4},{6,7},{7,6}} | collective-permute-start | bytes 4325384 | tf_op jit(solution)/shard_map/ppermute | solution.py:459
  390.1 60.9 %collective-permute-start.8 = (bf16[256,2816]{1,0:T(8,128)(2,1)S(1)}, bf16[256,2816]{1,0:T(8,128)(2,1)S(1)}, u32[]{:S(2)}, u32[]{:S(2)}) collective-permute-start(bf16[256,2816]{1,0:T(8,128)(2,1)S(1)} %copy-done.9), channel_id=1, source_target_pairs={{0,2},{1,3},{2,0},{3,1},{4,6},{5,7},{6,4},{7,5}} | collective-permute-start | bytes 4325384 | tf_op jit(solution)/shard_map/ppermute | solution.py:446
  392.4 58.7 %collective-permute-start.9 = (bf16[256,2816]{1,0:T(8,128)(2,1)S(1)}, bf16[256,2816]{1,0:T(8,128)(2,1)S(1)}, u32[]{:S(2)}, u32[]{:S(2)}) collective-permute-start(bf16[256,2816]{1,0:T(8,128)(2,1)S(1)} %copy-done.9), channel_id=1, source_target_pairs={{0,1},{1,0},{2,3},{3,2},{4,5},{5,4},{6,7},{7,6}} | collective-permute-start | bytes 4325384 | tf_op jit(solution)/shard_map/ppermute | solution.py:447
  392.4 5.6 %collective-permute-start.17 = (bf16[256,2816]{1,0:T(8,128)(2,1)}, bf16[256,2816]{1,0:T(8,128)(2,1)S(1)}, u32[]{:S(2)}, u32[]{:S(2)}) collective-permute-start(bf16[256,2816]{1,0:T(8,128)(2,1)} %collective-permute-done.12), channel_id=1, source_target_pairs={{0,1},{1,0},{2,3},{3,2},{4,5},{5,4},{6,7},{7,6}} | collective-permute-start | bytes 4325384 | tf_op jit(solution)/shard_map/ppermute | solution.py:459
  398.0 82.1 %collective-permute-start.6 = (bf16[704,1024]{1,0:T(8,128)(2,1)S(1)}, bf16[704,1024]{1,0:T(8,128)(2,1)S(1)}, u32[]{:S(2)}, u32[]{:S(2)}) collective-permute-start(bf16[704,1024]{1,0:T(8,128)(2,1)S(1)} %copy-done.8), channel_id=1, source_target_pairs={{0,2},{1,3},{2,0},{3,1},{4,6},{5,7},{6,4},{7,5}} | collective-permute-start | bytes 4325384 | tf_op jit(solution)/shard_map/ppermute | solution.py:446
  420.3 59.9 %collective-permute-start.7 = (bf16[704,1024]{1,0:T(8,128)(2,1)S(1)}, bf16[704,1024]{1,0:T(8,128)(2,1)S(1)}, u32[]{:S(2)}, u32[]{:S(2)}) collective-permute-start(bf16[704,1024]{1,0:T(8,128)(2,1)S(1)} %copy-done.8), channel_id=1, source_target_pairs={{0,1},{1,0},{2,3},{3,2},{4,5},{5,4},{6,7},{7,6}} | collective-permute-start | bytes 4325384 | tf_op jit(solution)/shard_map/ppermute | solution.py:447
  420.3 5.3 %collective-permute-start.18 = (bf16[256,2816]{1,0:T(8,128)(2,1)}, bf16[256,2816]{1,0:T(8,128)(2,1)S(1)}, u32[]{:S(2)}, u32[]{:S(2)}) collective-permute-start(bf16[256,2816]{1,0:T(8,128)(2,1)} %collective-permute-done.10), channel_id=1, source_target_pairs={{0,1},{1,0},{2,3},{3,2},{4,5},{5,4},{6,7},{7,6}} | collective-permute-start | bytes 4325384 | tf_op jit(solution)/shard_map/ppermute | solution.py:459
  451.1 3.2 collective-permute-start.19
  480.1 4.3 collective-permute-start.20
  480.1 34.3 %collective-permute-start.4 = (bf16[704,1024]{1,0:T(8,128)(2,1)}, bf16[704,1024]{1,0:T(8,128)(2,1)}, u32[]{:S(2)}, u32[]{:S(2)}) collective-permute-start(bf16[704,1024]{1,0:T(8,128)(2,1)} %get-tuple-element.128), channel_id=1, source_target_pairs={{0,2},{1,3},{2,0},{3,1},{4,6},{5,7},{6,4},{7,5}} | collective-permute-start | bytes 4325384 | tf_op jit(solution)/shard_map/ppermute | solution.py:446
  481.8 32.7 %collective-permute-start.5 = (bf16[704,1024]{1,0:T(8,128)(2,1)}, bf16[704,1024]{1,0:T(8,128)(2,1)}, u32[]{:S(2)}, u32[]{:S(2)}) collective-permute-start(bf16[704,1024]{1,0:T(8,128)(2,1)} %get-tuple-element.128), channel_id=1, source_target_pairs={{0,1},{1,0},{2,3},{3,2},{4,5},{5,4},{6,7},{7,6}} | collective-permute-start | bytes 4325384 | tf_op jit(solution)/shard_map/ppermute | solution.py:447
  514.4 5.1 collective-permute-start.21
  (11 other events, 94.0 us)
where the time goes:
time: 527 us; the launch traced here: 521 us
  Pallas kernels  302 us (57%)
  waiting for transfers between devices  113 us (21%)
  other arithmetic  46.6 us (9%)
  local copies, waits for them, and re-layouts  34.7 us (7%)
  starting transfers between devices  12.8 us (2%)
  blocking collectives  7.15 us (1%)
  between operations  5.59 us (1%)
    pallas_call x2, Pallas kernels, hidden(): pl.pallas_call(kernel, grid=(CHUNKS,), in_specs=[whole(normed.shape), who...  142 us
    ppermute x6, waiting for transfers between devices, step(): over = lax.ppermute(mine, 'dp', across)  96.5 us
    pallas_call x1, Pallas kernels, forward_first(): pl.pallas_call(kernel, grid=(CHUNKS,), in_specs=[whole((T, D)), pl.BlockS...  51.4 us
    pallas_call x2, Pallas kernels, down_grad(): pl.pallas_call(kernel, grid=(DP,), in_specs=[pl.BlockSpec((rows_w, T), la...  38 us
    pallas_call x6, Pallas kernels, new_weight(): pl.pallas_call(kernel, grid_spec=pltpu.PrefetchScalarGridSpec(num_scalar_...  36.5 us
    pallas_call x1, Pallas kernels, into_states(): pl.pallas_call(kernel, grid=(T // tile,), in_specs=[long, long, weight, w...  33.8 us
    dynamic_update_slice x18, local copies, waits for them, and re-layouts, step(): lax.dynamic_update_slice(full[which], piece[None], (layer, who * piece.sh...  32.4 us
    add x3, other arithmetic, step(): new_v.append(0.95 * vs[which] + 0.05 * g * g)  25.6 us
  transfers between devices with their start and end apart: 22, of which 7 were waited for; matrix products, arithmetic and copies ran while one was open for 14% of the time, Pallas kernels for 31%

commit v1 on v0

--- a/solution.py
+++ b/solution.py
@@ -12,6 +12,7 @@
 CHUNK = 256
 CHUNKS = FF // CHUNK
 ROWS = 512
+TILE = 256
 VMEM_LIMIT = 62 * 2**20
 ANY = pl.BlockSpec(memory_space=pl.ANY)
 MESH = pl.DeviceIdType.MESH
@@ -45,21 +46,21 @@
     piece = 128
     pieces = D // piece
 
-    def kernel(x_ref, wg_ref, wu_ref, wd_ref, g_ref, u_ref, t_ref, h_ref, n_ref, a_ref, acc):
+    def kernel(x_ref, wg_ref, wu_ref, wd_ref, g_ref, u_ref, t_ref, h_ref, n_ref, a_ref, held_h, acc, h_sem, n_sem):
         j = pl.program_id(0)
 
         @pl.when(j == 0)
         def _():
-            for t in range(0, T, ROWS):
-                rows = slice(t, t + ROWS)
+            @pl.loop(0, T // TILE)
+            def _(t):
+                rows = pl.ds(pl.multiple_of(t * TILE, TILE), TILE)
                 wide = x_ref[rows].astype(F32)
                 a_ref[rows] = (wide * root_mean_scale(wide)).astype(BF16)
-                acc[rows] = jnp.zeros((ROWS, D), F32)
 
         k = jnp.minimum(j, pieces - 1)
         per = D // DP // piece
         source = pl.multiple_of(block_of(k // per) * (D // DP) + lax.rem(k, per) * piece, piece)
-        t_ref[pl.ds(pl.multiple_of(k * piece, piece), piece)] = a_ref[:, pl.ds(source, piece)].T
+        t_ref[...] = a_ref[:, pl.ds(source, piece)].T
 
         for t in range(0, T, ROWS):
             rows = slice(t, t + ROWS)
@@ -69,16 +70,31 @@
             g_ref[rows] = g
             u_ref[rows] = u
             act = (g * jax.nn.sigmoid(g) * u).astype(BF16)
-            acc[rows] += dot(act, wd_ref[...])
+            acc[rows] = jnp.where(j > 0, acc[rows], 0.0) + dot(act, wd_ref[...])
 
         @pl.when(j == CHUNKS - 1)
         def _():
-            for t in range(0, T, ROWS):
-                rows = slice(t, t + ROWS)
+            def copies(t):
+                rows = pl.ds(pl.multiple_of(t * TILE, TILE), TILE)
+                return (
+                    pltpu.make_async_copy(held_h.at[rows], h_ref.at[rows], h_sem.at[t]),
+                    pltpu.make_async_copy(a_ref.at[rows], n_ref.at[rows], n_sem.at[t]),
+                )
+
+            @pl.loop(0, T // TILE)
+            def _(t):
+                rows = pl.ds(pl.multiple_of(t * TILE, TILE), TILE)
                 h = x_ref[rows] + acc[rows].astype(BF16)
-                h_ref[rows] = h
+                held_h[rows] = h
                 wide = h.astype(F32)
-                n_ref[rows] = (wide * root_mean_scale(wide)).astype(BF16)
+                a_ref[rows] = (wide * root_mean_scale(wide)).astype(BF16)
+                for one in copies(t):
+                    one.start()
+
+            @pl.loop(0, T // TILE)
+            def _(t):
+                for one in copies(t):
+                    one.wait()
 
     tall = jax.ShapeDtypeStruct((T, FF), F32)
     flat = jax.ShapeDtypeStruct((T, D), BF16)
@@ -92,9 +108,14 @@
             pl.BlockSpec((None, D, CHUNK), lambda j: (0, 0, j)),
             pl.BlockSpec((None, CHUNK, D), lambda j: (0, j, 0)),
         ],
-        out_specs=[wide_block, wide_block, whole((D, T)), whole((T, D)), whole((T, D))],
+        out_specs=[wide_block, wide_block, pl.BlockSpec((piece, T), lambda j: (jnp.minimum(j, pieces - 1), 0)), ANY, ANY],
         out_shape=[tall, tall, jax.ShapeDtypeStruct((D, T), BF16), flat, flat],
-        scratch_shapes=[pltpu.VMEM((T, D), BF16), pltpu.VMEM((T, D), F32)],
+        scratch_shapes=[
+            pltpu.VMEM((T, D), BF16),
+            pltpu.VMEM((T, D), BF16),
+            pltpu.VMEM((T, D), F32),
+            *(pltpu.SemaphoreType.DMA((T // TILE,)),) * 2,
+        ],
         compiler_params=params(),
         cost_estimate=cost(3, 90e6),
     )(x, w_gate, w_up, w_down)
@@ -132,7 +153,7 @@
     )
 
 
-def hidden(ident, layer, inside, lag, normed, by_out, weights, gate_up, after):
+def hidden(ident, layer, inside, lag, quick, normed, by_out, weights, gate_up, after):
     w_gate, w_up, w_down = weights
     computed = gate_up is None
     n_after = len(after)
@@ -159,37 +180,39 @@
         def over(k):
             return remote(far.at[k], landed.at[k], over_send.at[k], over_recv.at[k], opposite)
 
-        def add(k):
-            mine = keep.at[lax.rem(k, 2)]
-
-            def sums(which):
-                there = (mine[which, 0].astype(F32) + got[k, which, 0].astype(F32)).astype(BF16)
-                return there, mine[which, 1].astype(F32) + got[k, which, 1].astype(F32)
-
-            @pl.when(k < inside)
-            def _():
-                for which in range(2):
-                    far[k, which], near[k, which] = sums(which)
-
-            @pl.when(k >= inside)
-            def _():
-                columns = pl.ds(pl.multiple_of((k - inside) * CHUNK, CHUNK), CHUNK)
-                for which in range(2):
-                    far_ref[which, :, columns], near_ref[which, :, columns] = sums(which)
-
-        def finish(k):
-            over(k).wait()
+        def add(k, at):
+            mine = keep.at[lax.rem(k + 2, 2)]
+            for which in range(2):
+                far[at, which] = (mine[which, 0].astype(F32) + got[at, which, 0].astype(F32)).astype(BF16)
+                near[at, which] = mine[which, 1].astype(F32) + got[at, which, 1].astype(F32)
+
+        def finish(k, at):
             columns = pl.ds(pl.multiple_of(k * CHUNK, CHUNK), CHUNK)
             for which in range(2):
-                sum_ref[which, :, columns] = (near[k, which] + landed[k, which].astype(F32)).astype(BF16)
+                sum_ref[which, :, columns] = (near[k, which] + landed[at, which].astype(F32)).astype(BF16)
+
+        barrier = pltpu.get_barrier_semaphore()
 
         @pl.when(j == 0)
         def _():
-            greet(sib, opposite)
+            for other in (sib, opposite):
+                pl.semaphore_signal(barrier, inc=1, device_id={"dp": other}, device_id_type=MESH)
             if computed:
-                for k in range(DP):
+
+                @pl.loop(0, DP)
+                def _(k):
                     columns = pl.ds(pl.multiple_of(block_of(k) * rows_w, rows_w), rows_w)
-                    n_t[k * rows_w : (k + 1) * rows_w] = n_ref[:, columns].T
+                    n_t[pl.ds(pl.multiple_of(k * rows_w, rows_w), rows_w)] = n_ref[:, columns].T
+
+        if not quick:
+
+            @pl.when(j > 1)
+            def _():
+                beside(j - 2).wait()
+
+        @pl.when((j >= lag) & (j < lag + inside))
+        def _():
+            over(j - lag).wait()
 
         for t in range(0, T, ROWS):
             rows = slice(t, t + ROWS)
@@ -205,33 +228,56 @@
             du_ref[rows] = (p * silu).astype(BF16)
             dg_ref[rows] = (p * u * (sig + silu * (1.0 - sig))).astype(BF16)
 
-        @pl.when(j > 0)
-        def _():
-            beside(j - 1).wait()
-            add(j - 1)
-
+        if not quick:
+            add(j - 2, jnp.where(j > 1, j - 2, CHUNKS))
+        finish(jnp.clip(j - lag, 0, inside - 1), jnp.where(j < lag, inside, jnp.minimum(j - lag, inside - 1)))
         act_ref[...] = act[...].T
         half = D // CORES
         for which, d_ref in ((0, dg_ref), (1, du_ref)):
             out[lax.rem(j, 2), which] = dot(n_t[:half], d_ref[...]).astype(BF16).reshape(CORES, rows_w, CHUNK)
         for which, d_ref in ((0, dg_ref), (1, du_ref)):
             keep[lax.rem(j, 2), which] = dot(n_t[half:], d_ref[...]).astype(BF16).reshape(CORES, rows_w, CHUNK)
+
+        @pl.when(j == 0)
+        def _():
+            pl.semaphore_wait(barrier, 2)
+
         beside(j).start()
-
-        @pl.when((j > 0) & (j <= inside))
-        def _():
-            over(j - 1).start()
-
-        @pl.when((j >= lag) & (j < lag + inside))
-        def _():
-            finish(j - lag)
+        late = 1 if quick else 2
+
+        def meet(k):
+            beside(k).wait()
+            add(k, k)
+
+        if quick:
+
+            @pl.when(j == 0)
+            def _():
+                meet(0)
+                over(0).start()
+
+            @pl.when(j > 1)
+            def _():
+                meet(j - 1)
+
+        @pl.when((j >= 2) & (j < inside + late))
+        def _():
+            over(j - late).start()
 
         @pl.when(j == CHUNKS - 1)
         def _():
-            beside(j).wait()
-            add(j)
-            for k in range(CHUNKS - lag, inside):
-                finish(k)
+            pl.loop(CHUNKS - late, CHUNKS)(meet)
+
+            @pl.loop(CHUNKS - lag, inside)
+            def _(k):
+                over(k).wait()
+                finish(k, k)
+
+            @pl.loop(inside, CHUNKS)
+            def _(k):
+                columns = pl.ds(pl.multiple_of((k - inside) * CHUNK, CHUNK), CHUNK)
+                for which in range(2):
+                    far_ref[which, :, columns], near_ref[which, :, columns] = far[k, which], near[k, which]
 
     column = pl.BlockSpec((None, D, CHUNK), lambda j: (layer, 0, j))
     block = pl.BlockSpec((T, CHUNK), lambda j: (0, j))
@@ -239,15 +285,15 @@
     turned = pl.BlockSpec((CHUNK, T), lambda j: (j, 0))
     out_specs = [whole(inner), whole(outer), whole(outer), turned]
     out_shape = [(inner, BF16), (outer, BF16), (outer, F32), ((FF, T), BF16)]
-    part, block_part = (2, CORES, rows_w, CHUNK), (inside, 2, rows_w, CHUNK)
+    part, block_part = (2, CORES, rows_w, CHUNK), (2, rows_w, CHUNK)
     scratch = [
         pltpu.VMEM((T, CHUNK), BF16),
         pltpu.VMEM((2, *part), BF16),
         pltpu.VMEM((2, *part), BF16),
-        pltpu.VMEM((CHUNKS, *part), BF16),
-        pltpu.VMEM(block_part, BF16),
-        pltpu.VMEM(block_part, F32),
-        pltpu.VMEM(block_part, BF16),
+        pltpu.VMEM((CHUNKS + 1, *part), BF16),
+        pltpu.VMEM((CHUNKS + 1, *block_part), BF16),
+        pltpu.VMEM((CHUNKS + 1, *block_part), F32),
+        pltpu.VMEM((inside + 1, *block_part), BF16),
         *(pltpu.SemaphoreType.DMA((CHUNKS,)),) * 2,
         *(pltpu.SemaphoreType.DMA((inside,)),) * 2,
     ]
@@ -275,19 +321,28 @@
     )(normed, by_out, w_down, *((w_gate, w_up) if computed else gate_up), *after)
 
 
-def down_grad(ident, act_t, by_out, first, count, after):
+def down_grad(ident, act_t, by_out, parts, after):
     n_after = len(after)
     rows_w = FF // DP
 
     def kernel(act_ref, by_ref, *rest):
-        far_ref, near_ref, out, got, send_sem, recv_sem = rest[n_after:]
+        *far_refs, near_ref, out, got, send_sem, recv_sem = rest[n_after:]
         i = pl.program_id(0)
         sib = peers()[2]
 
         def copy(k):
             return remote(out.at[k], got.at[k], send_sem.at[k], recv_sem.at[k], sib)
 
-        pl.when(i == 0)(lambda: greet(sib))
+        barrier = pltpu.get_barrier_semaphore()
+
+        @pl.when(i == 0)
+        def _():
+            pl.semaphore_signal(barrier, inc=1, device_id={"dp": sib}, device_id_type=MESH)
+
+        @pl.when(i == 1)
+        def _():
+            pl.semaphore_wait(barrier, 1)
+
         term = dot(act_ref[...], by_ref[...]).astype(BF16)
 
         @pl.when(i < CORES)
@@ -303,24 +358,26 @@
         @pl.when(i == CORES)
         def _():
             copy(0).wait()
-            far_ref[...] = (term.astype(F32) + got[0].astype(F32)).astype(BF16)
+            far = (term.astype(F32) + got[0].astype(F32)).astype(BF16)
+            for k, far_ref in enumerate(far_refs):
+                far_ref[...] = far[:, k * D // parts : (k + 1) * D // parts]
 
         @pl.when(i == CORES + 1)
         def _():
             copy(1).wait()
             near_ref[...] = term.astype(F32) + got[1].astype(F32)
 
-    shape = (rows_w, count)
+    shape, far_shape = (rows_w, D), (rows_w, D // parts)
     return pl.pallas_call(
         kernel,
         grid=(DP,),
         in_specs=[
             pl.BlockSpec((rows_w, T), lambda i: (block_of(i), 0)),
-            pl.BlockSpec((T, count), lambda i: (0, first // count), pipeline_mode=pl.Buffered(1)),
+            whole((T, D)),
             *(ANY,) * n_after,
         ],
-        out_specs=[whole(shape), whole(shape)],
-        out_shape=[jax.ShapeDtypeStruct(shape, BF16), jax.ShapeDtypeStruct(shape, F32)],
+        out_specs=[*(whole(far_shape),) * parts, whole(shape)],
+        out_shape=[*(jax.ShapeDtypeStruct(far_shape, BF16),) * parts, jax.ShapeDtypeStruct(shape, F32)],
         scratch_shapes=[
             pltpu.VMEM((CORES, *shape), BF16),
             pltpu.VMEM((CORES, *shape), BF16),
@@ -328,8 +385,71 @@
             pltpu.SemaphoreType.DMA((CORES,)),
         ],
         compiler_params=remote_params(ident),
-        cost_estimate=cost(count / D, 20e6),
+        cost_estimate=cost(1, 20e6),
     )(act_t, by_out, *after)
+
+
+def clip_and_first(ident, squares, g, m, v, w):
+    rows, columns = g.shape
+    tile = 64
+
+    def kernel(squares_ref, g_ref, m_ref, v_ref, w_ref, factor_ref, out_ref, held_g, held_m, held_v, held_w, mine, theirs, load, send_sem, recv_sem):
+        chip, core, sib, opposite = peers()
+        own = pl.ds(pl.multiple_of((chip * CORES + core) * rows, rows), rows)
+        loads = [
+            pltpu.make_async_copy(g_ref, held_g, load.at[0]),
+            pltpu.make_async_copy(m_ref.at[0], held_m, load.at[1]),
+            pltpu.make_async_copy(v_ref.at[0], held_v, load.at[2]),
+            pltpu.make_async_copy(w_ref.at[0, own], held_w, load.at[3]),
+        ]
+        for one in loads:
+            one.start()
+        mine[...] = jnp.full(mine.shape, squares_ref[0], F32)
+        others = (sib, opposite, opposite + 1 - 2 * core)
+        greet(*others)
+        copies = [remote(mine, theirs.at[k], send_sem.at[k], recv_sem.at[k], other) for k, other in enumerate(others)]
+        for one in copies:
+            one.start()
+        for one in copies:
+            one.wait()
+        total = (mine[...] + theirs[0]) + (theirs[1] + theirs[2])
+        factor = jnp.minimum(1.0, 0.5 * lax.rsqrt(total / COUNT + 1e-30))
+        factor_ref[...] = factor
+        for one in loads:
+            one.wait()
+
+        @pl.loop(0, rows // tile)
+        def _(t):
+            at = pl.ds(pl.multiple_of(t * tile, tile), tile)
+            out_ref[at] = updated(factor[:1, :1], held_g[at], held_m[at], held_v[at], held_w[at])
+
+    return pl.pallas_call(
+        kernel,
+        in_specs=[pl.BlockSpec(memory_space=pltpu.SMEM), *(ANY,) * 4],
+        out_specs=[pl.BlockSpec(memory_space=pltpu.VMEM)] * 2,
+        out_shape=[jax.ShapeDtypeStruct((8, 128), F32), jax.ShapeDtypeStruct((rows, columns), BF16)],
+        scratch_shapes=[
+            pltpu.VMEM((rows, columns), BF16),
+            pltpu.VMEM((rows, columns), F32),
+            pltpu.VMEM((rows, columns), F32),
+            pltpu.VMEM((rows, columns), BF16),
+            pltpu.VMEM((8, 128), F32),
+            pltpu.VMEM((DP - 1, 8, 128), F32),
+            pltpu.SemaphoreType.DMA((4,)),
+            pltpu.SemaphoreType.DMA((DP - 1,)),
+            pltpu.SemaphoreType.DMA((DP - 1,)),
+        ],
+        compiler_params=pltpu.CompilerParams(vmem_limit_bytes=VMEM_LIMIT, collective_id=ident, has_side_effects=True),
+        cost_estimate=cost(0.1, 10e6),
+    )(squares.reshape(1), g, m, v, w)
+
+
+def updated(factor, g, m, v, w):
+    g = g.astype(F32) * factor
+    m = 0.9 * m + 0.1 * g
+    v = 0.95 * v + 0.05 * g * g
+    w = w.astype(F32)
+    return (w - 0.02 * (m * lax.rsqrt(v + 1e-8) + 0.1 * w)).astype(BF16)
 
 
 def new_weight(layer, me, factor, g, m, v, w, full):
@@ -340,11 +460,7 @@
 
     def kernel(me_ref, factor_ref, g_ref, m_ref, v_ref, w_ref, *rest):
         out_ref, full_ref = rest[n_full:]
-        g = g_ref[...].astype(F32) * factor_ref[0]
-        m = 0.9 * m_ref[...] + 0.1 * g
-        v = 0.95 * v_ref[...] + 0.05 * g * g
-        w = w_ref[...].astype(F32)
-        new = (w - 0.02 * (m * lax.rsqrt(v + 1e-8) + 0.1 * w)).astype(BF16)
+        new = updated(factor_ref[:1, :1], g_ref[...], m_ref[...], v_ref[...], w_ref[...])
         out_ref[...] = new
         full_ref[...] = new
 
@@ -356,14 +472,14 @@
         grid_spec=pltpu.PrefetchScalarGridSpec(
             num_scalar_prefetch=1,
             grid=(steps,),
-            in_specs=[pl.BlockSpec(memory_space=pltpu.SMEM), mine, state, state, own, *(ANY,) * n_full],
+            in_specs=[whole((8, 128)), mine, state, state, own, *(ANY,) * n_full],
             out_specs=[mine, own],
         ),
         out_shape=[jax.ShapeDtypeStruct((rows, columns), BF16), jax.ShapeDtypeStruct(w.shape, BF16)],
         input_output_aliases={6: 1} if n_full else {},
         compiler_params=params(),
         cost_estimate=cost(0.1, 10e6),
-    )(me.reshape(1), factor.reshape(1), g, m, v, w, *((full,) if n_full else ()))
+    )(me.reshape(1), factor, g, m, v, w, *((full,) if n_full else ()))
 
 
 def into_states(dg, du, w_gate, w_up, h, by_out, after):
@@ -406,18 +522,19 @@
 
         g1, u1, a1, h1, a2 = forward_first(x, *weights)
         units = {}
-        sum_b, far, near, act2, dg2, du2 = hidden(0, 1, 9, 3, a2, dy, weights, None, ())
+        sum_b, far, near, act2, dg2, du2 = hidden(0, 1, 8, 6, False, a2, dy, weights, None, ())
         units["b"] = near, cross(far)
-        far, near = down_grad(1, act2, dy, 0, D, (far,))
+        far, near = down_grad(1, act2, dy, 1, (far,))
         units["d"] = near, cross(far)
         dh1 = into_states(dg2, du2, w_gate, w_up, h1, dy, (far,))
-        sum_e, far, near, act1 = hidden(2, 0, 7, 5, a1, dh1, weights, (g1, u1), ())
+        sum_e, far, near, act1 = hidden(2, 0, 7, 7, True, a1, dh1, weights, (g1, u1), ())
         units["e"] = near, cross(far)
-        far, near = down_grad(3, act1, dh1, 0, D, (far,))
-        units["f"] = near, cross(far)
+        *fars, near = down_grad(3, act1, dh1, 2, (far,))
+        for k, far in enumerate(fars):
+            units[f"f{k}"] = near[:, k * D // 2 : (k + 1) * D // 2], cross(far)
 
         nears = {name: near for name, (near, _) in units.items()}
-        nears, sum_b, sum_e, _ = lax.optimization_barrier((nears, sum_b, sum_e, far))
+        nears, sum_b, sum_e, _ = lax.optimization_barrier((nears, sum_b, sum_e, fars))
         units = {name: (nears[name], landed) for name, (_, landed) in units.items()}
         grads, squared = {}, []
         for name, (near, landed) in units.items():
@@ -430,23 +547,25 @@
 
         def of(which, layer):
             if which == 2:
-                return grads["d" if layer else "f"]
+                return grads["d"] if layer else jnp.concatenate([grads["f0"], grads["f1"]], 1)
             return grads["b" if layer else "e"][which]
 
         each = {(which, layer): of(which, layer) for which in range(3) for layer in range(2)}
         squares, each = lax.optimization_barrier((sum(squared), each))
-        squares = lax.psum(squares, "dp")
-        factor = jnp.minimum(1.0, 0.5 * lax.rsqrt(squares / COUNT + 1e-30))
 
         ms, vs = (m_gate, m_up, m_down), (v_gate, v_up, v_down)
         full, sent = [None] * 3, []
         for (which, layer), g in each.items():
             name = f"{which}{layer}"
-            mine, full[which] = new_weight(layer, me, factor, g, ms[which], vs[which], weights[which], full[which])
+            if not sent:
+                factor, mine = clip_and_first(4, squares, g, ms[which], vs[which], weights[which])
+            else:
+                mine, full[which] = new_weight(layer, me, factor, g, ms[which], vs[which], weights[which], full[which])
             over = lax.ppermute(mine, "dp", across)
             beside = lax.ppermute(mine, "dp", sibling)
             sent.append((which, layer, over, beside))
-        factor, _ = lax.optimization_barrier((factor, mine))
+            first = mine if which + layer == 0 else first
+        factor, _ = lax.optimization_barrier((factor[0, 0], mine))
         new_m, new_v = [], []
         for which in range(3):
             g = jnp.stack([each[which, 0], each[which, 1]]).astype(F32) * factor
@@ -457,7 +576,8 @@
                 full, new_m[k - 1], new_v[k - 1] = lax.optimization_barrier((full, new_m[k - 1], new_v[k - 1]))
             over, beside, full = lax.optimization_barrier((over, beside, full))
             corner = lax.ppermute(over, "dp", sibling)
-            for piece, who in ((beside, me ^ 1), (over, me ^ 2), (corner, me ^ 3)):
+            own = ((first, me),) if k == 0 else ()
+            for piece, who in (*own, (beside, me ^ 1), (over, me ^ 2), (corner, me ^ 3)):
                 full[which] = lax.dynamic_update_slice(full[which], piece[None], (layer, who * piece.shape[0], 0))
         return (*full, *new_m, *new_v)
 

time: 527 us -> 533 us (1.011)
  blocking collectives: 7.15 us -> 0 us
  waiting for transfers between devices: 113 us -> 119 us
    ppermute x4 -> x5, waiting for transfers between devices: 14.1 us -> 26.3 us  [cross(): return lax.ppermute(far, 'dp', across)]
    pallas_call x0 -> x1, Pallas kernels: none -> 8.02 us  [clip_and_first(): pl.pallas_call(kernel, in_specs=[pl.BlockSpec(memory_space=pltpu.SMEM), *...]
    psum x1 -> x0, blocking collectives: 7.15 us -> none  [step(): squares = lax.psum(squares, 'dp')]
    pallas_call x2, Pallas kernels: 142 us -> 136 us  [hidden(): pl.pallas_call(kernel, grid=(CHUNKS,), in_specs=[whole(normed.shape), who...]
    ppermute x6, waiting for transfers between devices: 96.5 us -> 91.2 us  [step(): over = lax.ppermute(mine, 'dp', across)]
    pallas_call x6 -> x5, Pallas kernels: 36.5 us -> 34.8 us  [new_weight(): pl.pallas_call(kernel, grid_spec=pltpu.PrefetchScalarGridSpec(num_scalar_...]
    dynamic_update_slice x18 -> x19, local copies, waits for them, and re-layouts: 32.4 us -> 33.7 us  [step(): lax.dynamic_update_slice(full[which], piece[None], (layer, who * piece.sh...]
    reduce_sum x4 -> x5, other arithmetic: 12.9 us -> 12.9 us  [step(): squared.append(jnp.sum(grads[name].astype(F32) ** 2))]
  transfers between devices with their start and end apart: 22 -> 23, of which waited for: 7 -> 9; matrix products, arithmetic and copies ran while one was open for 14% -> 15% of each run, Pallas kernels for 31% -> 32%
where the time goes in v1:
time: 533 us; the launch traced here: 524 us
  Pallas kernels  301 us (56%)
  waiting for transfers between devices  119 us (22%)
  other arithmetic  46.7 us (9%)
  local copies, waits for them, and re-layouts  39.8 us (7%)
  starting transfers between devices  12 us (2%)
  between operations  5.56 us (1%)
    pallas_call x2, Pallas kernels, hidden(): pl.pallas_call(kernel, grid=(CHUNKS,), in_specs=[whole(normed.shape), who...  136 us
    ppermute x6, waiting for transfers between devices, step(): over = lax.ppermute(mine, 'dp', across)  91.2 us
    pallas_call x1, Pallas kernels, forward_first(): pl.pallas_call(kernel, grid=(CHUNKS,), in_specs=[whole((T, D)), pl.BlockS...  49.5 us
    pallas_call x2, Pallas kernels, down_grad(): pl.pallas_call(kernel, grid=(DP,), in_specs=[pl.BlockSpec((rows_w, T), la...  38.2 us
    pallas_call x5, Pallas kernels, new_weight(): pl.pallas_call(kernel, grid_spec=pltpu.PrefetchScalarGridSpec(num_scalar_...  34.8 us
    pallas_call x1, Pallas kernels, into_states(): pl.pallas_call(kernel, grid=(T // tile,), in_specs=[long, long, weight, w...  34.1 us
    dynamic_update_slice x19, local copies, waits for them, and re-layouts, step(): lax.dynamic_update_slice(full[which], piece[None], (layer, who * piece.sh...  33.7 us
    ppermute x5, waiting for transfers between devices, cross(): return lax.ppermute(far, 'dp', across)  26.3 us
  transfers between devices with their start and end apart: 23, of which 9 were waited for; matrix products, arithmetic and copies ran while one was open for 15% of the time, Pallas kernels for 32%

profile of v1, /device:TPU:0, one launch (start us, length us, event | category | flops | bytes accessed | tf_op | source)
XLA Modules:
  0.0 524.4 jit_solution(16663627951601334544)
XLA Ops:
  0.6 49.5 %shard_map.178 = (f32[2048,2816]{1,0:T(8,128)}, f32[2048,2816]{1,0:T(8,128)}, bf16[1024,2048]{1,0:T(8,128)(2,1)}, bf16[2048,1024]{1,0:T(8,128)(2,1)}, bf16[2048,1024]{1,0:T(8,128)(2,1)}) custom-call(bf16[2048,1024]{1,0:T(8,128)(2,1)} %bitcast.67, bf16[2,1024,2816]{2,1,0:T(8,128)(2,1)} %w_ref.11, bf16[2,1024,2816]{2,1,0:T(8,128)(2,1)} %w_ref.10, ...), custom_call_target="tpu_custom_call" | custom-call | flops 35433480192 | bytes 90000000 | tf_op jit(solution)/shard_map/pallas_call | solution.py:102
  50.1 78.2 %shard_map.179 = (bf16[2,256,2048]{2,1,0:T(8,128)(2,1)}, bf16[2,256,768]{2,1,0:T(8,128)(2,1)}, f32[2,256,768]{2,1,0:T(8,128)}, bf16[2816,2048]{1,0:T(8,128)(2,1)...) custom-call(bf16[2048,1024]{1,0:T(8,128)(2,1)} %get-tuple-element.101.n_ref, bf16[2048,1024]{1,0:T(8,128)(2,1)} %bitcast.68, ...), custom_call_target="tpu_custom_call" | custom-call | flops 59055800320 | bytes 60000000 | tf_op jit(solution)/shard_map/pallas_call | solution.py:306
  129.7 18.9 %shard_map.180 = (bf16[704,1024]{1,0:T(8,128)(2,1)}, f32[704,1024]{1,0:T(8,128)}) custom-call(bf16[2816,2048]{1,0:T(8,128)(2,1)} %get-tuple-element.103.act_ref, bf16[2048,1024]{1,0:T(8,128)(2,1)} %bitcast.69, bf16[2,256,768]{2,1,0:T(8,128)(2,1)} %get-tuple-element.104.rest_0_), custom_call_target="tpu_custom_call" | custom-call | flops 11811160064 | bytes 20000000 | tf_op jit(solution)/shard_map/pallas_call | solution.py:371
  149.2 34.1 %shard_map.181.by_ref = bf16[2048,1024]{1,0:T(8,128)(2,1)} custom-call(bf16[2048,2816]{1,0:T(8,128)(2,1)} %get-tuple-element.107.dg_ref, bf16[2048,2816]{1,0:T(8,128)(2,1)} %get-tuple-element.108.du_ref, bf16[2,1024,2816]{2,1,0:T(8,128)(2,1)} %w_ref.11, bf16[2,1024,2816]{2,1,0:T(8,128)(2,1)} %w_ref.10, bf16[2048,1024]{1,0:T(8,128)(2,1)} %get-tuple-element.109.h_ref, ...), custom_call_target="tpu_custom_call" | custom-call | flops 23622320128 | bytes 50000000 | tf_op jit(solution)/shard_map/pallas_call | solution.py:500
  183.3 58.1 %shard_map.182 = (bf16[2,256,1792]{2,1,0:T(8,128)(2,1)}, bf16[2,256,1024]{2,1,0:T(8,128)(2,1)}, f32[2,256,1024]{2,1,0:T(8,128)}, bf16[2816,2048]{1,0:T(8,128)(2,1)}) custom-call(bf16[1024,2048]{1,0:T(8,128)(2,1)} %get-tuple-element.106.n_ref, bf16[2048,1024]{1,0:T(8,128)(2,1)} %shard_map.181.by_ref, bf16[2,2816,1024]{2,1,0:T(8,128)(2,1)} %w_ref.8, ...), custom_call_target="tpu_custom_call" | custom-call | flops 35433480192 | bytes 60000000 | tf_op jit(solution)/shard_map/pallas_call | solution.py:306
  242.1 19.3 %shard_map.183 = (bf16[704,512]{1,0:T(8,128)(2,1)}, bf16[704,512]{1,0:T(8,128)(2,1)}, f32[704,1024]{1,0:T(8,128)}) custom-call(bf16[2816,2048]{1,0:T(8,128)(2,1)} %get-tuple-element.114.act_ref, bf16[2048,1024]{1,0:T(8,128)(2,1)} %shard_map.181.by_ref, bf16[2,256,1024]{2,1,0:T(8,128)(2,1)} %get-tuple-element.115.rest_0_), custom_call_target="tpu_custom_call" | custom-call | flops 11811160064 | bytes 20000000 | tf_op jit(solution)/shard_map/pallas_call | solution.py:371
  269.2 14.1 %collective-permute-done.4 = bf16[704,512]{1,0:T(8,128)(2,1)} collective-permute-done((bf16[704,512]{1,0:T(8,128)(2,1)}, bf16[704,512]{1,0:T(8,128)(2,1)}, u32[]{:S(2)}, u32[]{:S(2)}) %collective-permute-start.4) | collective-permute-done | bytes 720928 | tf_op jit(solution)/shard_map/ppermute | solution.py:521
  285.4 12.2 %collective-permute-done.3 = bf16[704,512]{1,0:T(8,128)(2,1)} collective-permute-done((bf16[704,512]{1,0:T(8,128)(2,1)}, bf16[704,512]{1,0:T(8,128)(2,1)}, u32[]{:S(2)}, u32[]{:S(2)}) %collective-permute-start.3) | collective-permute-done | bytes 720928 | tf_op jit(solution)/shard_map/ppermute | solution.py:521
  306.8 3.7 fusion.7
  310.7 4.1 multiply_reduce_fusion.2
  318.1 8.0 %shard_map.184 = (f32[8,128]{1,0:T(8,128)}, bf16[256,2816]{1,0:T(8,128)(2,1)}) custom-call(f32[1]{0:T(128)} %bitcast.7.squares_ref, bf16[256,2816]{1,0:T(8,128)(2,1)} %get-tuple-element.129.g_ref, f32[2,256,2816]{2,1,0:T(8,128)} %m_ref.11, f32[2,256,2816]{2,1,0:T(8,128)} %v_ref.11, bf16[2,1024,2816]{2,1,0:T(8,128)(2,1)} %w_ref.11), custom_call_target="tpu_custom_call" | custom-call | flops 1181116032 | bytes 10000000 | tf_op jit(solution)/shard_map/pallas_call | solution.py:426
  328.0 6.9 %shard_map.189 = (bf16[256,2816]{1,0:T(8,128)(2,1)}, bf16[2,1024,2816]{2,1,0:T(8,128)(2,1)}) custom-call(s32[1]{0:T(128)} %bitcast.me_ref, f32[8,128]{1,0:T(8,128)} %get-tuple-element.130.factor_ref, bf16[256,2816]{1,0:T(8,128)(2,1)} %get-tuple-element.141.g_ref, f32[2,256,2816]{2,1,0:T(8,128)} %m_ref.11, f32[2,256,2816]{2,1,0:T(8,128)} %v_ref.11, ...), custom_call_target="tpu_custom_call" | custom-call | flops 1181116032 | bytes 10000000 | tf_op jit(solution)/shard_map/pallas_call | solution.py:470
  336.5 6.9 %shard_map.185 = (bf16[704,1024]{1,0:T(8,128)(2,1)}, bf16[2,2816,1024]{2,1,0:T(8,128)(2,1)}) custom-call(s32[1]{0:T(128)} %bitcast.me_ref, f32[8,128]{1,0:T(8,128)} %get-tuple-element.130.factor_ref, bf16[704,1024]{1,0:T(8,128)(2,1)} %pad_maximum_fusion.5.g_ref, f32[2,704,1024]{2,1,0:T(8,128)} %m_ref.8, f32[2,704,1024]{2,1,0:T(8,128)} %v_ref.8, ...), custom_call_target="tpu_custom_call" | custom-call | flops 1181116032 | bytes 10000000 | tf_op jit(solution)/shard_map/pallas_call | solution.py:470
  343.4 6.9 %shard_map.186 = (bf16[704,1024]{1,0:T(8,128)(2,1)}, bf16[2,2816,1024]{2,1,0:T(8,128)(2,1)}) custom-call(s32[1]{0:T(128)} %bitcast.me_ref, f32[8,128]{1,0:T(8,128)} %get-tuple-element.130.factor_ref, bf16[704,1024]{1,0:T(8,128)(2,1)} %get-tuple-element.131.g_ref, f32[2,704,1024]{2,1,0:T(8,128)} %m_ref.8, ...), custom_call_target="tpu_custom_call", output_to_operand_aliasing={{1}: (6, {})} | custom-call | flops 1181116032 | bytes 10000000 | tf_op jit(solution)/shard_map/pallas_call | solution.py:470
  350.3 6.9 %shard_map.187 = (bf16[256,2816]{1,0:T(8,128)(2,1)}, bf16[2,1024,2816]{2,1,0:T(8,128)(2,1)}) custom-call(s32[1]{0:T(128)} %bitcast.me_ref, f32[8,128]{1,0:T(8,128)} %get-tuple-element.130.factor_ref, bf16[256,2816]{1,0:T(8,128)(2,1)} %get-tuple-element.137.g_ref, f32[2,256,2816]{2,1,0:T(8,128)} %m_ref.10, f32[2,256,2816]{2,1,0:T(8,128)} %v_ref.10, ...), custom_call_target="tpu_custom_call" | custom-call | flops 1181116032 | bytes 10000000 | tf_op jit(solution)/shard_map/pallas_call | solution.py:470
  358.0 10.7 %fusion.1 = (f32[2,256,2816]{2,1,0:T(8,128)}, f32[2,256,2816]{2,1,0:T(8,128)}) fusion(f32[2,256,2816]{2,1,0:T(8,128)} %v_ref.10, f32[]{:T(128)} %bitcast.14, bf16[1,256,2816]{2,1,0:T(8,128)(2,1)S(1)} %bitcast.61, bf16[1,256,2816]{2,1,0:T(8,128)(2,1)} %bitcast.65, f32[2,256,2816]{2,1,0:T(8,128)} %m_ref.10), kind=kLoop, calls=%fused_computation.4 | loop fusion | flops 14417920 | bytes 25952260 | tf_op jit(solution)/shard_map/add | solution.py:573
  370.9 6.0 %fusion.2 = (f32[2,704,1024]{2,1,0:T(8,128)}, f32[2,704,1024]{2,1,0:T(8,128)}) fusion(f32[2,704,1024]{2,1,0:T(8,128)S(1)} %bitcast.60, f32[]{:T(128)} %bitcast.14, bf16[1,704,1024]{2,1,0:T(8,128)(2,1)S(1)} %bitcast.62, bf16[1,704,1024]{2,1,0:T(8,128)(2,1)S(1)} %bitcast.63, f32[2,704,1024]{2,1,0:T(8,128)S(1)} %bitcast.58), kind=kLoop, calls=%fused_computation.5 | loop fusion | flops 14417920 | bytes 25952260 | tf_op jit(solution)/shard_map/add | solution.py:573
  376.9 7.3 %shard_map.188 = (bf16[256,2816]{1,0:T(8,128)(2,1)}, bf16[2,1024,2816]{2,1,0:T(8,128)(2,1)}) custom-call(s32[1]{0:T(128)} %bitcast.me_ref, f32[8,128]{1,0:T(8,128)} %get-tuple-element.130.factor_ref, bf16[256,2816]{1,0:T(8,128)(2,1)} %copy-done, f32[2,256,2816]{2,1,0:T(8,128)} %m_ref.10, f32[2,256,2816]{2,1,0:T(8,128)} %v_ref.10, ...), custom_call_target="tpu_custom_call", output_to_operand_aliasing={{1}: (6, {})} | custom-call | flops 1181116032 | bytes 10000000 | tf_op jit(solution)/shard_map/pallas_call | solution.py:470
  384.2 8.9 %fusion = (f32[2,256,2816]{2,1,0:T(8,128)}, f32[2,256,2816]{2,1,0:T(8,128)}) fusion(f32[2,256,2816]{2,1,0:T(8,128)} %v_ref.11, f32[]{:T(128)} %bitcast.14, bf16[1,256,2816]{2,1,0:T(8,128)(2,1)S(1)} %bitcast.64, bf16[1,256,2816]{2,1,0:T(8,128)(2,1)} %bitcast.66, f32[2,256,2816]{2,1,0:T(8,128)} %m_ref.11), kind=kLoop, calls=%fused_computation.3 | loop fusion | flops 14417920 | bytes 25952260 | tf_op jit(solution)/shard_map/add | solution.py:573
  394.9 2.7 bitcast_dynamic-update-slice_fusion.17
  409.9 12.8 %collective-permute-done.11 = bf16[256,2816]{1,0:T(8,128)(2,1)} collective-permute-done((bf16[256,2816]{1,0:T(8,128)(2,1)}, bf16[256,2816]{1,0:T(8,128)(2,1)}, u32[]{:S(2)}, u32[]{:S(2)}) %collective-permute-start.11) | collective-permute-done | bytes 1441824 | tf_op jit(solution)/shard_map/ppermute | solution.py:564
  429.2 24.3 %collective-permute-done.9 = bf16[256,2816]{1,0:T(8,128)(2,1)S(1)} collective-permute-done((bf16[256,2816]{1,0:T(8,128)(2,1)S(1)}, bf16[256,2816]{1,0:T(8,128)(2,1)S(1)}, u32[]{:S(2)}, u32[]{:S(2)}) %collective-permute-start.9) | collective-permute-done | bytes 1441824 | tf_op jit(solution)/shard_map/ppermute | solution.py:564
  457.9 25.6 %collective-permute-done.7 = bf16[704,1024]{1,0:T(8,128)(2,1)S(1)} collective-permute-done((bf16[704,1024]{1,0:T(8,128)(2,1)S(1)}, bf16[704,1024]{1,0:T(8,128)(2,1)S(1)}, u32[]{:S(2)}, u32[]{:S(2)}) %collective-permute-start.7) | collective-permute-done | bytes 1441824 | tf_op jit(solution)/shard_map/ppermute | solution.py:564
  489.5 28.4 %collective-permute-done.5 = bf16[704,1024]{1,0:T(8,128)(2,1)} collective-permute-done((bf16[704,1024]{1,0:T(8,128)(2,1)}, bf16[704,1024]{1,0:T(8,128)(2,1)}, u32[]{:S(2)}, u32[]{:S(2)}) %collective-permute-start.5) | collective-permute-done | bytes 1441824 | tf_op jit(solution)/shard_map/ppermute | solution.py:564
  (103 shorter events, 64.4 us)
Async XLA Ops:
  128.3 172.6 %collective-permute-start = (bf16[2,256,768]{2,1,0:T(8,128)(2,1)}, bf16[2,256,768]{2,1,0:T(8,128)(2,1)}, u32[]{:S(2)}, u32[]{:S(2)}) collective-permute-start(bf16[2,256,768]{2,1,0:T(8,128)(2,1)} %get-tuple-element.104.rest_0_), channel_id=1, source_target_pairs={{0,2},{1,3},{2,0},{3,1},{4,6},{5,7},{6,4},{7,5}} | collective-permute-start | bytes 2359304 | tf_op jit(solution)/shard_map/ppermute | solution.py:521
  148.6 162.0 %collective-permute-start.1 = (bf16[704,1024]{1,0:T(8,128)(2,1)}, bf16[704,1024]{1,0:T(8,128)(2,1)}, u32[]{:S(2)}, u32[]{:S(2)}) collective-permute-start(bf16[704,1024]{1,0:T(8,128)(2,1)} %get-tuple-element.110.rest_0_), channel_id=1, source_target_pairs={{0,2},{1,3},{2,0},{3,1},{4,6},{5,7},{6,4},{7,5}} | collective-permute-start | bytes 4325384 | tf_op jit(solution)/shard_map/ppermute | solution.py:521
  241.5 63.0 %collective-permute-start.2 = (bf16[2,256,1024]{2,1,0:T(8,128)(2,1)}, bf16[2,256,1024]{2,1,0:T(8,128)(2,1)}, u32[]{:S(2)}, u32[]{:S(2)}) collective-permute-start(bf16[2,256,1024]{2,1,0:T(8,128)(2,1)} %get-tuple-element.115.rest_0_), channel_id=1, source_target_pairs={{0,2},{1,3},{2,0},{3,1},{4,6},{5,7},{6,4},{7,5}} | collective-permute-start | bytes 3145736 | tf_op jit(solution)/shard_map/ppermute | solution.py:521
  261.4 21.9 %collective-permute-start.4 = (bf16[704,512]{1,0:T(8,128)(2,1)}, bf16[704,512]{1,0:T(8,128)(2,1)}, u32[]{:S(2)}, u32[]{:S(2)}) collective-permute-start(bf16[704,512]{1,0:T(8,128)(2,1)} %get-tuple-element.120), channel_id=1, source_target_pairs={{0,2},{1,3},{2,0},{3,1},{4,6},{5,7},{6,4},{7,5}} | collective-permute-start | bytes 2162696 | tf_op jit(solution)/shard_map/ppermute | solution.py:521
  262.8 34.7 %collective-permute-start.3 = (bf16[704,512]{1,0:T(8,128)(2,1)}, bf16[704,512]{1,0:T(8,128)(2,1)}, u32[]{:S(2)}, u32[]{:S(2)}) collective-permute-start(bf16[704,512]{1,0:T(8,128)(2,1)} %get-tuple-element.119), channel_id=1, source_target_pairs={{0,2},{1,3},{2,0},{3,1},{4,6},{5,7},{6,4},{7,5}} | collective-permute-start | bytes 2162696 | tf_op jit(solution)/shard_map/ppermute | solution.py:521
  310.6 47.4 %copy-start = (bf16[256,2816]{1,0:T(8,128)(2,1)}, bf16[256,2816]{1,0:T(8,128)(2,1)S(1)}, u32[]{:S(2)}) copy-start(bf16[256,2816]{1,0:T(8,128)(2,1)S(1)} %get-tuple-element.136.g_ref) | copy-start | bytes 4325380
  326.1 67.0 %collective-permute-start.15 = (bf16[256,2816]{1,0:T(8,128)(2,1)}, bf16[256,2816]{1,0:T(8,128)(2,1)}, u32[]{:S(2)}, u32[]{:S(2)}) collective-permute-start(bf16[256,2816]{1,0:T(8,128)(2,1)} %get-tuple-element.143), channel_id=1, source_target_pairs={{0,2},{1,3},{2,0},{3,1},{4,6},{5,7},{6,4},{7,5}} | collective-permute-start | bytes 4325384 | tf_op jit(solution)/shard_map/ppermute | solution.py:564
  326.8 66.4 %collective-permute-start.16 = (bf16[256,2816]{1,0:T(8,128)(2,1)}, bf16[256,2816]{1,0:T(8,128)(2,1)}, u32[]{:S(2)}, u32[]{:S(2)}) collective-permute-start(bf16[256,2816]{1,0:T(8,128)(2,1)} %get-tuple-element.143), channel_id=1, source_target_pairs={{0,1},{1,0},{2,3},{3,2},{4,5},{5,4},{6,7},{7,6}} | collective-permute-start | bytes 4325384 | tf_op jit(solution)/shard_map/ppermute | solution.py:565
  334.9 66.4 %collective-permute-start.13 = (bf16[256,2816]{1,0:T(8,128)(2,1)}, bf16[256,2816]{1,0:T(8,128)(2,1)}, u32[]{:S(2)}, u32[]{:S(2)}) collective-permute-start(bf16[256,2816]{1,0:T(8,128)(2,1)} %get-tuple-element.142), channel_id=1, source_target_pairs={{0,2},{1,3},{2,0},{3,1},{4,6},{5,7},{6,4},{7,5}} | collective-permute-start | bytes 4325384 | tf_op jit(solution)/shard_map/ppermute | solution.py:564
  336.3 66.4 %collective-permute-start.14 = (bf16[256,2816]{1,0:T(8,128)(2,1)}, bf16[256,2816]{1,0:T(8,128)(2,1)}, u32[]{:S(2)}, u32[]{:S(2)}) collective-permute-start(bf16[256,2816]{1,0:T(8,128)(2,1)} %get-tuple-element.142), channel_id=1, source_target_pairs={{0,1},{1,0},{2,3},{3,2},{4,5},{5,4},{6,7},{7,6}} | collective-permute-start | bytes 4325384 | tf_op jit(solution)/shard_map/ppermute | solution.py:565
  357.2 65.5 %collective-permute-start.11 = (bf16[256,2816]{1,0:T(8,128)(2,1)}, bf16[256,2816]{1,0:T(8,128)(2,1)}, u32[]{:S(2)}, u32[]{:S(2)}) collective-permute-start(bf16[256,2816]{1,0:T(8,128)(2,1)} %get-tuple-element.140), channel_id=1, source_target_pairs={{0,2},{1,3},{2,0},{3,1},{4,6},{5,7},{6,4},{7,5}} | collective-permute-start | bytes 4325384 | tf_op jit(solution)/shard_map/ppermute | solution.py:564
  393.1 29.6 %collective-permute-start.12 = (bf16[256,2816]{1,0:T(8,128)(2,1)S(1)}, bf16[256,2816]{1,0:T(8,128)(2,1)S(1)}, u32[]{:S(2)}, u32[]{:S(2)}) collective-permute-start(bf16[256,2816]{1,0:T(8,128)(2,1)S(1)} %copy-done.12), channel_id=1, source_target_pairs={{0,1},{1,0},{2,3},{3,2},{4,5},{5,4},{6,7},{7,6}} | collective-permute-start | bytes 4325384 | tf_op jit(solution)/shard_map/ppermute | solution.py:565
  393.2 6.9 %collective-permute-start.17 = (bf16[256,2816]{1,0:T(8,128)(2,1)}, bf16[256,2816]{1,0:T(8,128)(2,1)S(1)}, u32[]{:S(2)}, u32[]{:S(2)}) collective-permute-start(bf16[256,2816]{1,0:T(8,128)(2,1)} %collective-permute-done.15), channel_id=1, source_target_pairs={{0,1},{1,0},{2,3},{3,2},{4,5},{5,4},{6,7},{7,6}} | collective-permute-start | bytes 4325384 | tf_op jit(solution)/shard_map/ppermute | solution.py:578
  400.1 29.1 %collective-permute-start.10 = (bf16[256,2816]{1,0:T(8,128)(2,1)S(1)}, bf16[256,2816]{1,0:T(8,128)(2,1)S(1)}, u32[]{:S(2)}, u32[]{:S(2)}) collective-permute-start(bf16[256,2816]{1,0:T(8,128)(2,1)S(1)} %copy-done.11), channel_id=1, source_target_pairs={{0,1},{1,0},{2,3},{3,2},{4,5},{5,4},{6,7},{7,6}} | collective-permute-start | bytes 4325384 | tf_op jit(solution)/shard_map/ppermute | solution.py:565
  401.3 52.1 %collective-permute-start.9 = (bf16[256,2816]{1,0:T(8,128)(2,1)S(1)}, bf16[256,2816]{1,0:T(8,128)(2,1)S(1)}, u32[]{:S(2)}, u32[]{:S(2)}) collective-permute-start(bf16[256,2816]{1,0:T(8,128)(2,1)S(1)} %copy-done.11), channel_id=1, source_target_pairs={{0,2},{1,3},{2,0},{3,1},{4,6},{5,7},{6,4},{7,5}} | collective-permute-start | bytes 4325384 | tf_op jit(solution)/shard_map/ppermute | solution.py:564
  402.7 5.2 collective-permute-start.18
  407.9 75.6 %collective-permute-start.7 = (bf16[704,1024]{1,0:T(8,128)(2,1)S(1)}, bf16[704,1024]{1,0:T(8,128)(2,1)S(1)}, u32[]{:S(2)}, u32[]{:S(2)}) collective-permute-start(bf16[704,1024]{1,0:T(8,128)(2,1)S(1)} %copy-done.10), channel_id=1, source_target_pairs={{0,2},{1,3},{2,0},{3,1},{4,6},{5,7},{6,4},{7,5}} | collective-permute-start | bytes 4325384 | tf_op jit(solution)/shard_map/ppermute | solution.py:564
  422.7 60.8 %collective-permute-start.8 = (bf16[704,1024]{1,0:T(8,128)(2,1)S(1)}, bf16[704,1024]{1,0:T(8,128)(2,1)S(1)}, u32[]{:S(2)}, u32[]{:S(2)}) collective-permute-start(bf16[704,1024]{1,0:T(8,128)(2,1)S(1)} %copy-done.10), channel_id=1, source_target_pairs={{0,1},{1,0},{2,3},{3,2},{4,5},{5,4},{6,7},{7,6}} | collective-permute-start | bytes 4325384 | tf_op jit(solution)/shard_map/ppermute | solution.py:565
  422.7 5.3 %collective-permute-start.19 = (bf16[256,2816]{1,0:T(8,128)(2,1)}, bf16[256,2816]{1,0:T(8,128)(2,1)S(1)}, u32[]{:S(2)}, u32[]{:S(2)}) collective-permute-start(bf16[256,2816]{1,0:T(8,128)(2,1)} %collective-permute-done.11), channel_id=1, source_target_pairs={{0,1},{1,0},{2,3},{3,2},{4,5},{5,4},{6,7},{7,6}} | collective-permute-start | bytes 4325384 | tf_op jit(solution)/shard_map/ppermute | solution.py:578
  453.5 3.2 collective-permute-start.20
  483.5 3.4 collective-permute-start.21
  483.5 34.3 %collective-permute-start.5 = (bf16[704,1024]{1,0:T(8,128)(2,1)}, bf16[704,1024]{1,0:T(8,128)(2,1)}, u32[]{:S(2)}, u32[]{:S(2)}) collective-permute-start(bf16[704,1024]{1,0:T(8,128)(2,1)} %get-tuple-element.134), channel_id=1, source_target_pairs={{0,2},{1,3},{2,0},{3,1},{4,6},{5,7},{6,4},{7,5}} | collective-permute-start | bytes 4325384 | tf_op jit(solution)/shard_map/ppermute | solution.py:564
  484.2 33.7 %collective-permute-start.6 = (bf16[704,1024]{1,0:T(8,128)(2,1)}, bf16[704,1024]{1,0:T(8,128)(2,1)}, u32[]{:S(2)}, u32[]{:S(2)}) collective-permute-start(bf16[704,1024]{1,0:T(8,128)(2,1)} %get-tuple-element.134), channel_id=1, source_target_pairs={{0,1},{1,0},{2,3},{3,2},{4,5},{5,4},{6,7},{7,6}} | collective-permute-start | bytes 4325384 | tf_op jit(solution)/shard_map/ppermute | solution.py:565
  517.9 5.1 collective-permute-start.22
  (16 other events, 138.7 us)

commit v2 on v1

--- a/solution.py
+++ b/solution.py
@@ -268,16 +268,16 @@
         def _():
             pl.loop(CHUNKS - late, CHUNKS)(meet)
 
-            @pl.loop(CHUNKS - lag, inside)
-            def _(k):
-                over(k).wait()
-                finish(k, k)
-
             @pl.loop(inside, CHUNKS)
             def _(k):
                 columns = pl.ds(pl.multiple_of((k - inside) * CHUNK, CHUNK), CHUNK)
                 for which in range(2):
                     far_ref[which, :, columns], near_ref[which, :, columns] = far[k, which], near[k, which]
+
+            @pl.loop(CHUNKS - lag, inside)
+            def _(k):
+                over(k).wait()
+                finish(k, k)
 
     column = pl.BlockSpec((None, D, CHUNK), lambda j: (layer, 0, j))
     block = pl.BlockSpec((T, CHUNK), lambda j: (0, j))
@@ -391,7 +391,7 @@
 
 def clip_and_first(ident, squares, g, m, v, w):
     rows, columns = g.shape
-    tile = 64
+    tile = 16
 
     def kernel(squares_ref, g_ref, m_ref, v_ref, w_ref, factor_ref, out_ref, held_g, held_m, held_v, held_w, mine, theirs, load, send_sem, recv_sem):
         chip, core, sib, opposite = peers()
@@ -460,9 +460,12 @@
 
     def kernel(me_ref, factor_ref, g_ref, m_ref, v_ref, w_ref, *rest):
         out_ref, full_ref = rest[n_full:]
-        new = updated(factor_ref[:1, :1], g_ref[...], m_ref[...], v_ref[...], w_ref[...])
-        out_ref[...] = new
-        full_ref[...] = new
+        factor = factor_ref[:1, :1]
+
+        @pl.loop(0, tile // 16)
+        def _(t):
+            at = pl.ds(pl.multiple_of(t * 16, 16), 16)
+            out_ref[at] = full_ref[at] = updated(factor, g_ref[at], m_ref[at], v_ref[at], w_ref[at])
 
     mine = pl.BlockSpec((tile, columns), lambda i, _: (i, 0))
     state = pl.BlockSpec((None, tile, columns), lambda i, _: (layer, i, 0))
@@ -551,11 +554,13 @@
             return grads["b" if layer else "e"][which]
 
         each = {(which, layer): of(which, layer) for which in range(3) for layer in range(2)}
+        late = each.pop((2, 0))
         squares, each = lax.optimization_barrier((sum(squared), each))
+        each[2, 0] = late
 
         ms, vs = (m_gate, m_up, m_down), (v_gate, v_up, v_down)
         full, sent = [None] * 3, []
-        for (which, layer), g in each.items():
+        for (which, layer), g in sorted(each.items(), key=lambda one: one[0]):
             name = f"{which}{layer}"
             if not sent:
                 factor, mine = clip_and_first(4, squares, g, ms[which], vs[which], weights[which])
@@ -574,11 +579,17 @@
         for k, (which, layer, over, beside) in enumerate(sent):
             if 1 <= k <= 3:
                 full, new_m[k - 1], new_v[k - 1] = lax.optimization_barrier((full, new_m[k - 1], new_v[k - 1]))
-            over, beside, full = lax.optimization_barrier((over, beside, full))
+
+            def put(piece, who):
+                full[which] = lax.dynamic_update_slice(full[which], piece[None], (layer, who * piece.shape[0], 0))
+
+            if k == 0:
+                put(first, me)
+            put(beside, me ^ 1)
+            over, full = lax.optimization_barrier((over, full))
             corner = lax.ppermute(over, "dp", sibling)
-            own = ((first, me),) if k == 0 else ()
-            for piece, who in (*own, (beside, me ^ 1), (over, me ^ 2), (corner, me ^ 3)):
-                full[which] = lax.dynamic_update_slice(full[which], piece[None], (layer, who * piece.shape[0], 0))
+            put(over, me ^ 2)
+            put(corner, me ^ 3)
         return (*full, *new_m, *new_v)
 
     batch, replicated, rows = P(("rep", "dp"), None, None), P(None, None, None), P(None, "dp", None)

time: 533 us -> 528 us (level); the launches traced: 524 us -> 527 us
  local copies, waits for them, and re-layouts: 39.8 us -> 46.3 us
    dynamic_update_slice x19, local copies, waits for them, and re-layouts: 33.7 us -> 40.8 us  [put(): lax.dynamic_update_slice(full[which], piece[None], (layer, who * piece.sh...]
  transfers between devices with their start and end apart: 23 -> 23, of which waited for: 9 -> 9; matrix products, arithmetic and copies ran while one was open for 15% -> 17% of each run, Pallas kernels for 32% -> 31%
where the time goes in v2:
time: 528 us; the launch traced here: 527 us
  Pallas kernels  298 us (56%)
  waiting for transfers between devices  118 us (22%)
  other arithmetic  47.5 us (9%)
  local copies, waits for them, and re-layouts  46.3 us (9%)
  starting transfers between devices  11.6 us (2%)
  between operations  5.37 us (1%)
    pallas_call x2, Pallas kernels, hidden(): pl.pallas_call(kernel, grid=(CHUNKS,), in_specs=[whole(normed.shape), who...  136 us
    ppermute x6, waiting for transfers between devices, step(): over = lax.ppermute(mine, 'dp', across)  89.7 us
    pallas_call x1, Pallas kernels, forward_first(): pl.pallas_call(kernel, grid=(CHUNKS,), in_specs=[whole((T, D)), pl.BlockS...  49.5 us
    dynamic_update_slice x19, local copies, waits for them, and re-layouts, put(): lax.dynamic_update_slice(full[which], piece[None], (layer, who * piece.sh...  40.8 us
    pallas_call x2, Pallas kernels, down_grad(): pl.pallas_call(kernel, grid=(DP,), in_specs=[pl.BlockSpec((rows_w, T), la...  37.7 us
    pallas_call x5, Pallas kernels, new_weight(): pl.pallas_call(kernel, grid_spec=pltpu.PrefetchScalarGridSpec(num_scalar_...  34 us
    pallas_call x1, Pallas kernels, into_states(): pl.pallas_call(kernel, grid=(T // tile,), in_specs=[long, long, weight, w...  33.8 us
    ppermute x5, waiting for transfers between devices, cross(): return lax.ppermute(far, 'dp', across)  25.2 us
  transfers between devices with their start and end apart: 23, of which 9 were waited for; matrix products, arithmetic and copies ran while one was open for 17% of the time, Pallas kernels for 31%

profile of v2, /device:TPU:0, one launch (start us, length us, event | category | flops | bytes accessed | tf_op | source)
XLA Modules:
  0.0 527.3 jit_solution(16217493983442077583)
XLA Ops:
  0.6 49.5 %shard_map.178 = (f32[2048,2816]{1,0:T(8,128)}, f32[2048,2816]{1,0:T(8,128)}, bf16[1024,2048]{1,0:T(8,128)(2,1)}, bf16[2048,1024]{1,0:T(8,128)(2,1)}, bf16[2048,1024]{1,0:T(8,128)(2,1)}) custom-call(bf16[2048,1024]{1,0:T(8,128)(2,1)} %bitcast.71, bf16[2,1024,2816]{2,1,0:T(8,128)(2,1)} %w_ref.11, bf16[2,1024,2816]{2,1,0:T(8,128)(2,1)} %w_ref.10, ...), custom_call_target="tpu_custom_call" | custom-call | flops 35433480192 | bytes 90000000 | tf_op jit(solution)/shard_map/pallas_call | solution.py:102
  50.1 78.0 %shard_map.179 = (bf16[2,256,2048]{2,1,0:T(8,128)(2,1)}, bf16[2,256,768]{2,1,0:T(8,128)(2,1)}, f32[2,256,768]{2,1,0:T(8,128)}, bf16[2816,2048]{1,0:T(8,128)(2,1)...) custom-call(bf16[2048,1024]{1,0:T(8,128)(2,1)} %get-tuple-element.94.n_ref, bf16[2048,1024]{1,0:T(8,128)(2,1)} %bitcast.72, ...), custom_call_target="tpu_custom_call" | custom-call | flops 59055800320 | bytes 60000000 | tf_op jit(solution)/shard_map/pallas_call | solution.py:306
  129.6 18.8 %shard_map.180 = (bf16[704,1024]{1,0:T(8,128)(2,1)}, f32[704,1024]{1,0:T(8,128)}) custom-call(bf16[2816,2048]{1,0:T(8,128)(2,1)} %get-tuple-element.96.act_ref, bf16[2048,1024]{1,0:T(8,128)(2,1)} %bitcast.73, bf16[2,256,768]{2,1,0:T(8,128)(2,1)} %get-tuple-element.97.rest_0_), custom_call_target="tpu_custom_call" | custom-call | flops 11811160064 | bytes 20000000 | tf_op jit(solution)/shard_map/pallas_call | solution.py:371
  149.0 33.8 %shard_map.181.by_ref = bf16[2048,1024]{1,0:T(8,128)(2,1)} custom-call(bf16[2048,2816]{1,0:T(8,128)(2,1)} %get-tuple-element.100.dg_ref, bf16[2048,2816]{1,0:T(8,128)(2,1)} %get-tuple-element.101.du_ref, bf16[2,1024,2816]{2,1,0:T(8,128)(2,1)} %w_ref.11, bf16[2,1024,2816]{2,1,0:T(8,128)(2,1)} %w_ref.10, bf16[2048,1024]{1,0:T(8,128)(2,1)} %get-tuple-element.102.h_ref, ...), custom_call_target="tpu_custom_call" | custom-call | flops 23622320128 | bytes 50000000 | tf_op jit(solution)/shard_map/pallas_call | solution.py:503
  182.8 57.9 %shard_map.182 = (bf16[2,256,1792]{2,1,0:T(8,128)(2,1)}, bf16[2,256,1024]{2,1,0:T(8,128)(2,1)}, f32[2,256,1024]{2,1,0:T(8,128)}, bf16[2816,2048]{1,0:T(8,128)(2,1)}) custom-call(bf16[1024,2048]{1,0:T(8,128)(2,1)} %get-tuple-element.99.n_ref, bf16[2048,1024]{1,0:T(8,128)(2,1)} %shard_map.181.by_ref, bf16[2,2816,1024]{2,1,0:T(8,128)(2,1)} %w_ref.8, ...), custom_call_target="tpu_custom_call" | custom-call | flops 35433480192 | bytes 60000000 | tf_op jit(solution)/shard_map/pallas_call | solution.py:306
  241.3 18.9 %shard_map.183 = (bf16[704,512]{1,0:T(8,128)(2,1)}, bf16[704,512]{1,0:T(8,128)(2,1)}, f32[704,1024]{1,0:T(8,128)}) custom-call(bf16[2816,2048]{1,0:T(8,128)(2,1)} %get-tuple-element.107.act_ref, bf16[2048,1024]{1,0:T(8,128)(2,1)} %shard_map.181.by_ref, bf16[2,256,1024]{2,1,0:T(8,128)(2,1)} %get-tuple-element.108.rest_0_), custom_call_target="tpu_custom_call" | custom-call | flops 11811160064 | bytes 20000000 | tf_op jit(solution)/shard_map/pallas_call | solution.py:371
  262.2 3.3 fusion.10
  268.7 13.8 %collective-permute-done.4 = bf16[704,512]{1,0:T(8,128)(2,1)} collective-permute-done((bf16[704,512]{1,0:T(8,128)(2,1)}, bf16[704,512]{1,0:T(8,128)(2,1)}, u32[]{:S(2)}, u32[]{:S(2)}) %collective-permute-start.4) | collective-permute-done | bytes 720928 | tf_op jit(solution)/shard_map/ppermute | solution.py:524
  285.5 11.3 %collective-permute-done.3 = bf16[704,512]{1,0:T(8,128)(2,1)} collective-permute-done((bf16[704,512]{1,0:T(8,128)(2,1)}, bf16[704,512]{1,0:T(8,128)(2,1)}, u32[]{:S(2)}, u32[]{:S(2)}) %collective-permute-start.3) | collective-permute-done | bytes 720928 | tf_op jit(solution)/shard_map/ppermute | solution.py:524
  310.2 3.8 multiply_reduce_fusion.2
  317.1 7.6 %shard_map.184 = (f32[8,128]{1,0:T(8,128)}, bf16[256,2816]{1,0:T(8,128)(2,1)}) custom-call(f32[1]{0:T(128)} %bitcast.7.squares_ref, bf16[256,2816]{1,0:T(8,128)(2,1)} %get-tuple-element.122.g_ref, f32[2,256,2816]{2,1,0:T(8,128)} %m_ref.11, f32[2,256,2816]{2,1,0:T(8,128)} %v_ref.11, bf16[2,1024,2816]{2,1,0:T(8,128)(2,1)} %w_ref.11), custom_call_target="tpu_custom_call" | custom-call | flops 1181116032 | bytes 10000000 | tf_op jit(solution)/shard_map/pallas_call | solution.py:426
  329.3 6.7 %shard_map.189 = (bf16[256,2816]{1,0:T(8,128)(2,1)}, bf16[2,1024,2816]{2,1,0:T(8,128)(2,1)}) custom-call(s32[1]{0:T(128)} %bitcast.me_ref, f32[8,128]{1,0:T(8,128)} %get-tuple-element.123.factor_ref, bf16[256,2816]{1,0:T(8,128)(2,1)} %get-tuple-element.133.g_ref, f32[2,256,2816]{2,1,0:T(8,128)} %m_ref.11, f32[2,256,2816]{2,1,0:T(8,128)} %v_ref.11, ...), custom_call_target="tpu_custom_call" | custom-call | flops 1181116032 | bytes 10000000 | tf_op jit(solution)/shard_map/pallas_call | solution.py:473
  337.7 6.8 %shard_map.185 = (bf16[704,1024]{1,0:T(8,128)(2,1)}, bf16[2,2816,1024]{2,1,0:T(8,128)(2,1)}) custom-call(s32[1]{0:T(128)} %bitcast.me_ref, f32[8,128]{1,0:T(8,128)} %get-tuple-element.123.factor_ref, bf16[704,1024]{1,0:T(8,128)(2,1)} %get-tuple-element.202.g_ref, f32[2,704,1024]{2,1,0:T(8,128)} %m_ref.8, f32[2,704,1024]{2,1,0:T(8,128)} %v_ref.8, ...), custom_call_target="tpu_custom_call" | custom-call | flops 1181116032 | bytes 10000000 | tf_op jit(solution)/shard_map/pallas_call | solution.py:473
  344.5 6.9 %shard_map.186 = (bf16[704,1024]{1,0:T(8,128)(2,1)}, bf16[2,2816,1024]{2,1,0:T(8,128)(2,1)}) custom-call(s32[1]{0:T(128)} %bitcast.me_ref, f32[8,128]{1,0:T(8,128)} %get-tuple-element.123.factor_ref, bf16[704,1024]{1,0:T(8,128)(2,1)} %get-tuple-element.124.g_ref, f32[2,704,1024]{2,1,0:T(8,128)} %m_ref.8, ...), custom_call_target="tpu_custom_call", output_to_operand_aliasing={{1}: (6, {})} | custom-call | flops 1181116032 | bytes 10000000 | tf_op jit(solution)/shard_map/pallas_call | solution.py:473
  351.5 6.7 %shard_map.187 = (bf16[256,2816]{1,0:T(8,128)(2,1)}, bf16[2,1024,2816]{2,1,0:T(8,128)(2,1)}) custom-call(s32[1]{0:T(128)} %bitcast.me_ref, f32[8,128]{1,0:T(8,128)} %get-tuple-element.123.factor_ref, bf16[256,2816]{1,0:T(8,128)(2,1)} %get-tuple-element.129.g_ref, f32[2,256,2816]{2,1,0:T(8,128)} %m_ref.10, f32[2,256,2816]{2,1,0:T(8,128)} %v_ref.10, ...), custom_call_target="tpu_custom_call" | custom-call | flops 1181116032 | bytes 10000000 | tf_op jit(solution)/shard_map/pallas_call | solution.py:473
  358.3 6.8 %shard_map.188 = (bf16[256,2816]{1,0:T(8,128)(2,1)}, bf16[2,1024,2816]{2,1,0:T(8,128)(2,1)}) custom-call(s32[1]{0:T(128)} %bitcast.me_ref, f32[8,128]{1,0:T(8,128)} %get-tuple-element.123.factor_ref, bf16[256,2816]{1,0:T(8,128)(2,1)} %get-tuple-element.128.g_ref, f32[2,256,2816]{2,1,0:T(8,128)} %m_ref.10, ...), custom_call_target="tpu_custom_call", output_to_operand_aliasing={{1}: (6, {})} | custom-call | flops 1181116032 | bytes 10000000 | tf_op jit(solution)/shard_map/pallas_call | solution.py:473
  370.9 10.4 %fusion = (f32[2,256,2816]{2,1,0:T(8,128)}, f32[2,256,2816]{2,1,0:T(8,128)}) fusion(f32[2,256,2816]{2,1,0:T(8,128)} %v_ref.11, f32[]{:T(128)} %bitcast.14, bf16[1,256,2816]{2,1,0:T(8,128)(2,1)S(1)} %bitcast.69, bf16[1,256,2816]{2,1,0:T(8,128)(2,1)S(1)} %bitcast.70, f32[2,256,2816]{2,1,0:T(8,128)} %m_ref.11), kind=kLoop, calls=%fused_computation.3 | loop fusion | flops 14417920 | bytes 25952260 | tf_op jit(solution)/shard_map/add | solution.py:578
  390.0 3.3 collective-permute-done.9
  393.4 7.2 %fusion.1 = (f32[2,256,2816]{2,1,0:T(8,128)}, f32[2,256,2816]{2,1,0:T(8,128)}) fusion(f32[2,256,2816]{2,1,0:T(8,128)S(1)} %bitcast.61, f32[]{:T(128)} %bitcast.14, bf16[1,256,2816]{2,1,0:T(8,128)(2,1)S(1)} %bitcast.67, bf16[1,256,2816]{2,1,0:T(8,128)(2,1)S(1)} %bitcast.68, f32[2,256,2816]{2,1,0:T(8,128)S(1)} %bitcast.59), kind=kLoop, calls=%fused_computation.4 | loop fusion | flops 14417920 | bytes 25952260 | tf_op jit(solution)/shard_map/add | solution.py:578
  408.8 15.4 %collective-permute-done.8 = bf16[256,2816]{1,0:T(8,128)(2,1)} collective-permute-done((bf16[256,2816]{1,0:T(8,128)(2,1)}, bf16[256,2816]{1,0:T(8,128)(2,1)}, u32[]{:S(2)}, u32[]{:S(2)}) %collective-permute-start.8) | collective-permute-done | bytes 1441824 | tf_op jit(solution)/shard_map/ppermute | solution.py:569
  424.3 6.0 %fusion.2 = (f32[2,704,1024]{2,1,0:T(8,128)}, f32[2,704,1024]{2,1,0:T(8,128)}) fusion(f32[2,704,1024]{2,1,0:T(8,128)S(1)} %bitcast.65, f32[]{:T(128)} %bitcast.14, bf16[1,704,1024]{2,1,0:T(8,128)(2,1)S(1)} %bitcast.66, bf16[1,704,1024]{2,1,0:T(8,128)(2,1)S(1)} %get-tuple-element.201, f32[2,704,1024]{2,1,0:T(8,128)S(1)} %bitcast.63), kind=kLoop, calls=%fused_computation.5 | loop fusion | flops 14417920 | bytes 25952260 | tf_op jit(solution)/shard_map/add | solution.py:578
  436.5 17.9 %collective-permute-done.7 = bf16[256,2816]{1,0:T(8,128)(2,1)S(1)} collective-permute-done((bf16[256,2816]{1,0:T(8,128)(2,1)}, bf16[256,2816]{1,0:T(8,128)(2,1)S(1)}, u32[]{:S(2)}, u32[]{:S(2)}) %collective-permute-start.7) | collective-permute-done | bytes 1441824 | tf_op jit(solution)/shard_map/ppermute | solution.py:569
  461.2 27.4 %collective-permute-done.6 = bf16[704,1024]{1,0:T(8,128)(2,1)S(1)} collective-permute-done((bf16[704,1024]{1,0:T(8,128)(2,1)}, bf16[704,1024]{1,0:T(8,128)(2,1)S(1)}, u32[]{:S(2)}, u32[]{:S(2)}) %collective-permute-start.6) | collective-permute-done | bytes 1441824 | tf_op jit(solution)/shard_map/ppermute | solution.py:569
  497.1 25.7 %collective-permute-done.5 = bf16[704,1024]{1,0:T(8,128)(2,1)S(1)} collective-permute-done((bf16[704,1024]{1,0:T(8,128)(2,1)}, bf16[704,1024]{1,0:T(8,128)(2,1)S(1)}, u32[]{:S(2)}, u32[]{:S(2)}) %collective-permute-start.5) | collective-permute-done | bytes 1441824 | tf_op jit(solution)/shard_map/ppermute | solution.py:569
  (109 shorter events, 77.8 us)
Async XLA Ops:
  128.1 171.7 %collective-permute-start = (bf16[2,256,768]{2,1,0:T(8,128)(2,1)}, bf16[2,256,768]{2,1,0:T(8,128)(2,1)}, u32[]{:S(2)}, u32[]{:S(2)}) collective-permute-start(bf16[2,256,768]{2,1,0:T(8,128)(2,1)} %get-tuple-element.97.rest_0_), channel_id=1, source_target_pairs={{0,2},{1,3},{2,0},{3,1},{4,6},{5,7},{6,4},{7,5}} | collective-permute-start | bytes 2359304 | tf_op jit(solution)/shard_map/ppermute | solution.py:524
  148.5 160.8 %collective-permute-start.1 = (bf16[704,1024]{1,0:T(8,128)(2,1)}, bf16[704,1024]{1,0:T(8,128)(2,1)}, u32[]{:S(2)}, u32[]{:S(2)}) collective-permute-start(bf16[704,1024]{1,0:T(8,128)(2,1)} %get-tuple-element.103.rest_0_), channel_id=1, source_target_pairs={{0,2},{1,3},{2,0},{3,1},{4,6},{5,7},{6,4},{7,5}} | collective-permute-start | bytes 4325384 | tf_op jit(solution)/shard_map/ppermute | solution.py:524
  240.8 62.5 %collective-permute-start.2 = (bf16[2,256,1024]{2,1,0:T(8,128)(2,1)}, bf16[2,256,1024]{2,1,0:T(8,128)(2,1)}, u32[]{:S(2)}, u32[]{:S(2)}) collective-permute-start(bf16[2,256,1024]{2,1,0:T(8,128)(2,1)} %get-tuple-element.108.rest_0_), channel_id=1, source_target_pairs={{0,2},{1,3},{2,0},{3,1},{4,6},{5,7},{6,4},{7,5}} | collective-permute-start | bytes 3145736 | tf_op jit(solution)/shard_map/ppermute | solution.py:524
  260.1 22.4 %collective-permute-start.4 = (bf16[704,512]{1,0:T(8,128)(2,1)}, bf16[704,512]{1,0:T(8,128)(2,1)}, u32[]{:S(2)}, u32[]{:S(2)}) collective-permute-start(bf16[704,512]{1,0:T(8,128)(2,1)} %get-tuple-element.113), channel_id=1, source_target_pairs={{0,2},{1,3},{2,0},{3,1},{4,6},{5,7},{6,4},{7,5}} | collective-permute-start | bytes 2162696 | tf_op jit(solution)/shard_map/ppermute | solution.py:524
  261.7 35.1 %collective-permute-start.3 = (bf16[704,512]{1,0:T(8,128)(2,1)}, bf16[704,512]{1,0:T(8,128)(2,1)}, u32[]{:S(2)}, u32[]{:S(2)}) collective-permute-start(bf16[704,512]{1,0:T(8,128)(2,1)} %get-tuple-element.112), channel_id=1, source_target_pairs={{0,2},{1,3},{2,0},{3,1},{4,6},{5,7},{6,4},{7,5}} | collective-permute-start | bytes 2162696 | tf_op jit(solution)/shard_map/ppermute | solution.py:524
  268.7 31.0 %copy-start.10 = (f32[2,256,768]{2,1,0:T(8,128)S(1)}, f32[2,256,768]{2,1,0:T(8,128)}, u32[]{:S(2)}) copy-start(f32[2,256,768]{2,1,0:T(8,128)} %get-tuple-element.114) | copy-start | bytes 4718596
  324.7 43.2 %collective-permute-start.11 = (bf16[256,2816]{1,0:T(8,128)(2,1)}, bf16[256,2816]{1,0:T(8,128)(2,1)}, u32[]{:S(2)}, u32[]{:S(2)}) collective-permute-start(bf16[256,2816]{1,0:T(8,128)(2,1)} %get-tuple-element.135), channel_id=1, source_target_pairs={{0,1},{1,0},{2,3},{3,2},{4,5},{5,4},{6,7},{7,6}} | collective-permute-start | bytes 4325384 | tf_op jit(solution)/shard_map/ppermute | solution.py:570
  327.6 43.1 %collective-permute-start.10 = (bf16[256,2816]{1,0:T(8,128)(2,1)}, bf16[256,2816]{1,0:T(8,128)(2,1)}, u32[]{:S(2)}, u32[]{:S(2)}) collective-permute-start(bf16[256,2816]{1,0:T(8,128)(2,1)} %get-tuple-element.135), channel_id=1, source_target_pairs={{0,2},{1,3},{2,0},{3,1},{4,6},{5,7},{6,4},{7,5}} | collective-permute-start | bytes 4325384 | tf_op jit(solution)/shard_map/ppermute | solution.py:569
  336.0 49.7 %collective-permute-start.13 = (bf16[256,2816]{1,0:T(8,128)(2,1)}, bf16[256,2816]{1,0:T(8,128)(2,1)}, u32[]{:S(2)}, u32[]{:S(2)}) collective-permute-start(bf16[256,2816]{1,0:T(8,128)(2,1)} %get-tuple-element.134), channel_id=1, source_target_pairs={{0,1},{1,0},{2,3},{3,2},{4,5},{5,4},{6,7},{7,6}} | collective-permute-start | bytes 4325384 | tf_op jit(solution)/shard_map/ppermute | solution.py:570
  336.2 57.1 %collective-permute-start.9 = (bf16[256,2816]{1,0:T(8,128)(2,1)}, bf16[256,2816]{1,0:T(8,128)(2,1)}, u32[]{:S(2)}, u32[]{:S(2)}) collective-permute-start(bf16[256,2816]{1,0:T(8,128)(2,1)} %get-tuple-element.134), channel_id=1, source_target_pairs={{0,2},{1,3},{2,0},{3,1},{4,6},{5,7},{6,4},{7,5}} | collective-permute-start | bytes 4325384 | tf_op jit(solution)/shard_map/ppermute | solution.py:569
  358.2 48.1 %collective-permute-start.15 = (bf16[256,2816]{1,0:T(8,128)(2,1)}, bf16[256,2816]{1,0:T(8,128)(2,1)}, u32[]{:S(2)}, u32[]{:S(2)}) collective-permute-start(bf16[256,2816]{1,0:T(8,128)(2,1)} %get-tuple-element.132), channel_id=1, source_target_pairs={{0,1},{1,0},{2,3},{3,2},{4,5},{5,4},{6,7},{7,6}} | collective-permute-start | bytes 4325384 | tf_op jit(solution)/shard_map/ppermute | solution.py:570
  367.9 56.4 %collective-permute-start.8 = (bf16[256,2816]{1,0:T(8,128)(2,1)}, bf16[256,2816]{1,0:T(8,128)(2,1)}, u32[]{:S(2)}, u32[]{:S(2)}) collective-permute-start(bf16[256,2816]{1,0:T(8,128)(2,1)} %get-tuple-element.132), channel_id=1, source_target_pairs={{0,2},{1,3},{2,0},{3,1},{4,6},{5,7},{6,4},{7,5}} | collective-permute-start | bytes 4325384 | tf_op jit(solution)/shard_map/ppermute | solution.py:569
  370.7 13.4 %collective-permute-start.12 = (bf16[256,2816]{1,0:T(8,128)(2,1)}, bf16[256,2816]{1,0:T(8,128)(2,1)S(1)}, u32[]{:S(2)}, u32[]{:S(2)}) collective-permute-start(bf16[256,2816]{1,0:T(8,128)(2,1)} %collective-permute-done.10), channel_id=1, source_target_pairs={{0,1},{1,0},{2,3},{3,2},{4,5},{5,4},{6,7},{7,6}} | collective-permute-start | bytes 4325384 | tf_op jit(solution)/shard_map/ppermute | solution.py:590
  384.1 49.9 %collective-permute-start.17 = (bf16[256,2816]{1,0:T(8,128)(2,1)}, bf16[256,2816]{1,0:T(8,128)(2,1)}, u32[]{:S(2)}, u32[]{:S(2)}) collective-permute-start(bf16[256,2816]{1,0:T(8,128)(2,1)} %get-tuple-element.131), channel_id=1, source_target_pairs={{0,1},{1,0},{2,3},{3,2},{4,5},{5,4},{6,7},{7,6}} | collective-permute-start | bytes 4325384 | tf_op jit(solution)/shard_map/ppermute | solution.py:570
  385.7 68.7 %collective-permute-start.7 = (bf16[256,2816]{1,0:T(8,128)(2,1)}, bf16[256,2816]{1,0:T(8,128)(2,1)S(1)}, u32[]{:S(2)}, u32[]{:S(2)}) collective-permute-start(bf16[256,2816]{1,0:T(8,128)(2,1)} %get-tuple-element.131), channel_id=1, source_target_pairs={{0,2},{1,3},{2,0},{3,1},{4,6},{5,7},{6,4},{7,5}} | collective-permute-start | bytes 4325384 | tf_op jit(solution)/shard_map/ppermute | solution.py:569
  393.3 9.9 %collective-permute-start.14 = (bf16[256,2816]{1,0:T(8,128)(2,1)}, bf16[256,2816]{1,0:T(8,128)(2,1)}, u32[]{:S(2)}, u32[]{:S(2)}) collective-permute-start(bf16[256,2816]{1,0:T(8,128)(2,1)} %collective-permute-done.9), channel_id=1, source_target_pairs={{0,1},{1,0},{2,3},{3,2},{4,5},{5,4},{6,7},{7,6}} | collective-permute-start | bytes 4325384 | tf_op jit(solution)/shard_map/ppermute | solution.py:590
  403.2 51.7 %collective-permute-start.19 = (bf16[704,1024]{1,0:T(8,128)(2,1)}, bf16[704,1024]{1,0:T(8,128)(2,1)}, u32[]{:S(2)}, u32[]{:S(2)}) collective-permute-start(bf16[704,1024]{1,0:T(8,128)(2,1)} %get-tuple-element.127), channel_id=1, source_target_pairs={{0,1},{1,0},{2,3},{3,2},{4,5},{5,4},{6,7},{7,6}} | collective-permute-start | bytes 4325384 | tf_op jit(solution)/shard_map/ppermute | solution.py:570
  424.2 8.6 %collective-permute-start.16 = (bf16[256,2816]{1,0:T(8,128)(2,1)}, bf16[256,2816]{1,0:T(8,128)(2,1)S(1)}, u32[]{:S(2)}, u32[]{:S(2)}) collective-permute-start(bf16[256,2816]{1,0:T(8,128)(2,1)} %collective-permute-done.8), channel_id=1, source_target_pairs={{0,1},{1,0},{2,3},{3,2},{4,5},{5,4},{6,7},{7,6}} | collective-permute-start | bytes 4325384 | tf_op jit(solution)/shard_map/ppermute | solution.py:590
  454.4 4.2 collective-permute-start.18
  454.4 34.2 %collective-permute-start.6 = (bf16[704,1024]{1,0:T(8,128)(2,1)}, bf16[704,1024]{1,0:T(8,128)(2,1)S(1)}, u32[]{:S(2)}, u32[]{:S(2)}) collective-permute-start(bf16[704,1024]{1,0:T(8,128)(2,1)} %get-tuple-element.127), channel_id=1, source_target_pairs={{0,2},{1,3},{2,0},{3,1},{4,6},{5,7},{6,4},{7,5}} | collective-permute-start | bytes 4325384 | tf_op jit(solution)/shard_map/ppermute | solution.py:569
  488.6 3.4 collective-permute-start.20
  488.6 5.9 %collective-permute-start.21 = (bf16[704,1024]{1,0:T(8,128)(2,1)}, bf16[704,1024]{1,0:T(8,128)(2,1)}, u32[]{:S(2)}, u32[]{:S(2)}) collective-permute-start(bf16[704,1024]{1,0:T(8,128)(2,1)} %get-tuple-element.126), channel_id=1, source_target_pairs={{0,1},{1,0},{2,3},{3,2},{4,5},{5,4},{6,7},{7,6}} | collective-permute-start | bytes 4325384 | tf_op jit(solution)/shard_map/ppermute | solution.py:570
  489.2 33.7 %collective-permute-start.5 = (bf16[704,1024]{1,0:T(8,128)(2,1)}, bf16[704,1024]{1,0:T(8,128)(2,1)S(1)}, u32[]{:S(2)}, u32[]{:S(2)}) collective-permute-start(bf16[704,1024]{1,0:T(8,128)(2,1)} %get-tuple-element.126), channel_id=1, source_target_pairs={{0,2},{1,3},{2,0},{3,1},{4,6},{5,7},{6,4},{7,5}} | collective-permute-start | bytes 4325384 | tf_op jit(solution)/shard_map/ppermute | solution.py:569
  522.9 3.2 collective-permute-start.22
  (18 other events, 293.3 us)

commit v3 on v2

--- a/solution.py
+++ b/solution.py
@@ -359,15 +359,16 @@
         def _():
             copy(0).wait()
             far = (term.astype(F32) + got[0].astype(F32)).astype(BF16)
-            for k, far_ref in enumerate(far_refs):
-                far_ref[...] = far[:, k * D // parts : (k + 1) * D // parts]
+            for (start, stop), far_ref in zip(parts, far_refs, strict=True):
+                far_ref[...] = far[:, start:stop]
 
         @pl.when(i == CORES + 1)
         def _():
             copy(1).wait()
             near_ref[...] = term.astype(F32) + got[1].astype(F32)
 
-    shape, far_shape = (rows_w, D), (rows_w, D // parts)
+    shape = (rows_w, D)
+    far_shapes = [(rows_w, stop - start) for start, stop in parts]
     return pl.pallas_call(
         kernel,
         grid=(DP,),
@@ -376,8 +377,8 @@
             whole((T, D)),
             *(ANY,) * n_after,
         ],
-        out_specs=[*(whole(far_shape),) * parts, whole(shape)],
-        out_shape=[*(jax.ShapeDtypeStruct(far_shape, BF16),) * parts, jax.ShapeDtypeStruct(shape, F32)],
+        out_specs=[*map(whole, far_shapes), whole(shape)],
+        out_shape=[*(jax.ShapeDtypeStruct(one, BF16) for one in far_shapes), jax.ShapeDtypeStruct(shape, F32)],
         scratch_shapes=[
             pltpu.VMEM((CORES, *shape), BF16),
             pltpu.VMEM((CORES, *shape), BF16),
@@ -485,30 +486,129 @@
     )(me.reshape(1), factor, g, m, v, w, *((full,) if n_full else ()))
 
 
-def into_states(dg, du, w_gate, w_up, h, by_out, after):
-    tile = 256
+def middle(ident, act_t, dg, du, w_gate, w_up, h, by_out, after):
+    tile, rows_w, rest_columns = 256, FF // DP, D // 4
+    inner = D - rest_columns
+    steps = T // tile
     n_after = len(after)
 
-    def kernel(dg_ref, du_ref, wg_ref, wu_ref, h_ref, by_ref, *rest):
-        out_ref = rest[n_after]
-        by_a = dot_t(dg_ref[...], wg_ref[...]).astype(BF16) + dot_t(du_ref[...], wu_ref[...]).astype(BF16)
-        c, wide = by_a.astype(F32), h_ref[...].astype(F32)
-        scale = root_mean_scale(wide)
-        along = jnp.sum(c * wide, -1, keepdims=True)
-        out_ref[...] = by_ref[...] + (c * scale - wide * (scale * scale * scale * along * (1.0 / D))).astype(BF16)
-
-    long = pl.BlockSpec((tile, FF), lambda i: (i, 0))
-    short = pl.BlockSpec((tile, D), lambda i: (i, 0))
-    weight = pl.BlockSpec((None, D, FF), lambda i: (1, 0, 0), pipeline_mode=pl.Buffered(1))
+    def kernel(act_ref, by_ref, dg_ref, du_ref, wg_hbm, wu_hbm, h_ref, *rest):
+        rest = rest[n_after:]
+        out_ref, sum_ref, far_ref, near_ref, wg, wu, out, got, far, near, landed, load, send_sem, recv_sem, over_send, over_recv = rest
+        i = pl.program_id(0)
+        _, _, sib, opposite = peers()
+        barrier = pltpu.get_barrier_semaphore()
+        loads = [
+            pltpu.make_async_copy(wg_hbm.at[1], wg, load.at[0]),
+            pltpu.make_async_copy(wu_hbm.at[1], wu, load.at[1]),
+        ]
+
+        def beside(k):
+            return remote(out.at[k], got.at[k], send_sem.at[k], recv_sem.at[k], sib)
+
+        def over():
+            return remote(far, landed, over_send.at[0], over_recv.at[0], opposite)
+
+        @pl.when(i == 0)
+        def _():
+            for one in loads:
+                one.start()
+            for other in (sib, opposite):
+                pl.semaphore_signal(barrier, inc=1, device_id={"dp": other}, device_id_type=MESH)
+
+        @pl.when(i == 1)
+        def _():
+            pl.semaphore_wait(barrier, 2)
+            beside(0).start()
+
+        @pl.when(i == 2)
+        def _():
+            over().start()
+
+        @pl.when(i == 3)
+        def _():
+            beside(1).start()
+
+        @pl.when(i == DP)
+        def _():
+            for one in loads:
+                one.wait()
+
+        @pl.when(i < DP)
+        def _():
+            term = dot(act_ref[...], by_ref[...]).astype(BF16)
+
+            @pl.when(i == 0)
+            def _():
+                out[0] = term
+
+            @pl.when(i == 1)
+            def _():
+                beside(0).wait()
+                there = (term.astype(F32) + got[0].astype(F32)).astype(BF16)
+                far[...] = there[:, :inner]
+                far_ref[...] = there[:, inner:]
+
+            @pl.when(i == 2)
+            def _():
+                out[1] = term
+
+            @pl.when(i == 3)
+            def _():
+                beside(1).wait()
+                here = term.astype(F32) + got[1].astype(F32)
+                near[...] = here[:, :inner]
+                near_ref[...] = here[:, inner:]
+
+        @pl.when(i >= DP)
+        def _():
+            by_a = dot_t(dg_ref[...], wg[...]).astype(BF16) + dot_t(du_ref[...], wu[...]).astype(BF16)
+            c, wide = by_a.astype(F32), h_ref[...].astype(F32)
+            scale = root_mean_scale(wide)
+            along = jnp.sum(c * wide, -1, keepdims=True)
+            by = by_ref[pl.ds(pl.multiple_of((i - DP) * tile, tile), tile)]
+            out_ref[...] = by + (c * scale - wide * (scale * scale * scale * along * (1.0 / D))).astype(BF16)
+
+        @pl.when(i == DP + steps - 1)
+        def _():
+            over().wait()
+            sum_ref[...] = (near[...] + landed[...].astype(F32)).astype(BF16)
+
+    def row(i):
+        return jnp.maximum(i - DP, 0)
+
+    def source(i):
+        k = jnp.minimum(i, DP - 1)
+        return block_of(lax.rem(k, CORES) * CORES + k // CORES)
+
+    long = pl.BlockSpec((tile, FF), lambda i: (row(i), 0))
+    short = pl.BlockSpec((tile, D), lambda i: (row(i), 0))
+    most, few = (rows_w, inner), (rows_w, rest_columns)
     return pl.pallas_call(
         kernel,
-        grid=(T // tile,),
-        in_specs=[long, long, weight, weight, short, short, *(ANY,) * n_after],
-        out_specs=short,
-        out_shape=jax.ShapeDtypeStruct((T, D), BF16),
-        compiler_params=params(),
-        cost_estimate=cost(2, 50e6),
-    )(dg, du, w_gate, w_up, h, by_out, *after)
+        grid=(DP + steps,),
+        in_specs=[pl.BlockSpec((rows_w, T), lambda i: (source(i), 0)), whole((T, D)), long, long, ANY, ANY, short, *(ANY,) * n_after],
+        out_specs=[short, whole(most), whole(few), whole(few)],
+        out_shape=[
+            jax.ShapeDtypeStruct((T, D), BF16),
+            jax.ShapeDtypeStruct(most, BF16),
+            jax.ShapeDtypeStruct(few, BF16),
+            jax.ShapeDtypeStruct(few, F32),
+        ],
+        scratch_shapes=[
+            pltpu.VMEM((D, FF), BF16),
+            pltpu.VMEM((D, FF), BF16),
+            pltpu.VMEM((CORES, rows_w, D), BF16),
+            pltpu.VMEM((CORES, rows_w, D), BF16),
+            pltpu.VMEM(most, BF16),
+            pltpu.VMEM(most, F32),
+            pltpu.VMEM(most, BF16),
+            *(pltpu.SemaphoreType.DMA((CORES,)),) * 3,
+            *(pltpu.SemaphoreType.DMA((1,)),) * 2,
+        ],
+        compiler_params=remote_params(ident),
+        cost_estimate=cost(3, 70e6),
+    )(act_t, by_out, dg, du, w_gate, w_up, h, *after)
 
 
 def solution(mesh):
@@ -527,26 +627,25 @@
         units = {}
         sum_b, far, near, act2, dg2, du2 = hidden(0, 1, 8, 6, False, a2, dy, weights, None, ())
         units["b"] = near, cross(far)
-        far, near = down_grad(1, act2, dy, 1, (far,))
+        dh1, sum_d, far, near = middle(1, act2, dg2, du2, w_gate, w_up, h1, dy, (far,))
         units["d"] = near, cross(far)
-        dh1 = into_states(dg2, du2, w_gate, w_up, h1, dy, (far,))
         sum_e, far, near, act1 = hidden(2, 0, 7, 7, True, a1, dh1, weights, (g1, u1), ())
         units["e"] = near, cross(far)
-        *fars, near = down_grad(3, act1, dh1, 2, (far,))
-        for k, far in enumerate(fars):
-            units[f"f{k}"] = near[:, k * D // 2 : (k + 1) * D // 2], cross(far)
+        parts = ((0, 3 * D // 4), (3 * D // 4, D))
+        *fars, near = down_grad(3, act1, dh1, parts, (far,))
+        for k, (far, (start, stop)) in enumerate(zip(fars, parts, strict=True)):
+            units[f"f{k}"] = near[:, start:stop], cross(far)
 
         nears = {name: near for name, (near, _) in units.items()}
-        nears, sum_b, sum_e, _ = lax.optimization_barrier((nears, sum_b, sum_e, fars))
+        nears, inners, _ = lax.optimization_barrier((nears, {"b": sum_b, "d": sum_d, "e": sum_e}, fars))
         units = {name: (nears[name], landed) for name, (_, landed) in units.items()}
         grads, squared = {}, []
         for name, (near, landed) in units.items():
             grads[name] = (near + landed.astype(F32)).astype(BF16)
             squared.append(jnp.sum(grads[name].astype(F32) ** 2))
-            if name in "be":
-                inner = sum_b if name == "b" else sum_e
-                squared.append(jnp.sum(inner.astype(F32) ** 2))
-                grads[name] = jnp.concatenate([inner, grads[name]], 2)
+            if name in inners:
+                squared.append(jnp.sum(inners[name].astype(F32) ** 2))
+                grads[name] = jnp.concatenate([inners[name], grads[name]], -1)
 
         def of(which, layer):
             if which == 2:
@@ -566,10 +665,10 @@
                 factor, mine = clip_and_first(4, squares, g, ms[which], vs[which], weights[which])
             else:
                 mine, full[which] = new_weight(layer, me, factor, g, ms[which], vs[which], weights[which], full[which])
+            first = mine if which + layer == 0 else first
             over = lax.ppermute(mine, "dp", across)
             beside = lax.ppermute(mine, "dp", sibling)
             sent.append((which, layer, over, beside))
-            first = mine if which + layer == 0 else first
         factor, _ = lax.optimization_barrier((factor[0, 0], mine))
         new_m, new_v = [], []
         for which in range(3):

time: 528 us -> 531 us (level)
    pallas_call x2 -> x1, Pallas kernels: 37.7 us -> 18.9 us  [down_grad(): pl.pallas_call(kernel, grid=(DP,), in_specs=[pl.BlockSpec((rows_w, T), la...]
    pallas_call x1, Pallas kernels: 33.8 us -> 48 us  [middle(): pl.pallas_call(kernel, grid=(DP + steps,), in_specs=[pl.BlockSpec((rows_w...]
    ppermute x5, waiting for transfers between devices: 25.2 us -> 32.5 us  [cross(): return lax.ppermute(far, 'dp', across)]
  transfers between devices with their start and end apart: 23 -> 23, of which waited for: 9 -> 8; matrix products, arithmetic and copies ran while one was open for 17% -> 17% of each run, Pallas kernels for 31% -> 30%
where the time goes in v3:
time: 531 us; the launch traced here: 530 us
  Pallas kernels  293 us (55%)
  waiting for transfers between devices  120 us (23%)
  other arithmetic  50.1 us (9%)
  local copies, waits for them, and re-layouts  46.3 us (9%)
  starting transfers between devices  14.7 us (3%)
  between operations  6.11 us (1%)
    pallas_call x2, Pallas kernels, hidden(): pl.pallas_call(kernel, grid=(CHUNKS,), in_specs=[whole(normed.shape), who...  135 us
    ppermute x6, waiting for transfers between devices, step(): over = lax.ppermute(mine, 'dp', across)  85.6 us
    pallas_call x1, Pallas kernels, forward_first(): pl.pallas_call(kernel, grid=(CHUNKS,), in_specs=[whole((T, D)), pl.BlockS...  49.4 us
    pallas_call x1, Pallas kernels, middle(): pl.pallas_call(kernel, grid=(DP + steps,), in_specs=[pl.BlockSpec((rows_w...  48 us
    dynamic_update_slice x19, local copies, waits for them, and re-layouts, put(): lax.dynamic_update_slice(full[which], piece[None], (layer, who * piece.sh...  41 us
    pallas_call x5, Pallas kernels, new_weight(): pl.pallas_call(kernel, grid_spec=pltpu.PrefetchScalarGridSpec(num_scalar_...  34.1 us
    ppermute x5, waiting for transfers between devices, cross(): return lax.ppermute(far, 'dp', across)  32.5 us
    add x3, other arithmetic, step(): new_v.append(0.95 * vs[which] + 0.05 * g * g)  23.8 us
  transfers between devices with their start and end apart: 23, of which 8 were waited for; matrix products, arithmetic and copies ran while one was open for 17% of the time, Pallas kernels for 30%

profile of v3, /device:TPU:0, one launch (start us, length us, event | category | flops | bytes accessed | tf_op | source)
XLA Modules:
  0.0 530.2 jit_solution(13209994756537459)
XLA Ops:
  0.6 49.4 %shard_map.178 = (f32[2048,2816]{1,0:T(8,128)}, f32[2048,2816]{1,0:T(8,128)}, bf16[1024,2048]{1,0:T(8,128)(2,1)}, bf16[2048,1024]{1,0:T(8,128)(2,1)}, bf16[2048,1024]{1,0:T(8,128)(2,1)}) custom-call(bf16[2048,1024]{1,0:T(8,128)(2,1)} %bitcast.71, bf16[2,1024,2816]{2,1,0:T(8,128)(2,1)} %w_ref.11, bf16[2,1024,2816]{2,1,0:T(8,128)(2,1)} %w_ref.10, ...), custom_call_target="tpu_custom_call" | custom-call | flops 35433480192 | bytes 90000000 | tf_op jit(solution)/shard_map/pallas_call | solution.py:102
  50.1 78.1 %shard_map.179 = (bf16[2,256,2048]{2,1,0:T(8,128)(2,1)}, bf16[2,256,768]{2,1,0:T(8,128)(2,1)}, f32[2,256,768]{2,1,0:T(8,128)}, bf16[2816,2048]{1,0:T(8,128)(2,1)...) custom-call(bf16[2048,1024]{1,0:T(8,128)(2,1)} %get-tuple-element.97.n_ref, bf16[2048,1024]{1,0:T(8,128)(2,1)} %bitcast.72, ...), custom_call_target="tpu_custom_call" | custom-call | flops 59055800320 | bytes 60000000 | tf_op jit(solution)/shard_map/pallas_call | solution.py:306
  129.7 48.0 %shard_map.180 = (bf16[2048,1024]{1,0:T(8,128)(2,1)}, bf16[704,768]{1,0:T(8,128)(2,1)}, bf16[704,256]{1,0:T(8,128)(2,1)}, f32[704,256]{1,0:T(8,128)}) custom-call(bf16[2816,2048]{1,0:T(8,128)(2,1)} %get-tuple-element.99.act_ref, bf16[2048,1024]{1,0:T(8,128)(2,1)} %bitcast.73, bf16[2048,2816]{1,0:T(8,128)(2,1)} %get-tuple-element.100.dg_ref, ...), custom_call_target="tpu_custom_call" | custom-call | flops 35433480192 | bytes 70000000 | tf_op jit(solution)/shard_map/pallas_call | solution.py:587
  177.7 56.9 %shard_map.181 = (bf16[2,256,1792]{2,1,0:T(8,128)(2,1)}, bf16[2,256,1024]{2,1,0:T(8,128)(2,1)}, f32[2,256,1024]{2,1,0:T(8,128)}, bf16[2816,2048]{1,0:T(8,128)(2,1)}) custom-call(bf16[1024,2048]{1,0:T(8,128)(2,1)} %get-tuple-element.105.n_ref, bf16[2048,1024]{1,0:T(8,128)(2,1)} %get-tuple-element.106.by_ref, bf16[2,2816,1024]{2,1,0:T(8,128)(2,1)} %w_ref.8, ...), custom_call_target="tpu_custom_call" | custom-call | flops 35433480192 | bytes 60000000 | tf_op jit(solution)/shard_map/pallas_call | solution.py:306
  236.2 18.9 %shard_map.182 = (bf16[704,768]{1,0:T(8,128)(2,1)}, bf16[704,256]{1,0:T(8,128)(2,1)}, f32[704,1024]{1,0:T(8,128)}) custom-call(bf16[2816,2048]{1,0:T(8,128)(2,1)} %get-tuple-element.110.act_ref, bf16[2048,1024]{1,0:T(8,128)(2,1)} %get-tuple-element.106.by_ref, bf16[2,256,1024]{2,1,0:T(8,128)(2,1)} %get-tuple-element.111.rest_0_), custom_call_target="tpu_custom_call" | custom-call | flops 11811160064 | bytes 20000000 | tf_op jit(solution)/shard_map/pallas_call | solution.py:372
  266.0 32.4 %collective-permute-done.1 = bf16[704,256]{1,0:T(8,128)(2,1)} collective-permute-done((bf16[704,256]{1,0:T(8,128)(2,1)}, bf16[704,256]{1,0:T(8,128)(2,1)}, u32[]{:S(2)}, u32[]{:S(2)}) %collective-permute-start.1) | collective-permute-done | bytes 360480 | tf_op jit(solution)/shard_map/ppermute | solution.py:624
  304.2 3.0 multiply_reduce_fusion.5
  309.8 3.0 multiply_reduce_fusion.4
  314.1 4.2 fusion.7
  318.4 3.3 multiply_reduce_fusion.2
  323.0 7.5 %shard_map.183 = (f32[8,128]{1,0:T(8,128)}, bf16[256,2816]{1,0:T(8,128)(2,1)}) custom-call(f32[1]{0:T(128)} %bitcast.7.squares_ref, bf16[256,2816]{1,0:T(8,128)(2,1)} %get-tuple-element.128.g_ref, f32[2,256,2816]{2,1,0:T(8,128)} %m_ref.11, f32[2,256,2816]{2,1,0:T(8,128)} %v_ref.11, bf16[2,1024,2816]{2,1,0:T(8,128)(2,1)} %w_ref.11), custom_call_target="tpu_custom_call" | custom-call | flops 1181116032 | bytes 10000000 | tf_op jit(solution)/shard_map/pallas_call | solution.py:427
  333.3 6.8 %shard_map.188 = (bf16[256,2816]{1,0:T(8,128)(2,1)}, bf16[2,1024,2816]{2,1,0:T(8,128)(2,1)}) custom-call(s32[1]{0:T(128)} %bitcast.me_ref, f32[8,128]{1,0:T(8,128)} %get-tuple-element.129.factor_ref, bf16[256,2816]{1,0:T(8,128)(2,1)} %get-tuple-element.139.g_ref, f32[2,256,2816]{2,1,0:T(8,128)} %m_ref.11, f32[2,256,2816]{2,1,0:T(8,128)} %v_ref.11, ...), custom_call_target="tpu_custom_call" | custom-call | flops 1181116032 | bytes 10000000 | tf_op jit(solution)/shard_map/pallas_call | solution.py:474
  343.5 6.8 %shard_map.184 = (bf16[704,1024]{1,0:T(8,128)(2,1)}, bf16[2,2816,1024]{2,1,0:T(8,128)(2,1)}) custom-call(s32[1]{0:T(128)} %bitcast.me_ref, f32[8,128]{1,0:T(8,128)} %get-tuple-element.129.factor_ref, bf16[704,1024]{1,0:T(8,128)(2,1)} %get-tuple-element.206.g_ref, f32[2,704,1024]{2,1,0:T(8,128)} %m_ref.8, f32[2,704,1024]{2,1,0:T(8,128)} %v_ref.8, ...), custom_call_target="tpu_custom_call" | custom-call | flops 1181116032 | bytes 10000000 | tf_op jit(solution)/shard_map/pallas_call | solution.py:474
  350.3 6.8 %shard_map.185 = (bf16[704,1024]{1,0:T(8,128)(2,1)}, bf16[2,2816,1024]{2,1,0:T(8,128)(2,1)}) custom-call(s32[1]{0:T(128)} %bitcast.me_ref, f32[8,128]{1,0:T(8,128)} %get-tuple-element.129.factor_ref, bf16[704,1024]{1,0:T(8,128)(2,1)} %pad_maximum_fusion.5.g_ref, f32[2,704,1024]{2,1,0:T(8,128)} %m_ref.8, ...), custom_call_target="tpu_custom_call", output_to_operand_aliasing={{1}: (6, {})} | custom-call | flops 1181116032 | bytes 10000000 | tf_op jit(solution)/shard_map/pallas_call | solution.py:474
  357.2 6.7 %shard_map.186 = (bf16[256,2816]{1,0:T(8,128)(2,1)}, bf16[2,1024,2816]{2,1,0:T(8,128)(2,1)}) custom-call(s32[1]{0:T(128)} %bitcast.me_ref, f32[8,128]{1,0:T(8,128)} %get-tuple-element.129.factor_ref, bf16[256,2816]{1,0:T(8,128)(2,1)} %get-tuple-element.135.g_ref, f32[2,256,2816]{2,1,0:T(8,128)} %m_ref.10, f32[2,256,2816]{2,1,0:T(8,128)} %v_ref.10, ...), custom_call_target="tpu_custom_call" | custom-call | flops 1181116032 | bytes 10000000 | tf_op jit(solution)/shard_map/pallas_call | solution.py:474
  364.0 6.9 %shard_map.187 = (bf16[256,2816]{1,0:T(8,128)(2,1)}, bf16[2,1024,2816]{2,1,0:T(8,128)(2,1)}) custom-call(s32[1]{0:T(128)} %bitcast.me_ref, f32[8,128]{1,0:T(8,128)} %get-tuple-element.129.factor_ref, bf16[256,2816]{1,0:T(8,128)(2,1)} %get-tuple-element.134.g_ref, f32[2,256,2816]{2,1,0:T(8,128)} %m_ref.10, ...), custom_call_target="tpu_custom_call", output_to_operand_aliasing={{1}: (6, {})} | custom-call | flops 1181116032 | bytes 10000000 | tf_op jit(solution)/shard_map/pallas_call | solution.py:474
  377.9 10.3 %fusion = (f32[2,256,2816]{2,1,0:T(8,128)}, f32[2,256,2816]{2,1,0:T(8,128)}) fusion(f32[2,256,2816]{2,1,0:T(8,128)} %v_ref.11, f32[]{:T(128)} %bitcast.14, bf16[1,256,2816]{2,1,0:T(8,128)(2,1)S(1)} %bitcast.69, bf16[1,256,2816]{2,1,0:T(8,128)(2,1)S(1)} %bitcast.70, f32[2,256,2816]{2,1,0:T(8,128)} %m_ref.11), kind=kLoop, calls=%fused_computation.3 | loop fusion | flops 14417920 | bytes 25952260 | tf_op jit(solution)/shard_map/add | solution.py:677
  388.3 2.9 bitcast_dynamic-update-slice_fusion.16
  396.4 7.2 %fusion.1 = (f32[2,256,2816]{2,1,0:T(8,128)}, f32[2,256,2816]{2,1,0:T(8,128)}) fusion(f32[2,256,2816]{2,1,0:T(8,128)S(1)} %bitcast.61, f32[]{:T(128)} %bitcast.14, bf16[1,256,2816]{2,1,0:T(8,128)(2,1)S(1)} %bitcast.67, bf16[1,256,2816]{2,1,0:T(8,128)(2,1)S(1)} %bitcast.68, f32[2,256,2816]{2,1,0:T(8,128)S(1)} %bitcast.59), kind=kLoop, calls=%fused_computation.4 | loop fusion | flops 14417920 | bytes 25952260 | tf_op jit(solution)/shard_map/add | solution.py:677
  411.9 15.3 %collective-permute-done.8 = bf16[256,2816]{1,0:T(8,128)(2,1)} collective-permute-done((bf16[256,2816]{1,0:T(8,128)(2,1)}, bf16[256,2816]{1,0:T(8,128)(2,1)}, u32[]{:S(2)}, u32[]{:S(2)}) %collective-permute-start.8) | collective-permute-done | bytes 1441824 | tf_op jit(solution)/shard_map/ppermute | solution.py:669
  427.2 6.2 %fusion.2 = (f32[2,704,1024]{2,1,0:T(8,128)}, f32[2,704,1024]{2,1,0:T(8,128)}) fusion(f32[2,704,1024]{2,1,0:T(8,128)S(1)} %bitcast.65, f32[]{:T(128)} %bitcast.14, bf16[1,704,1024]{2,1,0:T(8,128)(2,1)S(1)} %bitcast.66, bf16[1,704,1024]{2,1,0:T(8,128)(2,1)S(1)} %get-tuple-element.205, f32[2,704,1024]{2,1,0:T(8,128)S(1)} %bitcast.63), kind=kLoop, calls=%fused_computation.5 | loop fusion | flops 14417920 | bytes 25952260 | tf_op jit(solution)/shard_map/add | solution.py:677
  439.7 17.7 %collective-permute-done.7 = bf16[256,2816]{1,0:T(8,128)(2,1)S(1)} collective-permute-done((bf16[256,2816]{1,0:T(8,128)(2,1)}, bf16[256,2816]{1,0:T(8,128)(2,1)S(1)}, u32[]{:S(2)}, u32[]{:S(2)}) %collective-permute-start.7) | collective-permute-done | bytes 1441824 | tf_op jit(solution)/shard_map/ppermute | solution.py:669
  465.2 26.3 %collective-permute-done.6 = bf16[704,1024]{1,0:T(8,128)(2,1)S(1)} collective-permute-done((bf16[704,1024]{1,0:T(8,128)(2,1)}, bf16[704,1024]{1,0:T(8,128)(2,1)S(1)}, u32[]{:S(2)}, u32[]{:S(2)}) %collective-permute-start.6) | collective-permute-done | bytes 1441824 | tf_op jit(solution)/shard_map/ppermute | solution.py:669
  500.1 25.7 %collective-permute-done.5 = bf16[704,1024]{1,0:T(8,128)(2,1)S(1)} collective-permute-done((bf16[704,1024]{1,0:T(8,128)(2,1)}, bf16[704,1024]{1,0:T(8,128)(2,1)S(1)}, u32[]{:S(2)}, u32[]{:S(2)}) %collective-permute-start.5) | collective-permute-done | bytes 1441824 | tf_op jit(solution)/shard_map/ppermute | solution.py:669
  (111 shorter events, 73.6 us)
Async XLA Ops:
  128.2 176.0 %collective-permute-start = (bf16[2,256,768]{2,1,0:T(8,128)(2,1)}, bf16[2,256,768]{2,1,0:T(8,128)(2,1)}, u32[]{:S(2)}, u32[]{:S(2)}) collective-permute-start(bf16[2,256,768]{2,1,0:T(8,128)(2,1)} %get-tuple-element.103.rest_0_), channel_id=1, source_target_pairs={{0,2},{1,3},{2,0},{3,1},{4,6},{5,7},{6,4},{7,5}} | collective-permute-start | bytes 2359304 | tf_op jit(solution)/shard_map/ppermute | solution.py:624
  234.6 75.1 %collective-permute-start.2 = (bf16[2,256,1024]{2,1,0:T(8,128)(2,1)}, bf16[2,256,1024]{2,1,0:T(8,128)(2,1)}, u32[]{:S(2)}, u32[]{:S(2)}) collective-permute-start(bf16[2,256,1024]{2,1,0:T(8,128)(2,1)} %get-tuple-element.111.rest_0_), channel_id=1, source_target_pairs={{0,2},{1,3},{2,0},{3,1},{4,6},{5,7},{6,4},{7,5}} | collective-permute-start | bytes 3145736 | tf_op jit(solution)/shard_map/ppermute | solution.py:624
  255.1 46.7 %collective-permute-start.4 = (bf16[704,256]{1,0:T(8,128)(2,1)}, bf16[704,256]{1,0:T(8,128)(2,1)}, u32[]{:S(2)}, u32[]{:S(2)}) collective-permute-start(bf16[704,256]{1,0:T(8,128)(2,1)} %get-tuple-element.117), channel_id=1, source_target_pairs={{0,2},{1,3},{2,0},{3,1},{4,6},{5,7},{6,4},{7,5}} | collective-permute-start | bytes 1081352 | tf_op jit(solution)/shard_map/ppermute | solution.py:624
  255.6 62.8 %collective-permute-start.3 = (bf16[704,768]{1,0:T(8,128)(2,1)}, bf16[704,768]{1,0:T(8,128)(2,1)}, u32[]{:S(2)}, u32[]{:S(2)}) collective-permute-start(bf16[704,768]{1,0:T(8,128)(2,1)} %get-tuple-element.116), channel_id=1, source_target_pairs={{0,2},{1,3},{2,0},{3,1},{4,6},{5,7},{6,4},{7,5}} | collective-permute-start | bytes 3244040 | tf_op jit(solution)/shard_map/ppermute | solution.py:624
  257.1 41.3 %collective-permute-start.1 = (bf16[704,256]{1,0:T(8,128)(2,1)}, bf16[704,256]{1,0:T(8,128)(2,1)}, u32[]{:S(2)}, u32[]{:S(2)}) collective-permute-start(bf16[704,256]{1,0:T(8,128)(2,1)} %get-tuple-element.121), channel_id=1, source_target_pairs={{0,2},{1,3},{2,0},{3,1},{4,6},{5,7},{6,4},{7,5}} | collective-permute-start | bytes 1081352 | tf_op jit(solution)/shard_map/ppermute | solution.py:624
  266.0 38.2 %copy-start.9 = (f32[2,256,768]{2,1,0:T(8,128)S(1)}, f32[2,256,768]{2,1,0:T(8,128)}, u32[]{:S(2)}) copy-start(f32[2,256,768]{2,1,0:T(8,128)} %get-tuple-element.118) | copy-start | bytes 4718596
  330.5 43.2 %collective-permute-start.11 = (bf16[256,2816]{1,0:T(8,128)(2,1)}, bf16[256,2816]{1,0:T(8,128)(2,1)}, u32[]{:S(2)}, u32[]{:S(2)}) collective-permute-start(bf16[256,2816]{1,0:T(8,128)(2,1)} %get-tuple-element.141), channel_id=1, source_target_pairs={{0,1},{1,0},{2,3},{3,2},{4,5},{5,4},{6,7},{7,6}} | collective-permute-start | bytes 4325384 | tf_op jit(solution)/shard_map/ppermute | solution.py:670
  330.6 47.1 %collective-permute-start.10 = (bf16[256,2816]{1,0:T(8,128)(2,1)}, bf16[256,2816]{1,0:T(8,128)(2,1)}, u32[]{:S(2)}, u32[]{:S(2)}) collective-permute-start(bf16[256,2816]{1,0:T(8,128)(2,1)} %get-tuple-element.141), channel_id=1, source_target_pairs={{0,2},{1,3},{2,0},{3,1},{4,6},{5,7},{6,4},{7,5}} | collective-permute-start | bytes 4325384 | tf_op jit(solution)/shard_map/ppermute | solution.py:669
  340.1 52.5 %collective-permute-start.13 = (bf16[256,2816]{1,0:T(8,128)(2,1)}, bf16[256,2816]{1,0:T(8,128)(2,1)}, u32[]{:S(2)}, u32[]{:S(2)}) collective-permute-start(bf16[256,2816]{1,0:T(8,128)(2,1)} %get-tuple-element.140), channel_id=1, source_target_pairs={{0,1},{1,0},{2,3},{3,2},{4,5},{5,4},{6,7},{7,6}} | collective-permute-start | bytes 4325384 | tf_op jit(solution)/shard_map/ppermute | solution.py:670
  340.2 56.0 %collective-permute-start.9 = (bf16[256,2816]{1,0:T(8,128)(2,1)}, bf16[256,2816]{1,0:T(8,128)(2,1)}, u32[]{:S(2)}, u32[]{:S(2)}) collective-permute-start(bf16[256,2816]{1,0:T(8,128)(2,1)} %get-tuple-element.140), channel_id=1, source_target_pairs={{0,2},{1,3},{2,0},{3,1},{4,6},{5,7},{6,4},{7,5}} | collective-permute-start | bytes 4325384 | tf_op jit(solution)/shard_map/ppermute | solution.py:669
  363.9 45.5 %collective-permute-start.15 = (bf16[256,2816]{1,0:T(8,128)(2,1)}, bf16[256,2816]{1,0:T(8,128)(2,1)}, u32[]{:S(2)}, u32[]{:S(2)}) collective-permute-start(bf16[256,2816]{1,0:T(8,128)(2,1)} %get-tuple-element.138), channel_id=1, source_target_pairs={{0,1},{1,0},{2,3},{3,2},{4,5},{5,4},{6,7},{7,6}} | collective-permute-start | bytes 4325384 | tf_op jit(solution)/shard_map/ppermute | solution.py:670
  373.6 53.6 %collective-permute-start.8 = (bf16[256,2816]{1,0:T(8,128)(2,1)}, bf16[256,2816]{1,0:T(8,128)(2,1)}, u32[]{:S(2)}, u32[]{:S(2)}) collective-permute-start(bf16[256,2816]{1,0:T(8,128)(2,1)} %get-tuple-element.138), channel_id=1, source_target_pairs={{0,2},{1,3},{2,0},{3,1},{4,6},{5,7},{6,4},{7,5}} | collective-permute-start | bytes 4325384 | tf_op jit(solution)/shard_map/ppermute | solution.py:669
  377.6 13.5 %collective-permute-start.12 = (bf16[256,2816]{1,0:T(8,128)(2,1)}, bf16[256,2816]{1,0:T(8,128)(2,1)S(1)}, u32[]{:S(2)}, u32[]{:S(2)}) collective-permute-start(bf16[256,2816]{1,0:T(8,128)(2,1)} %collective-permute-done.10), channel_id=1, source_target_pairs={{0,1},{1,0},{2,3},{3,2},{4,5},{5,4},{6,7},{7,6}} | collective-permute-start | bytes 4325384 | tf_op jit(solution)/shard_map/ppermute | solution.py:689
  391.2 46.0 %collective-permute-start.17 = (bf16[256,2816]{1,0:T(8,128)(2,1)}, bf16[256,2816]{1,0:T(8,128)(2,1)}, u32[]{:S(2)}, u32[]{:S(2)}) collective-permute-start(bf16[256,2816]{1,0:T(8,128)(2,1)} %get-tuple-element.137), channel_id=1, source_target_pairs={{0,1},{1,0},{2,3},{3,2},{4,5},{5,4},{6,7},{7,6}} | collective-permute-start | bytes 4325384 | tf_op jit(solution)/shard_map/ppermute | solution.py:670
  392.6 64.8 %collective-permute-start.7 = (bf16[256,2816]{1,0:T(8,128)(2,1)}, bf16[256,2816]{1,0:T(8,128)(2,1)S(1)}, u32[]{:S(2)}, u32[]{:S(2)}) collective-permute-start(bf16[256,2816]{1,0:T(8,128)(2,1)} %get-tuple-element.137), channel_id=1, source_target_pairs={{0,2},{1,3},{2,0},{3,1},{4,6},{5,7},{6,4},{7,5}} | collective-permute-start | bytes 4325384 | tf_op jit(solution)/shard_map/ppermute | solution.py:669
  396.3 10.0 %collective-permute-start.14 = (bf16[256,2816]{1,0:T(8,128)(2,1)}, bf16[256,2816]{1,0:T(8,128)(2,1)}, u32[]{:S(2)}, u32[]{:S(2)}) collective-permute-start(bf16[256,2816]{1,0:T(8,128)(2,1)} %collective-permute-done.9), channel_id=1, source_target_pairs={{0,1},{1,0},{2,3},{3,2},{4,5},{5,4},{6,7},{7,6}} | collective-permute-start | bytes 4325384 | tf_op jit(solution)/shard_map/ppermute | solution.py:689
  406.3 52.6 %collective-permute-start.19 = (bf16[704,1024]{1,0:T(8,128)(2,1)}, bf16[704,1024]{1,0:T(8,128)(2,1)}, u32[]{:S(2)}, u32[]{:S(2)}) collective-permute-start(bf16[704,1024]{1,0:T(8,128)(2,1)} %get-tuple-element.133), channel_id=1, source_target_pairs={{0,1},{1,0},{2,3},{3,2},{4,5},{5,4},{6,7},{7,6}} | collective-permute-start | bytes 4325384 | tf_op jit(solution)/shard_map/ppermute | solution.py:670
  427.2 8.8 %collective-permute-start.16 = (bf16[256,2816]{1,0:T(8,128)(2,1)}, bf16[256,2816]{1,0:T(8,128)(2,1)S(1)}, u32[]{:S(2)}, u32[]{:S(2)}) collective-permute-start(bf16[256,2816]{1,0:T(8,128)(2,1)} %collective-permute-done.8), channel_id=1, source_target_pairs={{0,1},{1,0},{2,3},{3,2},{4,5},{5,4},{6,7},{7,6}} | collective-permute-start | bytes 4325384 | tf_op jit(solution)/shard_map/ppermute | solution.py:689
  457.4 5.3 %collective-permute-start.18 = (bf16[256,2816]{1,0:T(8,128)(2,1)S(1)}, bf16[256,2816]{1,0:T(8,128)(2,1)}, u32[]{:S(2)}, u32[]{:S(2)}) collective-permute-start(bf16[256,2816]{1,0:T(8,128)(2,1)S(1)} %collective-permute-done.7), channel_id=1, source_target_pairs={{0,1},{1,0},{2,3},{3,2},{4,5},{5,4},{6,7},{7,6}} | collective-permute-start | bytes 4325384 | tf_op jit(solution)/shard_map/ppermute | solution.py:689
  457.4 34.2 %collective-permute-start.6 = (bf16[704,1024]{1,0:T(8,128)(2,1)}, bf16[704,1024]{1,0:T(8,128)(2,1)S(1)}, u32[]{:S(2)}, u32[]{:S(2)}) collective-permute-start(bf16[704,1024]{1,0:T(8,128)(2,1)} %get-tuple-element.133), channel_id=1, source_target_pairs={{0,2},{1,3},{2,0},{3,1},{4,6},{5,7},{6,4},{7,5}} | collective-permute-start | bytes 4325384 | tf_op jit(solution)/shard_map/ppermute | solution.py:669
  491.6 3.4 collective-permute-start.20
  491.6 5.9 %collective-permute-start.21 = (bf16[704,1024]{1,0:T(8,128)(2,1)}, bf16[704,1024]{1,0:T(8,128)(2,1)}, u32[]{:S(2)}, u32[]{:S(2)}) collective-permute-start(bf16[704,1024]{1,0:T(8,128)(2,1)} %get-tuple-element.132), channel_id=1, source_target_pairs={{0,1},{1,0},{2,3},{3,2},{4,5},{5,4},{6,7},{7,6}} | collective-permute-start | bytes 4325384 | tf_op jit(solution)/shard_map/ppermute | solution.py:670
  492.1 33.7 %collective-permute-start.5 = (bf16[704,1024]{1,0:T(8,128)(2,1)}, bf16[704,1024]{1,0:T(8,128)(2,1)S(1)}, u32[]{:S(2)}, u32[]{:S(2)}) collective-permute-start(bf16[704,1024]{1,0:T(8,128)(2,1)} %get-tuple-element.132), channel_id=1, source_target_pairs={{0,2},{1,3},{2,0},{3,1},{4,6},{5,7},{6,4},{7,5}} | collective-permute-start | bytes 4325384 | tf_op jit(solution)/shard_map/ppermute | solution.py:669
  525.8 3.2 collective-permute-start.22
  (18 other events, 311.5 us)

commit v4 on v3

--- a/solution.py
+++ b/solution.py
@@ -251,16 +251,11 @@
 
         if quick:
 
-            @pl.when(j == 0)
-            def _():
-                meet(0)
-                over(0).start()
-
-            @pl.when(j > 1)
+            @pl.when(j > 0)
             def _():
                 meet(j - 1)
 
-        @pl.when((j >= 2) & (j < inside + late))
+        @pl.when((j >= late) & (j < inside + late))
         def _():
             over(j - late).start()
 
@@ -487,7 +482,7 @@
 
 
 def middle(ident, act_t, dg, du, w_gate, w_up, h, by_out, after):
-    tile, rows_w, rest_columns = 256, FF // DP, D // 4
+    tile, half, rows_w, rest_columns = 512, 256, FF // DP, D // 4
     inner = D - rest_columns
     steps = T // tile
     n_after = len(after)
@@ -562,12 +557,14 @@
 
         @pl.when(i >= DP)
         def _():
-            by_a = dot_t(dg_ref[...], wg[...]).astype(BF16) + dot_t(du_ref[...], wu[...]).astype(BF16)
-            c, wide = by_a.astype(F32), h_ref[...].astype(F32)
-            scale = root_mean_scale(wide)
-            along = jnp.sum(c * wide, -1, keepdims=True)
-            by = by_ref[pl.ds(pl.multiple_of((i - DP) * tile, tile), tile)]
-            out_ref[...] = by + (c * scale - wide * (scale * scale * scale * along * (1.0 / D))).astype(BF16)
+            for t in range(0, tile, half):
+                rows = slice(t, t + half)
+                by_a = dot_t(dg_ref[rows], wg[...]).astype(BF16) + dot_t(du_ref[rows], wu[...]).astype(BF16)
+                c, wide = by_a.astype(F32), h_ref[rows].astype(F32)
+                scale = root_mean_scale(wide)
+                along = jnp.sum(c * wide, -1, keepdims=True)
+                by = by_ref[pl.ds(pl.multiple_of((i - DP) * tile + t, half), half)]
+                out_ref[rows] = by + (c * scale - wide * (scale * scale * scale * along * (1.0 / D))).astype(BF16)
 
         @pl.when(i == DP + steps - 1)
         def _():
@@ -629,9 +626,9 @@
         units["b"] = near, cross(far)
         dh1, sum_d, far, near = middle(1, act2, dg2, du2, w_gate, w_up, h1, dy, (far,))
         units["d"] = near, cross(far)
-        sum_e, far, near, act1 = hidden(2, 0, 7, 7, True, a1, dh1, weights, (g1, u1), ())
+        sum_e, far, near, act1 = hidden(2, 0, 6, 6, True, a1, dh1, weights, (g1, u1), ())
         units["e"] = near, cross(far)
-        parts = ((0, 3 * D // 4), (3 * D // 4, D))
+        parts = ((0, 7 * D // 8), (7 * D // 8, D))
         *fars, near = down_grad(3, act1, dh1, parts, (far,))
         for k, (far, (start, stop)) in enumerate(zip(fars, parts, strict=True)):
             units[f"f{k}"] = near[:, start:stop], cross(far)

time: 531 us -> 531 us (level)
  waiting for transfers between devices: 120 us -> 130 us
    ppermute x5, waiting for transfers between devices: 32.5 us -> 37.9 us  [cross(): return lax.ppermute(far, 'dp', across)]
  transfers between devices with their start and end apart: 23 -> 23, of which waited for: 8 -> 9; matrix products, arithmetic and copies ran while one was open for 17% -> 16% of each run, Pallas kernels for 30% -> 29%
where the time goes in v4:
time: 531 us; the launch traced here: 530 us
  Pallas kernels  288 us (54%)
  waiting for transfers between devices  130 us (24%)
  other arithmetic  46.8 us (9%)
  local copies, waits for them, and re-layouts  45.3 us (9%)
  starting transfers between devices  13 us (2%)
  between operations  6.12 us (1%)
    pallas_call x2, Pallas kernels, hidden(): pl.pallas_call(kernel, grid=(CHUNKS,), in_specs=[whole(normed.shape), who...  131 us
    ppermute x6, waiting for transfers between devices, step(): over = lax.ppermute(mine, 'dp', across)  89.4 us
    pallas_call x1, Pallas kernels, forward_first(): pl.pallas_call(kernel, grid=(CHUNKS,), in_specs=[whole((T, D)), pl.BlockS...  49.5 us
    pallas_call x1, Pallas kernels, middle(): pl.pallas_call(kernel, grid=(DP + steps,), in_specs=[pl.BlockSpec((rows_w...  47.5 us
    dynamic_update_slice x19, local copies, waits for them, and re-layouts, put(): lax.dynamic_update_slice(full[which], piece[None], (layer, who * piece.sh...  40.9 us
    ppermute x5, waiting for transfers between devices, cross(): return lax.ppermute(far, 'dp', across)  37.9 us
    pallas_call x5, Pallas kernels, new_weight(): pl.pallas_call(kernel, grid_spec=pltpu.PrefetchScalarGridSpec(num_scalar_...  34 us
    add x3, other arithmetic, step(): new_v.append(0.95 * vs[which] + 0.05 * g * g)  23.7 us
  transfers between devices with their start and end apart: 23, of which 9 were waited for; matrix products, arithmetic and copies ran while one was open for 16% of the time, Pallas kernels for 29%

profile of v4, /device:TPU:0, one launch (start us, length us, event | category | flops | bytes accessed | tf_op | source)
XLA Modules:
  0.0 529.7 jit_solution(11766612122375309445)
XLA Ops:
  0.6 49.5 %shard_map.178 = (f32[2048,2816]{1,0:T(8,128)}, f32[2048,2816]{1,0:T(8,128)}, bf16[1024,2048]{1,0:T(8,128)(2,1)}, bf16[2048,1024]{1,0:T(8,128)(2,1)}, bf16[2048,1024]{1,0:T(8,128)(2,1)}) custom-call(bf16[2048,1024]{1,0:T(8,128)(2,1)} %bitcast.71, bf16[2,1024,2816]{2,1,0:T(8,128)(2,1)} %w_ref.11, bf16[2,1024,2816]{2,1,0:T(8,128)(2,1)} %w_ref.10, ...), custom_call_target="tpu_custom_call" | custom-call | flops 35433480192 | bytes 90000000 | tf_op jit(solution)/shard_map/pallas_call | solution.py:102
  50.1 78.1 %shard_map.179 = (bf16[2,256,2048]{2,1,0:T(8,128)(2,1)}, bf16[2,256,768]{2,1,0:T(8,128)(2,1)}, f32[2,256,768]{2,1,0:T(8,128)}, bf16[2816,2048]{1,0:T(8,128)(2,1)...) custom-call(bf16[2048,1024]{1,0:T(8,128)(2,1)} %get-tuple-element.97.n_ref, bf16[2048,1024]{1,0:T(8,128)(2,1)} %bitcast.72, ...), custom_call_target="tpu_custom_call" | custom-call | flops 59055800320 | bytes 60000000 | tf_op jit(solution)/shard_map/pallas_call | solution.py:301
  129.8 47.5 %shard_map.180 = (bf16[2048,1024]{1,0:T(8,128)(2,1)}, bf16[704,768]{1,0:T(8,128)(2,1)}, bf16[704,256]{1,0:T(8,128)(2,1)}, f32[704,256]{1,0:T(8,128)}) custom-call(bf16[2816,2048]{1,0:T(8,128)(2,1)} %get-tuple-element.99.act_ref, bf16[2048,1024]{1,0:T(8,128)(2,1)} %bitcast.73, bf16[2048,2816]{1,0:T(8,128)(2,1)} %get-tuple-element.100.dg_ref, ...), custom_call_target="tpu_custom_call" | custom-call | flops 35433480192 | bytes 70000000 | tf_op jit(solution)/shard_map/pallas_call | solution.py:584
  177.4 52.7 %shard_map.181 = (bf16[2,256,1536]{2,1,0:T(8,128)(2,1)}, bf16[2,256,1280]{2,1,0:T(8,128)(2,1)}, f32[2,256,1280]{2,1,0:T(8,128)}, bf16[2816,2048]{1,0:T(8,128)(2,1)}) custom-call(bf16[1024,2048]{1,0:T(8,128)(2,1)} %get-tuple-element.105.n_ref, bf16[2048,1024]{1,0:T(8,128)(2,1)} %get-tuple-element.106.by_ref, bf16[2,2816,1024]{2,1,0:T(8,128)(2,1)} %w_ref.8, ...), custom_call_target="tpu_custom_call" | custom-call | flops 35433480192 | bytes 60000000 | tf_op jit(solution)/shard_map/pallas_call | solution.py:301
  230.8 18.9 %shard_map.182 = (bf16[704,896]{1,0:T(8,128)(2,1)}, bf16[704,128]{1,0:T(8,128)(2,1)}, f32[704,1024]{1,0:T(8,128)}) custom-call(bf16[2816,2048]{1,0:T(8,128)(2,1)} %get-tuple-element.110.act_ref, bf16[2048,1024]{1,0:T(8,128)(2,1)} %get-tuple-element.106.by_ref, bf16[2,256,1280]{2,1,0:T(8,128)(2,1)} %get-tuple-element.111.rest_0_), custom_call_target="tpu_custom_call" | custom-call | flops 11811160064 | bytes 20000000 | tf_op jit(solution)/shard_map/pallas_call | solution.py:367
  260.5 5.5 %collective-permute-done.4 = bf16[704,128]{1,0:T(8,128)(2,1)} collective-permute-done((bf16[704,128]{1,0:T(8,128)(2,1)}, bf16[704,128]{1,0:T(8,128)(2,1)}, u32[]{:S(2)}, u32[]{:S(2)}) %collective-permute-start.4) | collective-permute-done | bytes 180256 | tf_op jit(solution)/shard_map/ppermute | solution.py:621
  267.6 32.4 %collective-permute-done.1 = bf16[704,256]{1,0:T(8,128)(2,1)S(1)} collective-permute-done((bf16[704,256]{1,0:T(8,128)(2,1)}, bf16[704,256]{1,0:T(8,128)(2,1)S(1)}, u32[]{:S(2)}, u32[]{:S(2)}) %collective-permute-start.1) | collective-permute-done | bytes 360480 | tf_op jit(solution)/shard_map/ppermute | solution.py:621
  308.0 3.7 multiply_reduce_fusion.3
  311.7 2.8 multiply_reduce_fusion.2
  319.6 7.5 %shard_map.183 = (f32[8,128]{1,0:T(8,128)}, bf16[256,2816]{1,0:T(8,128)(2,1)}) custom-call(f32[1]{0:T(128)} %bitcast.7.squares_ref, bf16[256,2816]{1,0:T(8,128)(2,1)} %get-tuple-element.128.g_ref, f32[2,256,2816]{2,1,0:T(8,128)} %m_ref.11, f32[2,256,2816]{2,1,0:T(8,128)} %v_ref.11, bf16[2,1024,2816]{2,1,0:T(8,128)(2,1)} %w_ref.11), custom_call_target="tpu_custom_call" | custom-call | flops 1181116032 | bytes 10000000 | tf_op jit(solution)/shard_map/pallas_call | solution.py:422
  332.0 6.8 %shard_map.188 = (bf16[256,2816]{1,0:T(8,128)(2,1)}, bf16[2,1024,2816]{2,1,0:T(8,128)(2,1)}) custom-call(s32[1]{0:T(128)} %bitcast.me_ref, f32[8,128]{1,0:T(8,128)} %get-tuple-element.129.factor_ref, bf16[256,2816]{1,0:T(8,128)(2,1)} %get-tuple-element.139.g_ref, f32[2,256,2816]{2,1,0:T(8,128)} %m_ref.11, f32[2,256,2816]{2,1,0:T(8,128)} %v_ref.11, ...), custom_call_target="tpu_custom_call" | custom-call | flops 1181116032 | bytes 10000000 | tf_op jit(solution)/shard_map/pallas_call | solution.py:469
  340.1 6.9 %shard_map.184 = (bf16[704,1024]{1,0:T(8,128)(2,1)}, bf16[2,2816,1024]{2,1,0:T(8,128)(2,1)}) custom-call(s32[1]{0:T(128)} %bitcast.me_ref, f32[8,128]{1,0:T(8,128)} %get-tuple-element.129.factor_ref, bf16[704,1024]{1,0:T(8,128)(2,1)} %get-tuple-element.206.g_ref, f32[2,704,1024]{2,1,0:T(8,128)} %m_ref.8, f32[2,704,1024]{2,1,0:T(8,128)} %v_ref.8, ...), custom_call_target="tpu_custom_call" | custom-call | flops 1181116032 | bytes 10000000 | tf_op jit(solution)/shard_map/pallas_call | solution.py:469
  347.0 6.9 %shard_map.185 = (bf16[704,1024]{1,0:T(8,128)(2,1)}, bf16[2,2816,1024]{2,1,0:T(8,128)(2,1)}) custom-call(s32[1]{0:T(128)} %bitcast.me_ref, f32[8,128]{1,0:T(8,128)} %get-tuple-element.129.factor_ref, bf16[704,1024]{1,0:T(8,128)(2,1)} %pad_maximum_fusion.5.g_ref, f32[2,704,1024]{2,1,0:T(8,128)} %m_ref.8, ...), custom_call_target="tpu_custom_call", output_to_operand_aliasing={{1}: (6, {})} | custom-call | flops 1181116032 | bytes 10000000 | tf_op jit(solution)/shard_map/pallas_call | solution.py:469
  353.9 6.7 %shard_map.186 = (bf16[256,2816]{1,0:T(8,128)(2,1)}, bf16[2,1024,2816]{2,1,0:T(8,128)(2,1)}) custom-call(s32[1]{0:T(128)} %bitcast.me_ref, f32[8,128]{1,0:T(8,128)} %get-tuple-element.129.factor_ref, bf16[256,2816]{1,0:T(8,128)(2,1)} %get-tuple-element.135.g_ref, f32[2,256,2816]{2,1,0:T(8,128)} %m_ref.10, f32[2,256,2816]{2,1,0:T(8,128)} %v_ref.10, ...), custom_call_target="tpu_custom_call" | custom-call | flops 1181116032 | bytes 10000000 | tf_op jit(solution)/shard_map/pallas_call | solution.py:469
  360.7 6.8 %shard_map.187 = (bf16[256,2816]{1,0:T(8,128)(2,1)}, bf16[2,1024,2816]{2,1,0:T(8,128)(2,1)}) custom-call(s32[1]{0:T(128)} %bitcast.me_ref, f32[8,128]{1,0:T(8,128)} %get-tuple-element.129.factor_ref, bf16[256,2816]{1,0:T(8,128)(2,1)} %get-tuple-element.134.g_ref, f32[2,256,2816]{2,1,0:T(8,128)} %m_ref.10, ...), custom_call_target="tpu_custom_call", output_to_operand_aliasing={{1}: (6, {})} | custom-call | flops 1181116032 | bytes 10000000 | tf_op jit(solution)/shard_map/pallas_call | solution.py:469
  373.6 10.3 %fusion = (f32[2,256,2816]{2,1,0:T(8,128)}, f32[2,256,2816]{2,1,0:T(8,128)}) fusion(f32[2,256,2816]{2,1,0:T(8,128)} %v_ref.11, f32[]{:T(128)} %bitcast.14, bf16[1,256,2816]{2,1,0:T(8,128)(2,1)S(1)} %bitcast.69, bf16[1,256,2816]{2,1,0:T(8,128)(2,1)S(1)} %bitcast.70, f32[2,256,2816]{2,1,0:T(8,128)} %m_ref.11), kind=kLoop, calls=%fused_computation.3 | loop fusion | flops 14417920 | bytes 25952260 | tf_op jit(solution)/shard_map/add | solution.py:674
  384.0 2.9 bitcast_dynamic-update-slice_fusion.16
  392.4 3.4 collective-permute-done.9
  395.9 7.2 %fusion.1 = (f32[2,256,2816]{2,1,0:T(8,128)}, f32[2,256,2816]{2,1,0:T(8,128)}) fusion(f32[2,256,2816]{2,1,0:T(8,128)S(1)} %bitcast.61, f32[]{:T(128)} %bitcast.14, bf16[1,256,2816]{2,1,0:T(8,128)(2,1)S(1)} %bitcast.67, bf16[1,256,2816]{2,1,0:T(8,128)(2,1)S(1)} %bitcast.68, f32[2,256,2816]{2,1,0:T(8,128)S(1)} %bitcast.59), kind=kLoop, calls=%fused_computation.4 | loop fusion | flops 14417920 | bytes 25952260 | tf_op jit(solution)/shard_map/add | solution.py:674
  411.3 15.4 %collective-permute-done.8 = bf16[256,2816]{1,0:T(8,128)(2,1)} collective-permute-done((bf16[256,2816]{1,0:T(8,128)(2,1)}, bf16[256,2816]{1,0:T(8,128)(2,1)}, u32[]{:S(2)}, u32[]{:S(2)}) %collective-permute-start.8) | collective-permute-done | bytes 1441824 | tf_op jit(solution)/shard_map/ppermute | solution.py:666
  426.7 6.2 %fusion.2 = (f32[2,704,1024]{2,1,0:T(8,128)}, f32[2,704,1024]{2,1,0:T(8,128)}) fusion(f32[2,704,1024]{2,1,0:T(8,128)S(1)} %bitcast.65, f32[]{:T(128)} %bitcast.14, bf16[1,704,1024]{2,1,0:T(8,128)(2,1)S(1)} %bitcast.66, bf16[1,704,1024]{2,1,0:T(8,128)(2,1)S(1)} %get-tuple-element.205, f32[2,704,1024]{2,1,0:T(8,128)S(1)} %bitcast.63), kind=kLoop, calls=%fused_computation.5 | loop fusion | flops 14417920 | bytes 25952260 | tf_op jit(solution)/shard_map/add | solution.py:674
  439.2 17.7 %collective-permute-done.7 = bf16[256,2816]{1,0:T(8,128)(2,1)S(1)} collective-permute-done((bf16[256,2816]{1,0:T(8,128)(2,1)}, bf16[256,2816]{1,0:T(8,128)(2,1)S(1)}, u32[]{:S(2)}, u32[]{:S(2)}) %collective-permute-start.7) | collective-permute-done | bytes 1441824 | tf_op jit(solution)/shard_map/ppermute | solution.py:666
  463.9 27.2 %collective-permute-done.6 = bf16[704,1024]{1,0:T(8,128)(2,1)S(1)} collective-permute-done((bf16[704,1024]{1,0:T(8,128)(2,1)}, bf16[704,1024]{1,0:T(8,128)(2,1)S(1)}, u32[]{:S(2)}, u32[]{:S(2)}) %collective-permute-start.6) | collective-permute-done | bytes 1441824 | tf_op jit(solution)/shard_map/ppermute | solution.py:666
  499.6 25.7 %collective-permute-done.5 = bf16[704,1024]{1,0:T(8,128)(2,1)S(1)} collective-permute-done((bf16[704,1024]{1,0:T(8,128)(2,1)}, bf16[704,1024]{1,0:T(8,128)(2,1)S(1)}, u32[]{:S(2)}, u32[]{:S(2)}) %collective-permute-start.5) | collective-permute-done | bytes 1441824 | tf_op jit(solution)/shard_map/ppermute | solution.py:666
  (115 shorter events, 75.0 us)
Async XLA Ops:
  128.3 174.9 %collective-permute-start = (bf16[2,256,768]{2,1,0:T(8,128)(2,1)}, bf16[2,256,768]{2,1,0:T(8,128)(2,1)}, u32[]{:S(2)}, u32[]{:S(2)}) collective-permute-start(bf16[2,256,768]{2,1,0:T(8,128)(2,1)} %get-tuple-element.103.rest_0_), channel_id=1, source_target_pairs={{0,2},{1,3},{2,0},{3,1},{4,6},{5,7},{6,4},{7,5}} | collective-permute-start | bytes 2359304 | tf_op jit(solution)/shard_map/ppermute | solution.py:621
  230.1 81.6 %collective-permute-start.2 = (bf16[2,256,1280]{2,1,0:T(8,128)(2,1)}, bf16[2,256,1280]{2,1,0:T(8,128)(2,1)}, u32[]{:S(2)}, u32[]{:S(2)}) collective-permute-start(bf16[2,256,1280]{2,1,0:T(8,128)(2,1)} %get-tuple-element.111.rest_0_), channel_id=1, source_target_pairs={{0,2},{1,3},{2,0},{3,1},{4,6},{5,7},{6,4},{7,5}} | collective-permute-start | bytes 3932168 | tf_op jit(solution)/shard_map/ppermute | solution.py:621
  249.7 16.2 %collective-permute-start.4 = (bf16[704,128]{1,0:T(8,128)(2,1)}, bf16[704,128]{1,0:T(8,128)(2,1)}, u32[]{:S(2)}, u32[]{:S(2)}) collective-permute-start(bf16[704,128]{1,0:T(8,128)(2,1)} %get-tuple-element.117), channel_id=1, source_target_pairs={{0,2},{1,3},{2,0},{3,1},{4,6},{5,7},{6,4},{7,5}} | collective-permute-start | bytes 540680 | tf_op jit(solution)/shard_map/ppermute | solution.py:621
  251.0 57.0 %collective-permute-start.3 = (bf16[704,896]{1,0:T(8,128)(2,1)}, bf16[704,896]{1,0:T(8,128)(2,1)}, u32[]{:S(2)}, u32[]{:S(2)}) collective-permute-start(bf16[704,896]{1,0:T(8,128)(2,1)} %get-tuple-element.116), channel_id=1, source_target_pairs={{0,2},{1,3},{2,0},{3,1},{4,6},{5,7},{6,4},{7,5}} | collective-permute-start | bytes 3784712 | tf_op jit(solution)/shard_map/ppermute | solution.py:621
  251.8 48.2 %collective-permute-start.1 = (bf16[704,256]{1,0:T(8,128)(2,1)}, bf16[704,256]{1,0:T(8,128)(2,1)S(1)}, u32[]{:S(2)}, u32[]{:S(2)}) collective-permute-start(bf16[704,256]{1,0:T(8,128)(2,1)} %get-tuple-element.121), channel_id=1, source_target_pairs={{0,2},{1,3},{2,0},{3,1},{4,6},{5,7},{6,4},{7,5}} | collective-permute-start | bytes 1081352 | tf_op jit(solution)/shard_map/ppermute | solution.py:621
  260.5 42.7 %copy-start.12 = (f32[2,256,768]{2,1,0:T(8,128)S(1)}, f32[2,256,768]{2,1,0:T(8,128)}, u32[]{:S(2)}) copy-start(f32[2,256,768]{2,1,0:T(8,128)} %get-tuple-element.118) | copy-start | bytes 4718596
  327.2 43.1 %collective-permute-start.11 = (bf16[256,2816]{1,0:T(8,128)(2,1)}, bf16[256,2816]{1,0:T(8,128)(2,1)}, u32[]{:S(2)}, u32[]{:S(2)}) collective-permute-start(bf16[256,2816]{1,0:T(8,128)(2,1)} %get-tuple-element.141), channel_id=1, source_target_pairs={{0,1},{1,0},{2,3},{3,2},{4,5},{5,4},{6,7},{7,6}} | collective-permute-start | bytes 4325384 | tf_op jit(solution)/shard_map/ppermute | solution.py:667
  330.1 43.3 %collective-permute-start.10 = (bf16[256,2816]{1,0:T(8,128)(2,1)}, bf16[256,2816]{1,0:T(8,128)(2,1)}, u32[]{:S(2)}, u32[]{:S(2)}) collective-permute-start(bf16[256,2816]{1,0:T(8,128)(2,1)} %get-tuple-element.141), channel_id=1, source_target_pairs={{0,2},{1,3},{2,0},{3,1},{4,6},{5,7},{6,4},{7,5}} | collective-permute-start | bytes 4325384 | tf_op jit(solution)/shard_map/ppermute | solution.py:666
  338.7 49.7 %collective-permute-start.13 = (bf16[256,2816]{1,0:T(8,128)(2,1)}, bf16[256,2816]{1,0:T(8,128)(2,1)}, u32[]{:S(2)}, u32[]{:S(2)}) collective-permute-start(bf16[256,2816]{1,0:T(8,128)(2,1)} %get-tuple-element.140), channel_id=1, source_target_pairs={{0,1},{1,0},{2,3},{3,2},{4,5},{5,4},{6,7},{7,6}} | collective-permute-start | bytes 4325384 | tf_op jit(solution)/shard_map/ppermute | solution.py:667
  338.8 56.9 %collective-permute-start.9 = (bf16[256,2816]{1,0:T(8,128)(2,1)}, bf16[256,2816]{1,0:T(8,128)(2,1)}, u32[]{:S(2)}, u32[]{:S(2)}) collective-permute-start(bf16[256,2816]{1,0:T(8,128)(2,1)} %get-tuple-element.140), channel_id=1, source_target_pairs={{0,2},{1,3},{2,0},{3,1},{4,6},{5,7},{6,4},{7,5}} | collective-permute-start | bytes 4325384 | tf_op jit(solution)/shard_map/ppermute | solution.py:666
  360.6 48.1 %collective-permute-start.15 = (bf16[256,2816]{1,0:T(8,128)(2,1)}, bf16[256,2816]{1,0:T(8,128)(2,1)}, u32[]{:S(2)}, u32[]{:S(2)}) collective-permute-start(bf16[256,2816]{1,0:T(8,128)(2,1)} %get-tuple-element.138), channel_id=1, source_target_pairs={{0,1},{1,0},{2,3},{3,2},{4,5},{5,4},{6,7},{7,6}} | collective-permute-start | bytes 4325384 | tf_op jit(solution)/shard_map/ppermute | solution.py:667
  370.2 56.4 %collective-permute-start.8 = (bf16[256,2816]{1,0:T(8,128)(2,1)}, bf16[256,2816]{1,0:T(8,128)(2,1)}, u32[]{:S(2)}, u32[]{:S(2)}) collective-permute-start(bf16[256,2816]{1,0:T(8,128)(2,1)} %get-tuple-element.138), channel_id=1, source_target_pairs={{0,2},{1,3},{2,0},{3,1},{4,6},{5,7},{6,4},{7,5}} | collective-permute-start | bytes 4325384 | tf_op jit(solution)/shard_map/ppermute | solution.py:666
  373.4 13.5 %collective-permute-start.12 = (bf16[256,2816]{1,0:T(8,128)(2,1)}, bf16[256,2816]{1,0:T(8,128)(2,1)S(1)}, u32[]{:S(2)}, u32[]{:S(2)}) collective-permute-start(bf16[256,2816]{1,0:T(8,128)(2,1)} %collective-permute-done.10), channel_id=1, source_target_pairs={{0,1},{1,0},{2,3},{3,2},{4,5},{5,4},{6,7},{7,6}} | collective-permute-start | bytes 4325384 | tf_op jit(solution)/shard_map/ppermute | solution.py:686
  386.9 49.7 %collective-permute-start.17 = (bf16[256,2816]{1,0:T(8,128)(2,1)}, bf16[256,2816]{1,0:T(8,128)(2,1)}, u32[]{:S(2)}, u32[]{:S(2)}) collective-permute-start(bf16[256,2816]{1,0:T(8,128)(2,1)} %get-tuple-element.137), channel_id=1, source_target_pairs={{0,1},{1,0},{2,3},{3,2},{4,5},{5,4},{6,7},{7,6}} | collective-permute-start | bytes 4325384 | tf_op jit(solution)/shard_map/ppermute | solution.py:667
  388.4 68.5 %collective-permute-start.7 = (bf16[256,2816]{1,0:T(8,128)(2,1)}, bf16[256,2816]{1,0:T(8,128)(2,1)S(1)}, u32[]{:S(2)}, u32[]{:S(2)}) collective-permute-start(bf16[256,2816]{1,0:T(8,128)(2,1)} %get-tuple-element.137), channel_id=1, source_target_pairs={{0,2},{1,3},{2,0},{3,1},{4,6},{5,7},{6,4},{7,5}} | collective-permute-start | bytes 4325384 | tf_op jit(solution)/shard_map/ppermute | solution.py:666
  395.8 9.9 %collective-permute-start.14 = (bf16[256,2816]{1,0:T(8,128)(2,1)}, bf16[256,2816]{1,0:T(8,128)(2,1)}, u32[]{:S(2)}, u32[]{:S(2)}) collective-permute-start(bf16[256,2816]{1,0:T(8,128)(2,1)} %collective-permute-done.9), channel_id=1, source_target_pairs={{0,1},{1,0},{2,3},{3,2},{4,5},{5,4},{6,7},{7,6}} | collective-permute-start | bytes 4325384 | tf_op jit(solution)/shard_map/ppermute | solution.py:686
  405.7 51.9 %collective-permute-start.19 = (bf16[704,1024]{1,0:T(8,128)(2,1)}, bf16[704,1024]{1,0:T(8,128)(2,1)}, u32[]{:S(2)}, u32[]{:S(2)}) collective-permute-start(bf16[704,1024]{1,0:T(8,128)(2,1)} %get-tuple-element.133), channel_id=1, source_target_pairs={{0,1},{1,0},{2,3},{3,2},{4,5},{5,4},{6,7},{7,6}} | collective-permute-start | bytes 4325384 | tf_op jit(solution)/shard_map/ppermute | solution.py:667
  426.6 8.8 %collective-permute-start.16 = (bf16[256,2816]{1,0:T(8,128)(2,1)}, bf16[256,2816]{1,0:T(8,128)(2,1)S(1)}, u32[]{:S(2)}, u32[]{:S(2)}) collective-permute-start(bf16[256,2816]{1,0:T(8,128)(2,1)} %collective-permute-done.8), channel_id=1, source_target_pairs={{0,1},{1,0},{2,3},{3,2},{4,5},{5,4},{6,7},{7,6}} | collective-permute-start | bytes 4325384 | tf_op jit(solution)/shard_map/ppermute | solution.py:686
  456.9 4.5 collective-permute-start.18
  456.9 34.2 %collective-permute-start.6 = (bf16[704,1024]{1,0:T(8,128)(2,1)}, bf16[704,1024]{1,0:T(8,128)(2,1)S(1)}, u32[]{:S(2)}, u32[]{:S(2)}) collective-permute-start(bf16[704,1024]{1,0:T(8,128)(2,1)} %get-tuple-element.133), channel_id=1, source_target_pairs={{0,2},{1,3},{2,0},{3,1},{4,6},{5,7},{6,4},{7,5}} | collective-permute-start | bytes 4325384 | tf_op jit(solution)/shard_map/ppermute | solution.py:666
  491.1 3.4 collective-permute-start.20
  491.1 5.9 %collective-permute-start.21 = (bf16[704,1024]{1,0:T(8,128)(2,1)}, bf16[704,1024]{1,0:T(8,128)(2,1)}, u32[]{:S(2)}, u32[]{:S(2)}) collective-permute-start(bf16[704,1024]{1,0:T(8,128)(2,1)} %get-tuple-element.132), channel_id=1, source_target_pairs={{0,1},{1,0},{2,3},{3,2},{4,5},{5,4},{6,7},{7,6}} | collective-permute-start | bytes 4325384 | tf_op jit(solution)/shard_map/ppermute | solution.py:667
  491.6 33.7 %collective-permute-start.5 = (bf16[704,1024]{1,0:T(8,128)(2,1)}, bf16[704,1024]{1,0:T(8,128)(2,1)S(1)}, u32[]{:S(2)}, u32[]{:S(2)}) collective-permute-start(bf16[704,1024]{1,0:T(8,128)(2,1)} %get-tuple-element.132), channel_id=1, source_target_pairs={{0,2},{1,3},{2,0},{3,1},{4,6},{5,7},{6,4},{7,5}} | collective-permute-start | bytes 4325384 | tf_op jit(solution)/shard_map/ppermute | solution.py:666
  525.3 3.2 collective-permute-start.22
  (20 other events, 326.1 us)
